TPU v7x, 512 devices: a 8x2x16 block of a 8x16x16 slice. The times are simulated.
512 devices in a mesh: shot: 2 (over y), gx: 16 (over z), gy: 8 (over x), gz: 2 (over core).
Axes of the slice: x: 8, y: 2, z: 16, core: 2. Of those that a mesh axis runs over, the one named last changes fastest.
The devices are a block of a 8x16x16 slice.
Arguments:
- source_prev: float32 [384, 32, 1024], P(('shot', 'gx'), 'gy', 'gz'), parts along dimension 0, may hold values from -6 to 6
- source_now: float32 [384, 32, 1024], P(('shot', 'gx'), 'gy', 'gz'), parts along dimension 0, may hold values from -6 to 6
- receiver_prev: float32 [384, 32, 1024], P(('shot', 'gx'), 'gy', 'gz'), parts along dimension 0, may hold values from -6 to 6
- receiver_now: float32 [384, 32, 1024], P(('shot', 'gx'), 'gy', 'gz'), parts along dimension 0, may hold values from -6 to 6
- courant: float32 [192, 32, 1024], P('gx', 'gy', 'gz'), may hold values from 0.04 to 0.16
- absorbing: int32 [192, 32, 1024], P('gx', 'gy', 'gz'), may hold values from 0 to 8, as said below
- source_cell: int32 [6], P('shot'), parts along dimension 0, may hold values from 0 to 1023, as said below
- wavelet: float32 [8], P('shot'), parts along dimension 0, may hold values from -4 to 4
- receiver_cells: int32 [4096, 2], P('shot'), parts along dimension 0, may hold values from 0 to 191, as said below
- traces: float32 [4, 4096], P(None, 'shot'), parts along dimension 1, may hold values from -6 to 6
Outputs:
- source_field: float32 [384, 32, 1024], P(('shot', 'gx'), 'gy', 'gz'), parts along dimension 0
- receiver_field: float32 [384, 32, 1024], P(('shot', 'gx'), 'gy', 'gz'), parts along dimension 0
- filtered_image: bfloat16 [16, 384, 32, 1024], P(None, ('shot', 'gx'), 'gy', 'gz'), parts along dimension 1
There are 2 independent parts, one for each index of `shot`. A program takes and returns all parts, laid end to end along the dimension named above; an argument that names none is the same for every part. Nothing has to cross between parts.
Inputs may be any that keep to these rules, and one draw needn't show every extreme that they name: `source_cell`: the source's cell as (x, y, z), each coordinate within the grid. `receiver_cells`: each row is a receiver's (x, y) within the grid, on the top surface at depth 0; several receivers may share a cell. Depth of a cell into the absorbing layers along the four side faces and the bottom face, largest at the grid's faces; 0 in the interior; the top face has no layer.
All inputs are finite; a program needn't handle non-finite values.
Results may differ from a plain program's by a relative error of at most 0.001.
Values sent between devices are 32-bit elements; how exact they have to be, the bound alone decides.
No kernel may reach another device: no remote copies, remote signals or barrier semaphores. Data moves between devices by JAX's collectives and lax.ppermute only.
A program may use at most 64 MiB of HBM per device.

v0:
```python
import jax
import jax.numpy as jnp
from jax import lax
from jax.sharding import PartitionSpec as P

LAGS = 16
STEPS = 4
EVERY = 2


stencil_weights = (8.0 / 5.0, -1.0 / 5.0, 8.0 / 315.0, -1.0 / 560.0)
centre_weight = -205.0 / 72.0


def with_halo(array, sides, width):
    for axis, dim in sides:
        size, length = (lax.axis_size(axis), array.shape[dim])
        up = [(i, (i + 1) % size) for i in range(size - 1)]
        down = [(j, i) for i, j in up]
        last = lax.slice_in_dim(array, length - width, length, axis=dim)
        first = lax.slice_in_dim(array, 0, width, axis=dim)
        before = lax.ppermute(last, axis, up)
        after = lax.ppermute(first, axis, down)
        array = jnp.concatenate([before, array, after], axis=dim)
    return array


def extended(array, sides, width):
    edges = {}
    for axis, dim in sides:
        size, length = (lax.axis_size(axis), array.shape[dim])
        up = [(i, (i + 1) % size) for i in range(size - 1)]
        last = lax.slice_in_dim(array, length - width, length, axis=dim)
        first = lax.slice_in_dim(array, 0, width, axis=dim)
        edges[dim] = (
            lax.ppermute(last, axis, up),
            lax.ppermute(first, axis, [(b, a) for a, b in up]),
        )
    done = []
    for _, dim in sides:
        low, high = edges[dim]
        around = [(width, width) if d in done else (0, 0) for d in range(array.ndim)]
        array = jnp.concatenate([jnp.pad(low, around), array, jnp.pad(high, around)], axis=dim)
        done.append(dim)
    return array


def stencil(padded):
    size_x = padded.shape[-3] - 8
    size_y = padded.shape[-2] - 8
    size_z = padded.shape[-1] - 8

    def window(start_x, start_y, start_z):
        return padded[
            ..., start_x : start_x + size_x, start_y : start_y + size_y, start_z : start_z + size_z
        ]

    total = 3.0 * centre_weight * window(4, 4, 4)
    for reach, weight in enumerate(stencil_weights, 1):
        total = total + weight * (
            window(4 + reach, 4, 4)
            + window(4 - reach, 4, 4)
            + window(4, 4 + reach, 4)
            + window(4, 4 - reach, 4)
            + window(4, 4, 4 + reach)
            + window(4, 4, 4 - reach)
        )
    return total


def advance(padded, current, earlier, courant, damping):
    return (2.0 * current - (1.0 - damping) * earlier + courant * stencil(padded)) / (1.0 + damping)


def laplace(padded):
    size_x = padded.shape[-3] - 2
    size_y = padded.shape[-2] - 2
    size_z = padded.shape[-1] - 2

    def window(start_x, start_y, start_z):
        return padded[
            ..., start_x : start_x + size_x, start_y : start_y + size_y, start_z : start_z + size_z
        ]

    return 6.0 * window(1, 1, 1) - (
        window(2, 1, 1)
        + window(0, 1, 1)
        + window(1, 2, 1)
        + window(1, 0, 1)
        + window(1, 1, 2)
        + window(1, 1, 0)
    )


def correlate(widened, length):
    return jnp.stack(
        [
            widened[0, LAGS - offset : LAGS - offset + length]
            * widened[1, offset : offset + length]
            for offset in range(LAGS)
        ]
    )


def local(
    source_prev,
    source_now,
    receiver_prev,
    receiver_now,
    courant,
    absorbing,
    source_cell,
    wavelet,
    receiver_cells,
    traces,
):
    earlier = jnp.stack([source_prev, receiver_prev])
    current = jnp.stack([source_now, receiver_now])
    damping = absorbing.astype(jnp.float32) / 16.0
    tile_x, tile_y, tile_z = courant.shape
    x_anchor = lax.axis_index("gx") * tile_x
    y_cells = jnp.arange(tile_y, dtype=jnp.int32) + lax.axis_index("gy") * tile_y
    z_cells = jnp.arange(tile_z, dtype=jnp.int32) + lax.axis_index("gz") * tile_z
    surface = (lax.axis_index("gz") == 0).astype(jnp.float32)
    image = None
    x_cells = jnp.arange(tile_x, dtype=jnp.int32) + x_anchor
    for step_index in range(STEPS):
        padded = extended(current, (("gx", 1), ("gy", 2), ("gz", 3)), 4)
        upcoming = advance(padded, current, earlier, courant, damping)
        inject_upcoming = upcoming
        hit_x = (x_cells == source_cell[0]).astype(jnp.float32)
        hit_y = (y_cells == source_cell[1]).astype(jnp.float32)
        hit_z = (z_cells == source_cell[2]).astype(jnp.float32)
        point = hit_x[:, None, None] * hit_y[None, :, None] * hit_z[None, None, :]
        match_x = (receiver_cells[:, 0:1] == x_cells[None, :]).astype(jnp.float32) * traces[
            step_index
        ][:, None]
        match_y = (receiver_cells[:, 1:2] == y_cells[None, :]).astype(jnp.float32)
        sheet = jnp.einsum("rx,ry->xy", match_x, match_y, precision=lax.Precision.HIGHEST) * surface
        inject_upcoming = inject_upcoming.at[0].add(point * wavelet[step_index])
        upcoming = inject_upcoming.at[1, :, :, 0].add(sheet)
        earlier, current = (current, upcoming)
        if (step_index + 1) % EVERY == 0:
            widened = with_halo(current, (("gx", 1),), LAGS // 2)
            term = correlate(widened, tile_x)
            image = term if image is None else image + term
    framed = extended(image, (("gx", 1), ("gy", 2), ("gz", 3)), 1)
    filtered_image = laplace(framed).astype(jnp.bfloat16)
    return (current[0], current[1], filtered_image)


def solution(mesh):
    placed = (
        P(("shot", "gx"), "gy", "gz"),
        P(("shot", "gx"), "gy", "gz"),
        P(("shot", "gx"), "gy", "gz"),
        P(("shot", "gx"), "gy", "gz"),
        P("gx", "gy", "gz"),
        P("gx", "gy", "gz"),
        P("shot"),
        P("shot"),
        P("shot", None),
        P(None, "shot"),
    )
    return jax.shard_map(
        local,
        mesh=mesh,
        in_specs=placed,
        out_specs=(
            P(("shot", "gx"), "gy", "gz"),
            P(("shot", "gx"), "gy", "gz"),
            P(None, ("shot", "gx"), "gy", "gz"),
        ),
        check_vma=False,
    )
```

profile of v0, /device:TPU:65, one launch (start us, length us, event | category | flops | bytes accessed | tf_op | source)
XLA Modules:
  0.0 201.4 jit_solution(17542820368843097936)
XLA Ops:
  0.6 1.0 pad_maximum_fusion.16
  1.6 1.3 collective-permute-start.2
  2.9 4.8 %collective-permute-start.3 = (f32[2,12,4,512]{3,2,1,0:T(4,128)S(1)}, f32[2,12,4,512]{3,2,1,0:T(4,128)S(1)}, u32[]{:S(2)}, u32[]{:S(2)}) collective-permute-start(f32[2,12,4,512]{3,2,1,0:T(4,128)S(1)} %pad_maximum_fusion.16), channel_id=1, source_target_pairs={{0,2},{2,4},{4,6},{6,8},{8,10},{10,12},{12,14},{1,3},{3,5},{5,7},{... | collective-permute-start | bytes 589832 | tf_op jit(solution)/shard_map/ppermute | solution.py:36
  7.7 0.8 fusion.274
  8.6 1.3 collective-permute-start
  9.9 6.5 %collective-permute-start.1 = (f32[2,4,4,512]{3,2,1,0:T(4,128)S(1)}, f32[2,4,4,512]{3,2,1,0:T(4,128)S(1)}, u32[]{:S(2)}, u32[]{:S(2)}) collective-permute-start(f32[2,4,4,512]{3,2,1,0:T(4,128)S(1)} %get-tuple-element.185), channel_id=1, source_target_pairs={{0,16},{16,32},{32,48},{48,64},{64,80},{80,96},{96,112},{112,128},... | collective-permute-start | bytes 196616 | tf_op jit(solution)/shard_map/ppermute | solution.py:36
  16.4 0.9 fusion.275
  17.3 41.3 %collective-permute-start.4 = (f32[2,12,4,4]{3,2,1,0:T(4,128)S(1)}, f32[2,12,4,4]{3,2,1,0:T(4,128)S(1)}, u32[]{:S(2)}, u32[]{:S(2)}) collective-permute-start(f32[2,12,4,4]{3,2,1,0:T(4,128)S(1)} %get-tuple-element.183), channel_id=1, source_target_pairs={{1,0},{3,2},{5,4},{7,6},{9,8},{11,10},{13,12},{15,14},{17,16},{19,... | collective-permute-start | bytes 4616 | tf_op jit(solution)/shard_map/ppermute | solution.py:37
  58.6 0.9 fusion.272
  59.5 1.4 fusion.296
  62.2 1.5 fusion.295
  63.7 0.8 fusion.294
  64.5 0.9 fusion.293
  65.5 1.8 fusion.20
  67.4 1.9 fusion.26
  69.3 1.9 fusion.32
  71.9 1.3 collective-permute-start.5
  73.5 1.5 collective-permute-done.5
  75.0 2.5 %select_maximum_fusion.7 = (f32[2,20,12,516]{3,2,1,0:T(8,128)S(1)}, f32[2,20,12,516]{3,2,1,0:T(8,128)S(1)}) fusion(f32[2,12,4,4]{3,2,1,0:T(4,128)S(1)} %collective-permute-done.4, f32[2,20,4,512]{3,2,1,0:T(4,128)S(1)} %pad.88, f32[2,4,4,512]{3,2,1,0:T(4,128)S(1)} %collective-permute-done, f32[1,12,4,512]{3,2,1,0:T(4,128)S(1)} %bitcast.40, ...), kind=kLoop, calls=%fused_computation.20 | loop fusion | flops 3962880 | bytes 2967552 | tf_op jit(solution)/shard_map/concatenate | solution.py:43
  77.6 1.7 fusion.165
  79.3 0.8 fusion.178
  80.2 1.3 collective-permute-start.8
  81.5 4.0 %collective-permute-start.9 = (f32[2,12,4,512]{3,2,1,0:T(4,128)S(1)}, f32[2,12,4,512]{3,2,1,0:T(4,128)S(1)}, u32[]{:S(2)}, u32[]{:S(2)}) collective-permute-start(f32[2,12,4,512]{3,2,1,0:T(4,128)S(1)} %scatter-add.29), channel_id=1, source_target_pairs={{0,2},{2,4},{4,6},{6,8},{8,10},{10,12},{12,14},{1,3},{3,5},{5,7},{... | collective-permute-start | bytes 589832 | tf_op jit(solution)/shard_map/ppermute | solution.py:36
  85.7 1.3 collective-permute-start.6
  87.0 4.0 %collective-permute-start.7 = (f32[2,4,4,512]{3,2,1,0:T(4,128)S(1)}, f32[2,4,4,512]{3,2,1,0:T(4,128)S(1)}, u32[]{:S(2)}, u32[]{:S(2)}) collective-permute-start(f32[2,4,4,512]{3,2,1,0:T(4,128)S(1)} %get-tuple-element.179), channel_id=1, source_target_pairs={{0,16},{16,32},{32,48},{48,64},{64,80},{80,96},{96,112},{112,128},... | collective-permute-start | bytes 196616 | tf_op jit(solution)/shard_map/ppermute | solution.py:36
  91.0 3.2 %collective-permute-start.10 = (f32[2,12,4,4]{3,2,1,0:T(4,128)S(1)}, f32[2,12,4,4]{3,2,1,0:T(4,128)S(1)}, u32[]{:S(2)}, u32[]{:S(2)}) collective-permute-start(f32[2,12,4,4]{3,2,1,0:T(4,128)S(1)} %get-tuple-element.177), channel_id=1, source_target_pairs={{1,0},{3,2},{5,4},{7,6},{9,8},{11,10},{13,12},{15,14},{17,16},{19,... | collective-permute-start | bytes 4616 | tf_op jit(solution)/shard_map/ppermute | solution.py:37
  94.3 1.5 collective-permute-start.11
  95.8 1.8 fusion.38
  98.1 1.2 select_maximum_fusion.5
  99.3 1.3 add_divide_fusion.2
  101.6 1.3 collective-permute-start.14
  102.9 4.0 %collective-permute-start.15 = (f32[2,12,4,512]{3,2,1,0:T(4,128)S(1)}, f32[2,12,4,512]{3,2,1,0:T(4,128)S(1)}, u32[]{:S(2)}, u32[]{:S(2)}) collective-permute-start(f32[2,12,4,512]{3,2,1,0:T(4,128)S(1)} %scatter-add.31), channel_id=1, source_target_pairs={{0,2},{2,4},{4,6},{6,8},{8,10},{10,12},{12,14},{1,3},{3,5},{5,7},{... | collective-permute-start | bytes 589832 | tf_op jit(solution)/shard_map/ppermute | solution.py:36
  107.0 1.3 collective-permute-start.24
  108.4 4.0 %collective-permute-start.25 = (f32[2,8,4,512]{3,1,2,0:T(8,128)S(1)}, f32[2,8,4,512]{3,1,2,0:T(8,128)S(1)}, u32[]{:S(2)}, u32[]{:S(2)}) collective-permute-start(f32[2,8,4,512]{3,1,2,0:T(8,128)S(1)} %copy.644), channel_id=1, source_target_pairs={{0,16},{16,32},{32,48},{48,64},{64,80},{80,96},{96,112},{112,128},... | collective-permute-start | bytes 393224 | tf_op jit(solution)/shard_map/ppermute | solution.py:22
  112.5 1.3 collective-permute-start.12
  113.9 4.0 %collective-permute-start.13 = (f32[2,4,4,512]{3,2,1,0:T(4,128)S(1)}, f32[2,4,4,512]{3,2,1,0:T(4,128)S(1)}, u32[]{:S(2)}, u32[]{:S(2)}) collective-permute-start(f32[2,4,4,512]{3,2,1,0:T(4,128)S(1)} %get-tuple-element.175), channel_id=1, source_target_pairs={{0,16},{16,32},{32,48},{48,64},{64,80},{80,96},{96,112},{112,128},... | collective-permute-start | bytes 196616 | tf_op jit(solution)/shard_map/ppermute | solution.py:36
  118.0 4.8 %collective-permute-start.16 = (f32[2,12,4,4]{3,2,1,0:T(4,128)S(1)}, f32[2,12,4,4]{3,2,1,0:T(4,128)S(1)}, u32[]{:S(2)}, u32[]{:S(2)}) collective-permute-start(f32[2,12,4,4]{3,2,1,0:T(4,128)S(1)} %get-tuple-element.173), channel_id=1, source_target_pairs={{1,0},{3,2},{5,4},{7,6},{9,8},{11,10},{13,12},{15,14},{17,16},{19,... | collective-permute-start | bytes 4616 | tf_op jit(solution)/shard_map/ppermute | solution.py:37
  123.0 1.3 collective-permute-start.17
  124.5 1.6 collective-permute-done.17
  126.1 1.2 select_maximum_fusion.3
  127.3 1.3 add_divide_fusion.1
  129.5 1.3 collective-permute-start.20
  130.9 4.0 %collective-permute-start.21 = (f32[2,12,4,512]{3,2,1,0:T(4,128)S(1)}, f32[2,12,4,512]{3,2,1,0:T(4,128)S(1)}, u32[]{:S(2)}, u32[]{:S(2)}) collective-permute-start(f32[2,12,4,512]{3,2,1,0:T(4,128)S(1)} %scatter-add.35), channel_id=1, source_target_pairs={{0,2},{2,4},{4,6},{6,8},{8,10},{10,12},{12,14},{1,3},{3,5},{5,7},{... | collective-permute-start | bytes 589832 | tf_op jit(solution)/shard_map/ppermute | solution.py:36
  135.0 1.3 collective-permute-start.18
  136.3 4.0 %collective-permute-start.19 = (f32[2,4,4,512]{3,2,1,0:T(4,128)S(1)}, f32[2,4,4,512]{3,2,1,0:T(4,128)S(1)}, u32[]{:S(2)}, u32[]{:S(2)}) collective-permute-start(f32[2,4,4,512]{3,2,1,0:T(4,128)S(1)} %get-tuple-element.171), channel_id=1, source_target_pairs={{0,16},{16,32},{32,48},{48,64},{64,80},{80,96},{96,112},{112,128},... | collective-permute-start | bytes 196616 | tf_op jit(solution)/shard_map/ppermute | solution.py:36
  140.4 3.2 %collective-permute-start.22 = (f32[2,12,4,4]{3,2,1,0:T(4,128)S(1)}, f32[2,12,4,4]{3,2,1,0:T(4,128)S(1)}, u32[]{:S(2)}, u32[]{:S(2)}) collective-permute-start(f32[2,12,4,4]{3,2,1,0:T(4,128)S(1)} %get-tuple-element.169), channel_id=1, source_target_pairs={{1,0},{3,2},{5,4},{7,6},{9,8},{11,10},{13,12},{15,14},{17,16},{19,... | collective-permute-start | bytes 4616 | tf_op jit(solution)/shard_map/ppermute | solution.py:37
  143.6 1.3 collective-permute-start.23
  146.8 1.2 select_maximum_fusion.1
  148.0 1.3 add_divide_fusion
  150.3 1.3 collective-permute-start.26
  152.3 4.9 %collective-permute-start.27 = (f32[2,8,4,512]{3,1,2,0:T(8,128)}, f32[2,8,4,512]{3,1,2,0:T(8,128)}, u32[]{:S(2)}, u32[]{:S(2)}) collective-permute-start(f32[2,8,4,512]{3,1,2,0:T(8,128)} %copy.664), channel_id=1, source_target_pairs={{0,16},{16,32},{32,48},{48,64},{64,80},{80,96},{96,112},{112,128},... | collective-permute-start | bytes 393224 | tf_op jit(solution)/shard_map/ppermute | solution.py:22
  157.9 2.4 %stack.22 = f32[16,12,4,512]{3,0,2,1:T(8,128)S(1)} concatenate(f32[1,12,4,512]{3,0,2,1:T(1,128)S(1)} %copy.646, f32[1,12,4,512]{3,0,2,1:T(1,128)S(1)} %copy.647, f32[1,12,4,512]{3,0,2,1:T(1,128)S(1)} %copy.648, f32[1,12,4,512]{3,0,2,1:T(1,128)S(1)} %copy.649, f32[1,12,4,512]{3,0,2,1:T(1,128)S(1)} %copy.650, f32[1,12,4,512]{3,0,2,1:T(1,128)S(1)} %copy.651, ...), dimensions={0} | concatenate | bytes 3145728 | tf_op jit(solution)/shard_map/stack | solution.py:96
  160.3 1.0 copy.663
  161.3 1.0 copy.665
  173.3 4.9 %stack.23 = f32[16,12,4,512]{3,0,2,1:T(8,128)S(1)} concatenate(f32[1,12,4,512]{3,0,2,1:T(1,128)} %copy.666, f32[1,12,4,512]{3,0,2,1:T(1,128)} %copy.667, f32[1,12,4,512]{3,0,2,1:T(1,128)} %copy.668, f32[1,12,4,512]{3,0,2,1:T(1,128)} %copy.669, f32[1,12,4,512]{3,0,2,1:T(1,128)} %copy.670, f32[1,12,4,512]{3,0,2,1:T(1,128)} %copy.671, f32[1,12,4,512]{3,0,2,1:T(1,128)S(1)} %copy.672, ...), dimensions={0} | concatenate | bytes 3145728 | tf_op jit(solution)/shard_map/stack | solution.py:96
  178.7 1.3 collective-permute-start.30
  180.0 4.1 %collective-permute-start.31 = (f32[16,12,1,512]{3,0,2,1:T(8,128)S(1)}, f32[16,12,1,512]{3,0,2,1:T(8,128)S(1)}, u32[]{:S(2)}, u32[]{:S(2)}) collective-permute-start(f32[16,12,1,512]{3,0,2,1:T(8,128)S(1)} %get-tuple-element.121), channel_id=1, source_target_pairs={{0,2},{2,4},{4,6},{6,8},{8,10},{10,12},{12,14},{1,3},{3,5},{5,7},{... | collective-permute-start | bytes 1179656 | tf_op jit(solution)/shard_map/ppermute | solution.py:36
  184.1 1.3 collective-permute-start.28
  185.4 4.0 %collective-permute-start.29 = (f32[16,1,4,512]{3,0,2,1:T(8,128)S(1)}, f32[16,1,4,512]{3,0,2,1:T(8,128)S(1)}, u32[]{:S(2)}, u32[]{:S(2)}) collective-permute-start(f32[16,1,4,512]{3,0,2,1:T(8,128)S(1)} %get-tuple-element.119), channel_id=1, source_target_pairs={{0,16},{16,32},{32,48},{48,64},{64,80},{80,96},{96,112},{112,128},... | collective-permute-start | bytes 393224 | tf_op jit(solution)/shard_map/ppermute | solution.py:36
  189.7 4.4 %collective-permute-start.32 = (f32[16,12,4,1]{3,0,2,1:T(8,128)S(1)}, f32[16,12,4,1]{3,0,2,1:T(8,128)S(1)}, u32[]{:S(2)}, u32[]{:S(2)}) collective-permute-start(f32[16,12,4,1]{3,0,2,1:T(8,128)S(1)} %get-tuple-element.117), channel_id=1, source_target_pairs={{1,0},{3,2},{5,4},{7,6},{9,8},{11,10},{13,12},{15,14},{17,16},{19,... | collective-permute-start | bytes 9224 | tf_op jit(solution)/shard_map/ppermute | solution.py:37
  194.1 1.3 collective-permute-start.33
  195.5 2.2 %collective-permute-done.33 = f32[16,12,4,1]{3,0,2,1:T(8,128)S(1)} collective-permute-done((f32[16,12,4,1]{3,0,2,1:T(8,128)S(1)}, f32[16,12,4,1]{3,0,2,1:T(8,128)S(1)}, u32[]{:S(2)}, u32[]{:S(2)}) %collective-permute-start.33) | collective-permute-done | bytes 3104 | tf_op jit(solution)/shard_map/ppermute | solution.py:36
  197.7 2.2 %fusion.11 = bf16[16,12,4,512]{3,0,2,1:T(8,128)(2,1)S(1)} fusion(f32[16,12,4,1]{3,0,2,1:T(8,128)S(1)} %collective-permute-done.33, f32[16,14,1,512]{3,0,2,1:T(8,128)S(1)} %pad.104, f32[16,14,1,512]{3,0,2,1:T(8,128)S(1)} %pad.105, f32[16,1,4,512]{3,0,2,1:T(8,128)S(1)} %collective-permute-done.28, f32[16,12,4,512]{3,0,2,1:T(8,128)S(1)} %add.573, ...), kind=kLoop, calls=%fused_computation.26 | loop fusion | flops 12582912 | bytes 3545088 | tf_op jit(solution)/shard_map/convert_element_type | solution.py:148
  199.9 1.5 copy.682
  (131 shorter events, 21.3 us)
Async XLA Ops:
  1.6 71.7 %collective-permute-start.2 = (f32[2,12,4,512]{3,2,1,0:T(4,128)S(1)}, f32[2,12,4,512]{3,2,1,0:T(4,128)S(1)}, u32[]{:S(2)}, u32[]{:S(2)}) collective-permute-start(f32[2,12,4,512]{3,2,1,0:T(4,128)S(1)} %pad_maximum_fusion.16), channel_id=1, source_target_pairs={{2,0},{4,2},{6,4},{8,6},{10,8},{12,10},{14,12},{3,1},{5,3},{7,5},{... | collective-permute-start | bytes 589832 | tf_op jit(solution)/shard_map/ppermute | solution.py:37
  2.9 70.5 %collective-permute-start.3 = (f32[2,12,4,512]{3,2,1,0:T(4,128)S(1)}, f32[2,12,4,512]{3,2,1,0:T(4,128)S(1)}, u32[]{:S(2)}, u32[]{:S(2)}) collective-permute-start(f32[2,12,4,512]{3,2,1,0:T(4,128)S(1)} %pad_maximum_fusion.16), channel_id=1, source_target_pairs={{0,2},{2,4},{4,6},{6,8},{8,10},{10,12},{12,14},{1,3},{3,5},{5,7},{... | collective-permute-start | bytes 589832 | tf_op jit(solution)/shard_map/ppermute | solution.py:36
  8.6 63.3 %collective-permute-start = (f32[2,4,4,512]{3,2,1,0:T(4,128)S(1)}, f32[2,4,4,512]{3,2,1,0:T(4,128)S(1)}, u32[]{:S(2)}, u32[]{:S(2)}) collective-permute-start(f32[2,4,4,512]{3,2,1,0:T(4,128)S(1)} %get-tuple-element.186), channel_id=1, source_target_pairs={{16,0},{32,16},{48,32},{64,48},{80,64},{96,80},{112,96},{128,112},... | collective-permute-start | bytes 196616 | tf_op jit(solution)/shard_map/ppermute | solution.py:37
  9.9 63.3 %collective-permute-start.1 = (f32[2,4,4,512]{3,2,1,0:T(4,128)S(1)}, f32[2,4,4,512]{3,2,1,0:T(4,128)S(1)}, u32[]{:S(2)}, u32[]{:S(2)}) collective-permute-start(f32[2,4,4,512]{3,2,1,0:T(4,128)S(1)} %get-tuple-element.185), channel_id=1, source_target_pairs={{0,16},{16,32},{32,48},{48,64},{64,80},{80,96},{96,112},{112,128},... | collective-permute-start | bytes 196616 | tf_op jit(solution)/shard_map/ppermute | solution.py:36
  17.3 56.2 %collective-permute-start.4 = (f32[2,12,4,4]{3,2,1,0:T(4,128)S(1)}, f32[2,12,4,4]{3,2,1,0:T(4,128)S(1)}, u32[]{:S(2)}, u32[]{:S(2)}) collective-permute-start(f32[2,12,4,4]{3,2,1,0:T(4,128)S(1)} %get-tuple-element.183), channel_id=1, source_target_pairs={{1,0},{3,2},{5,4},{7,6},{9,8},{11,10},{13,12},{15,14},{17,16},{19,... | collective-permute-start | bytes 4616 | tf_op jit(solution)/shard_map/ppermute | solution.py:37
  65.4 7.8 %copy-start = (f32[12,4,512]{2,1,0:T(4,128)S(1)}, f32[12,4,512]{2,1,0:T(4,128)}, u32[]{:S(2)}) copy-start(f32[12,4,512]{2,1,0:T(4,128)} %param.27) | copy-start | bytes 294916
  65.5 7.8 %copy-start.1 = (f32[12,4,512]{2,1,0:T(4,128)S(1)}, f32[12,4,512]{2,1,0:T(4,128)}, u32[]{:S(2)}) copy-start(f32[12,4,512]{2,1,0:T(4,128)} %param.29) | copy-start | bytes 294916
  71.9 3.2 %collective-permute-start.5 = (f32[2,12,4,4]{3,2,1,0:T(4,128)S(1)}, f32[2,12,4,4]{3,2,1,0:T(4,128)S(1)}, u32[]{:S(2)}, u32[]{:S(2)}) collective-permute-start(f32[2,12,4,4]{3,2,1,0:T(4,128)S(1)} %get-tuple-element.184), channel_id=1, source_target_pairs={{0,1},{2,3},{4,5},{6,7},{8,9},{10,11},{12,13},{14,15},{16,17},{18,... | collective-permute-start | bytes 4616 | tf_op jit(solution)/shard_map/ppermute | solution.py:36
  73.5 4.1 %copy-start.2 = (f32[12,4,512]{2,1,0:T(4,128)S(1)}, f32[12,4,512]{2,1,0:T(4,128)}, u32[]{:S(2)}) copy-start(f32[12,4,512]{2,1,0:T(4,128)} %param.30) | copy-start | bytes 294916
  73.5 4.1 %copy-start.3 = (f32[12,4,512]{2,1,0:T(4,128)S(1)}, f32[12,4,512]{2,1,0:T(4,128)}, u32[]{:S(2)}) copy-start(f32[12,4,512]{2,1,0:T(4,128)} %param.28) | copy-start | bytes 294916
  73.5 4.1 %copy-start.4 = (f32[12,4,512]{2,1,0:T(4,128)S(1)}, f32[12,4,512]{2,1,0:T(4,128)}, u32[]{:S(2)}) copy-start(f32[12,4,512]{2,1,0:T(4,128)} %param.26) | copy-start | bytes 294916
  80.2 14.1 %collective-permute-start.8 = (f32[2,12,4,512]{3,2,1,0:T(4,128)S(1)}, f32[2,12,4,512]{3,2,1,0:T(4,128)S(1)}, u32[]{:S(2)}, u32[]{:S(2)}) collective-permute-start(f32[2,12,4,512]{3,2,1,0:T(4,128)S(1)} %scatter-add.29), channel_id=1, source_target_pairs={{2,0},{4,2},{6,4},{8,6},{10,8},{12,10},{14,12},{3,1},{5,3},{7,5},{... | collective-permute-start | bytes 589832 | tf_op jit(solution)/shard_map/ppermute | solution.py:37
  81.5 16.5 %collective-permute-start.9 = (f32[2,12,4,512]{3,2,1,0:T(4,128)S(1)}, f32[2,12,4,512]{3,2,1,0:T(4,128)S(1)}, u32[]{:S(2)}, u32[]{:S(2)}) collective-permute-start(f32[2,12,4,512]{3,2,1,0:T(4,128)S(1)} %scatter-add.29), channel_id=1, source_target_pairs={{0,2},{2,4},{4,6},{6,8},{8,10},{10,12},{12,14},{1,3},{3,5},{5,7},{... | collective-permute-start | bytes 589832 | tf_op jit(solution)/shard_map/ppermute | solution.py:36
  85.7 12.4 %collective-permute-start.6 = (f32[2,4,4,512]{3,2,1,0:T(4,128)S(1)}, f32[2,4,4,512]{3,2,1,0:T(4,128)S(1)}, u32[]{:S(2)}, u32[]{:S(2)}) collective-permute-start(f32[2,4,4,512]{3,2,1,0:T(4,128)S(1)} %get-tuple-element.180), channel_id=1, source_target_pairs={{16,0},{32,16},{48,32},{64,48},{80,64},{96,80},{112,96},{128,112},... | collective-permute-start | bytes 196616 | tf_op jit(solution)/shard_map/ppermute | solution.py:37
  87.0 11.1 %collective-permute-start.7 = (f32[2,4,4,512]{3,2,1,0:T(4,128)S(1)}, f32[2,4,4,512]{3,2,1,0:T(4,128)S(1)}, u32[]{:S(2)}, u32[]{:S(2)}) collective-permute-start(f32[2,4,4,512]{3,2,1,0:T(4,128)S(1)} %get-tuple-element.179), channel_id=1, source_target_pairs={{0,16},{16,32},{32,48},{48,64},{64,80},{80,96},{96,112},{112,128},... | collective-permute-start | bytes 196616 | tf_op jit(solution)/shard_map/ppermute | solution.py:36
  91.0 7.0 %collective-permute-start.10 = (f32[2,12,4,4]{3,2,1,0:T(4,128)S(1)}, f32[2,12,4,4]{3,2,1,0:T(4,128)S(1)}, u32[]{:S(2)}, u32[]{:S(2)}) collective-permute-start(f32[2,12,4,4]{3,2,1,0:T(4,128)S(1)} %get-tuple-element.177), channel_id=1, source_target_pairs={{1,0},{3,2},{5,4},{7,6},{9,8},{11,10},{13,12},{15,14},{17,16},{19,... | collective-permute-start | bytes 4616 | tf_op jit(solution)/shard_map/ppermute | solution.py:37
  94.3 3.8 %collective-permute-start.11 = (f32[2,12,4,4]{3,2,1,0:T(4,128)S(1)}, f32[2,12,4,4]{3,2,1,0:T(4,128)S(1)}, u32[]{:S(2)}, u32[]{:S(2)}) collective-permute-start(f32[2,12,4,4]{3,2,1,0:T(4,128)S(1)} %get-tuple-element.178), channel_id=1, source_target_pairs={{0,1},{2,3},{4,5},{6,7},{8,9},{10,11},{12,13},{14,15},{16,17},{18,... | collective-permute-start | bytes 4616 | tf_op jit(solution)/shard_map/ppermute | solution.py:36
  101.6 21.4 %collective-permute-start.14 = (f32[2,12,4,512]{3,2,1,0:T(4,128)S(1)}, f32[2,12,4,512]{3,2,1,0:T(4,128)S(1)}, u32[]{:S(2)}, u32[]{:S(2)}) collective-permute-start(f32[2,12,4,512]{3,2,1,0:T(4,128)S(1)} %scatter-add.31), channel_id=1, source_target_pairs={{2,0},{4,2},{6,4},{8,6},{10,8},{12,10},{14,12},{3,1},{5,3},{7,5},{... | collective-permute-start | bytes 589832 | tf_op jit(solution)/shard_map/ppermute | solution.py:37
  102.9 21.6 %collective-permute-start.15 = (f32[2,12,4,512]{3,2,1,0:T(4,128)S(1)}, f32[2,12,4,512]{3,2,1,0:T(4,128)S(1)}, u32[]{:S(2)}, u32[]{:S(2)}) collective-permute-start(f32[2,12,4,512]{3,2,1,0:T(4,128)S(1)} %scatter-add.31), channel_id=1, source_target_pairs={{0,2},{2,4},{4,6},{6,8},{8,10},{10,12},{12,14},{1,3},{3,5},{5,7},{... | collective-permute-start | bytes 589832 | tf_op jit(solution)/shard_map/ppermute | solution.py:36
  107.0 6.8 %collective-permute-start.24 = (f32[2,8,4,512]{3,1,2,0:T(8,128)S(1)}, f32[2,8,4,512]{3,1,2,0:T(8,128)S(1)}, u32[]{:S(2)}, u32[]{:S(2)}) collective-permute-start(f32[2,8,4,512]{3,1,2,0:T(8,128)S(1)} %copy.642), channel_id=1, source_target_pairs={{16,0},{32,16},{48,32},{64,48},{80,64},{96,80},{112,96},{128,112},... | collective-permute-start | bytes 393224 | tf_op jit(solution)/shard_map/ppermute | solution.py:23
  108.4 9.6 %collective-permute-start.25 = (f32[2,8,4,512]{3,1,2,0:T(8,128)S(1)}, f32[2,8,4,512]{3,1,2,0:T(8,128)S(1)}, u32[]{:S(2)}, u32[]{:S(2)}) collective-permute-start(f32[2,8,4,512]{3,1,2,0:T(8,128)S(1)} %copy.644), channel_id=1, source_target_pairs={{0,16},{16,32},{32,48},{48,64},{64,80},{80,96},{96,112},{112,128},... | collective-permute-start | bytes 393224 | tf_op jit(solution)/shard_map/ppermute | solution.py:22
  112.5 13.6 %collective-permute-start.12 = (f32[2,4,4,512]{3,2,1,0:T(4,128)S(1)}, f32[2,4,4,512]{3,2,1,0:T(4,128)S(1)}, u32[]{:S(2)}, u32[]{:S(2)}) collective-permute-start(f32[2,4,4,512]{3,2,1,0:T(4,128)S(1)} %get-tuple-element.176), channel_id=1, source_target_pairs={{16,0},{32,16},{48,32},{64,48},{80,64},{96,80},{112,96},{128,112},... | collective-permute-start | bytes 196616 | tf_op jit(solution)/shard_map/ppermute | solution.py:37
  113.9 12.3 %collective-permute-start.13 = (f32[2,4,4,512]{3,2,1,0:T(4,128)S(1)}, f32[2,4,4,512]{3,2,1,0:T(4,128)S(1)}, u32[]{:S(2)}, u32[]{:S(2)}) collective-permute-start(f32[2,4,4,512]{3,2,1,0:T(4,128)S(1)} %get-tuple-element.175), channel_id=1, source_target_pairs={{0,16},{16,32},{32,48},{48,64},{64,80},{80,96},{96,112},{112,128},... | collective-permute-start | bytes 196616 | tf_op jit(solution)/shard_map/ppermute | solution.py:36
  118.0 6.5 %collective-permute-start.16 = (f32[2,12,4,4]{3,2,1,0:T(4,128)S(1)}, f32[2,12,4,4]{3,2,1,0:T(4,128)S(1)}, u32[]{:S(2)}, u32[]{:S(2)}) collective-permute-start(f32[2,12,4,4]{3,2,1,0:T(4,128)S(1)} %get-tuple-element.173), channel_id=1, source_target_pairs={{1,0},{3,2},{5,4},{7,6},{9,8},{11,10},{13,12},{15,14},{17,16},{19,... | collective-permute-start | bytes 4616 | tf_op jit(solution)/shard_map/ppermute | solution.py:37
  123.0 3.2 %collective-permute-start.17 = (f32[2,12,4,4]{3,2,1,0:T(4,128)S(1)}, f32[2,12,4,4]{3,2,1,0:T(4,128)S(1)}, u32[]{:S(2)}, u32[]{:S(2)}) collective-permute-start(f32[2,12,4,4]{3,2,1,0:T(4,128)S(1)} %get-tuple-element.174), channel_id=1, source_target_pairs={{0,1},{2,3},{4,5},{6,7},{8,9},{10,11},{12,13},{14,15},{16,17},{18,... | collective-permute-start | bytes 4616 | tf_op jit(solution)/shard_map/ppermute | solution.py:36
  129.5 14.1 %collective-permute-start.20 = (f32[2,12,4,512]{3,2,1,0:T(4,128)S(1)}, f32[2,12,4,512]{3,2,1,0:T(4,128)S(1)}, u32[]{:S(2)}, u32[]{:S(2)}) collective-permute-start(f32[2,12,4,512]{3,2,1,0:T(4,128)S(1)} %scatter-add.35), channel_id=1, source_target_pairs={{2,0},{4,2},{6,4},{8,6},{10,8},{12,10},{14,12},{3,1},{5,3},{7,5},{... | collective-permute-start | bytes 589832 | tf_op jit(solution)/shard_map/ppermute | solution.py:37
  130.9 15.4 %collective-permute-start.21 = (f32[2,12,4,512]{3,2,1,0:T(4,128)S(1)}, f32[2,12,4,512]{3,2,1,0:T(4,128)S(1)}, u32[]{:S(2)}, u32[]{:S(2)}) collective-permute-start(f32[2,12,4,512]{3,2,1,0:T(4,128)S(1)} %scatter-add.35), channel_id=1, source_target_pairs={{0,2},{2,4},{4,6},{6,8},{8,10},{10,12},{12,14},{1,3},{3,5},{5,7},{... | collective-permute-start | bytes 589832 | tf_op jit(solution)/shard_map/ppermute | solution.py:36
  135.0 11.8 %collective-permute-start.18 = (f32[2,4,4,512]{3,2,1,0:T(4,128)S(1)}, f32[2,4,4,512]{3,2,1,0:T(4,128)S(1)}, u32[]{:S(2)}, u32[]{:S(2)}) collective-permute-start(f32[2,4,4,512]{3,2,1,0:T(4,128)S(1)} %get-tuple-element.172), channel_id=1, source_target_pairs={{16,0},{32,16},{48,32},{64,48},{80,64},{96,80},{112,96},{128,112},... | collective-permute-start | bytes 196616 | tf_op jit(solution)/shard_map/ppermute | solution.py:37
  136.3 10.4 %collective-permute-start.19 = (f32[2,4,4,512]{3,2,1,0:T(4,128)S(1)}, f32[2,4,4,512]{3,2,1,0:T(4,128)S(1)}, u32[]{:S(2)}, u32[]{:S(2)}) collective-permute-start(f32[2,4,4,512]{3,2,1,0:T(4,128)S(1)} %get-tuple-element.171), channel_id=1, source_target_pairs={{0,16},{16,32},{32,48},{48,64},{64,80},{80,96},{96,112},{112,128},... | collective-permute-start | bytes 196616 | tf_op jit(solution)/shard_map/ppermute | solution.py:36
  140.4 6.0 %collective-permute-start.22 = (f32[2,12,4,4]{3,2,1,0:T(4,128)S(1)}, f32[2,12,4,4]{3,2,1,0:T(4,128)S(1)}, u32[]{:S(2)}, u32[]{:S(2)}) collective-permute-start(f32[2,12,4,4]{3,2,1,0:T(4,128)S(1)} %get-tuple-element.169), channel_id=1, source_target_pairs={{1,0},{3,2},{5,4},{7,6},{9,8},{11,10},{13,12},{15,14},{17,16},{19,... | collective-permute-start | bytes 4616 | tf_op jit(solution)/shard_map/ppermute | solution.py:37
  143.6 3.2 %collective-permute-start.23 = (f32[2,12,4,4]{3,2,1,0:T(4,128)S(1)}, f32[2,12,4,4]{3,2,1,0:T(4,128)S(1)}, u32[]{:S(2)}, u32[]{:S(2)}) collective-permute-start(f32[2,12,4,4]{3,2,1,0:T(4,128)S(1)} %get-tuple-element.170), channel_id=1, source_target_pairs={{0,1},{2,3},{4,5},{6,7},{8,9},{10,11},{12,13},{14,15},{16,17},{18,... | collective-permute-start | bytes 4616 | tf_op jit(solution)/shard_map/ppermute | solution.py:36
  150.3 10.0 %collective-permute-start.26 = (f32[2,8,4,512]{3,1,2,0:T(8,128)S(1)}, f32[2,8,4,512]{3,1,2,0:T(8,128)}, u32[]{:S(2)}, u32[]{:S(2)}) collective-permute-start(f32[2,8,4,512]{3,1,2,0:T(8,128)S(1)} %copy.662), channel_id=1, source_target_pairs={{16,0},{32,16},{48,32},{64,48},{80,64},{96,80},{112,96},{128,112},... | collective-permute-start | bytes 393224 | tf_op jit(solution)/shard_map/ppermute | solution.py:23
  152.3 9.0 %collective-permute-start.27 = (f32[2,8,4,512]{3,1,2,0:T(8,128)}, f32[2,8,4,512]{3,1,2,0:T(8,128)}, u32[]{:S(2)}, u32[]{:S(2)}) collective-permute-start(f32[2,8,4,512]{3,1,2,0:T(8,128)} %copy.664), channel_id=1, source_target_pairs={{0,16},{16,32},{32,48},{48,64},{64,80},{80,96},{96,112},{112,128},... | collective-permute-start | bytes 393224 | tf_op jit(solution)/shard_map/ppermute | solution.py:22
  178.7 15.4 %collective-permute-start.30 = (f32[16,12,1,512]{3,0,2,1:T(8,128)S(1)}, f32[16,12,1,512]{3,0,2,1:T(8,128)S(1)}, u32[]{:S(2)}, u32[]{:S(2)}) collective-permute-start(f32[16,12,1,512]{3,0,2,1:T(8,128)S(1)} %get-tuple-element.122), channel_id=1, source_target_pairs={{2,0},{4,2},{6,4},{8,6},{10,8},{12,10},{14,12},{3,1},{5,3},{7,5},{... | collective-permute-start | bytes 1179656 | tf_op jit(solution)/shard_map/ppermute | solution.py:37
  180.0 15.4 %collective-permute-start.31 = (f32[16,12,1,512]{3,0,2,1:T(8,128)S(1)}, f32[16,12,1,512]{3,0,2,1:T(8,128)S(1)}, u32[]{:S(2)}, u32[]{:S(2)}) collective-permute-start(f32[16,12,1,512]{3,0,2,1:T(8,128)S(1)} %get-tuple-element.121), channel_id=1, source_target_pairs={{0,2},{2,4},{4,6},{6,8},{8,10},{10,12},{12,14},{1,3},{3,5},{5,7},{... | collective-permute-start | bytes 1179656 | tf_op jit(solution)/shard_map/ppermute | solution.py:36
  184.1 13.6 %collective-permute-start.28 = (f32[16,1,4,512]{3,0,2,1:T(8,128)S(1)}, f32[16,1,4,512]{3,0,2,1:T(8,128)S(1)}, u32[]{:S(2)}, u32[]{:S(2)}) collective-permute-start(f32[16,1,4,512]{3,0,2,1:T(8,128)S(1)} %get-tuple-element.120), channel_id=1, source_target_pairs={{16,0},{32,16},{48,32},{64,48},{80,64},{96,80},{112,96},{128,112},... | collective-permute-start | bytes 393224 | tf_op jit(solution)/shard_map/ppermute | solution.py:37
  185.4 12.3 %collective-permute-start.29 = (f32[16,1,4,512]{3,0,2,1:T(8,128)S(1)}, f32[16,1,4,512]{3,0,2,1:T(8,128)S(1)}, u32[]{:S(2)}, u32[]{:S(2)}) collective-permute-start(f32[16,1,4,512]{3,0,2,1:T(8,128)S(1)} %get-tuple-element.119), channel_id=1, source_target_pairs={{0,16},{16,32},{32,48},{48,64},{64,80},{80,96},{96,112},{112,128},... | collective-permute-start | bytes 393224 | tf_op jit(solution)/shard_map/ppermute | solution.py:36
  189.7 5.8 %collective-permute-start.32 = (f32[16,12,4,1]{3,0,2,1:T(8,128)S(1)}, f32[16,12,4,1]{3,0,2,1:T(8,128)S(1)}, u32[]{:S(2)}, u32[]{:S(2)}) collective-permute-start(f32[16,12,4,1]{3,0,2,1:T(8,128)S(1)} %get-tuple-element.117), channel_id=1, source_target_pairs={{1,0},{3,2},{5,4},{7,6},{9,8},{11,10},{13,12},{15,14},{17,16},{19,... | collective-permute-start | bytes 9224 | tf_op jit(solution)/shard_map/ppermute | solution.py:37
  194.1 3.6 %collective-permute-start.33 = (f32[16,12,4,1]{3,0,2,1:T(8,128)S(1)}, f32[16,12,4,1]{3,0,2,1:T(8,128)S(1)}, u32[]{:S(2)}, u32[]{:S(2)}) collective-permute-start(f32[16,12,4,1]{3,0,2,1:T(8,128)S(1)} %get-tuple-element.118), channel_id=1, source_target_pairs={{0,1},{2,3},{4,5},{6,7},{8,9},{10,11},{12,13},{14,15},{16,17},{18,... | collective-permute-start | bytes 9224 | tf_op jit(solution)/shard_map/ppermute | solution.py:36
where the time goes:
time: 203 us; the launch traced here: 201 us
  starting transfers between devices  132 us (65%)
  local copies, waits for them, and re-layouts  29.3 us (14%)
  other arithmetic  25.2 us (12%)
  matrix products  7.39 us (4%)
  waiting for transfers between devices  5.87 us (3%)
    ppermute x15, starting transfers between devices, extended(): lax.ppermute(first, axis, [(b, a) for a, b in up])  70 us
    ppermute x15, starting transfers between devices, extended(): lax.ppermute(last, axis, up)  50.3 us
    mul x32, local copies, waits for them, and re-layouts, correlate(): widened[0, LAGS - offset:LAGS - offset + length]  10.9 us
    ppermute x2, starting transfers between devices, with_halo(): before = lax.ppermute(last, axis, up)  8.93 us
    dot_general x4, matrix products, local(): jnp.einsum('rx,ry->xy', match_x, match_y, precision=lax.Precision.HIGHEST)  7.39 us
    another operation x2, local copies, waits for them, and re-layouts, correlate(): jnp.stack([widened[0, LAGS - offset:LAGS - offset + length] * widened[1,...  7.33 us
    concatenate x5, other arithmetic, extended(): jnp.concatenate([jnp.pad(low, around), array, jnp.pad(high, around)], axi...  6.16 us
    ppermute x15, waiting for transfers between devices, extended(): lax.ppermute(last, axis, up)  5.82 us
  transfers between devices with their start and end apart: 34, of which 4 were waited for; matrix products, arithmetic and copies ran while one was open for 12% of the time, Pallas kernels for 0%

commit v1 on v0

--- a/solution.py
+++ b/solution.py
@@ -12,30 +12,29 @@
 centre_weight = -205.0 / 72.0
 
 
+def edges_of(array, axis, dim, width):
+    size, here, length = (lax.axis_size(axis), lax.axis_index(axis), array.shape[dim])
+    last = lax.slice_in_dim(array, length - width, length, axis=dim)
+    first = lax.slice_in_dim(array, 0, width, axis=dim)
+    if size == 2:
+        other = lax.ppermute(jnp.where(here == 0, last, first), axis, [(0, 1), (1, 0)])
+        before = after = other
+    else:
+        up = [(i, (i + 1) % size) for i in range(size)]
+        before = lax.ppermute(last, axis, up)
+        after = lax.ppermute(first, axis, [(b, a) for a, b in up])
+    return (jnp.where(here > 0, before, 0.0), jnp.where(here < size - 1, after, 0.0))
+
+
 def with_halo(array, sides, width):
     for axis, dim in sides:
-        size, length = (lax.axis_size(axis), array.shape[dim])
-        up = [(i, (i + 1) % size) for i in range(size - 1)]
-        down = [(j, i) for i, j in up]
-        last = lax.slice_in_dim(array, length - width, length, axis=dim)
-        first = lax.slice_in_dim(array, 0, width, axis=dim)
-        before = lax.ppermute(last, axis, up)
-        after = lax.ppermute(first, axis, down)
+        before, after = edges_of(array, axis, dim, width)
         array = jnp.concatenate([before, array, after], axis=dim)
     return array
 
 
 def extended(array, sides, width):
-    edges = {}
-    for axis, dim in sides:
-        size, length = (lax.axis_size(axis), array.shape[dim])
-        up = [(i, (i + 1) % size) for i in range(size - 1)]
-        last = lax.slice_in_dim(array, length - width, length, axis=dim)
-        first = lax.slice_in_dim(array, 0, width, axis=dim)
-        edges[dim] = (
-            lax.ppermute(last, axis, up),
-            lax.ppermute(first, axis, [(b, a) for a, b in up]),
-        )
+    edges = {dim: edges_of(array, axis, dim, width) for axis, dim in sides}
     done = []
     for _, dim in sides:
         low, high = edges[dim]

time: 203 us -> 220 us (1.084)
  the two profiles are of different devices: /device:TPU:65 before, /device:TPU:80 now
where the time goes in v1:
time: 220 us; the launch traced here: 218 us
  starting transfers between devices  134 us (61%)
  other arithmetic  27.5 us (12%)
  local copies, waits for them, and re-layouts  27 us (12%)
  waiting for transfers between devices  19.8 us (9%)
  matrix products  7.41 us (3%)
    ppermute x12, starting transfers between devices, edges_of(): after = lax.ppermute(first, axis, [(b, a) for a, b in up])  97.2 us
    ppermute x12, starting transfers between devices, edges_of(): before = lax.ppermute(last, axis, up)  27.5 us
    ppermute x12, waiting for transfers between devices, edges_of(): before = lax.ppermute(last, axis, up)  14.3 us
    mul x32, local copies, waits for them, and re-layouts, correlate(): widened[0, LAGS - offset:LAGS - offset + length]  10.9 us
    ppermute x5, starting transfers between devices, edges_of(): lax.ppermute(jnp.where(here == 0, last, first), axis, [(0, 1), (1, 0)])  9.76 us
    dot_general x4, matrix products, local(): jnp.einsum('rx,ry->xy', match_x, match_y, precision=lax.Precision.HIGHEST)  7.41 us
    another operation x2, local copies, waits for them, and re-layouts, correlate(): jnp.stack([widened[0, LAGS - offset:LAGS - offset + length] * widened[1,...  7.33 us
    concatenate x5, other arithmetic, extended(): jnp.concatenate([jnp.pad(low, around), array, jnp.pad(high, around)], axi...  6.2 us
  transfers between devices with their start and end apart: 29, of which 10 were waited for; matrix products, arithmetic and copies ran while one was open for 11% of the time, Pallas kernels for 0%

profile of v1, /device:TPU:80, one launch (start us, length us, event | category | flops | bytes accessed | tf_op | source)
XLA Modules:
  0.0 218.1 jit_solution(8603617976995598589)
XLA Ops:
  0.6 1.0 pad_maximum_fusion.16
  1.6 5.8 %collective-permute-start.2 = (f32[2,12,4,512]{3,2,1,0:T(4,128)S(1)}, f32[2,12,4,512]{3,2,1,0:T(4,128)S(1)}, u32[]{:S(2)}, u32[]{:S(2)}) collective-permute-start(f32[2,12,4,512]{3,2,1,0:T(4,128)S(1)} %pad_maximum_fusion.16), channel_id=1, source_target_pairs={{2,0},{4,2},{6,4},{8,6},{10,8},{12,10},{14,12},{0,14},{3,1},{5,3},... | collective-permute-start | bytes 589832 | tf_op jit(solution)/shard_map/ppermute | solution.py:25
  7.4 2.0 collective-permute-start.3
  9.4 0.9 fusion.276
  10.3 2.0 collective-permute-start.4
  12.2 0.8 fusion.274
  13.1 6.0 %collective-permute-start.1 = (f32[2,4,4,512]{3,2,1,0:T(4,128)S(1)}, f32[2,4,4,512]{3,2,1,0:T(4,128)S(1)}, u32[]{:S(2)}, u32[]{:S(2)}) collective-permute-start(f32[2,4,4,512]{3,2,1,0:T(4,128)S(1)} %get-tuple-element.177), channel_id=1, source_target_pairs={{0,16},{16,32},{32,48},{48,64},{64,80},{80,96},{96,112},{112,128},... | collective-permute-start | bytes 196616 | tf_op jit(solution)/shard_map/ppermute | solution.py:24
  19.1 39.9 %collective-permute-start = (f32[2,4,4,512]{3,2,1,0:T(4,128)S(1)}, f32[2,4,4,512]{3,2,1,0:T(4,128)S(1)}, u32[]{:S(2)}, u32[]{:S(2)}) collective-permute-start(f32[2,4,4,512]{3,2,1,0:T(4,128)S(1)} %get-tuple-element.178), channel_id=1, source_target_pairs={{16,0},{32,16},{48,32},{64,48},{80,64},{96,80},{112,96},{128,112},... | collective-permute-start | bytes 196616 | tf_op jit(solution)/shard_map/ppermute | solution.py:25
  59.1 0.9 fusion.272
  60.0 1.4 fusion.293
  62.7 1.4 fusion.292
  64.1 0.8 fusion.291
  64.9 0.9 fusion.290
  65.9 1.8 fusion.20
  67.7 1.9 fusion.26
  69.6 1.9 fusion.32
  71.4 1.9 fusion.38
  75.0 2.5 %select_maximum_fusion.7 = (f32[2,20,12,516]{3,2,1,0:T(8,128)S(1)}, f32[2,20,12,516]{3,2,1,0:T(8,128)S(1)}) fusion(f32[2,12,4,4]{3,2,1,0:T(4,128)S(1)} %get-tuple-element.187, f32[2,20,4,512]{3,2,1,0:T(4,128)S(1)} %pad.88, f32[2,4,4,512]{3,2,1,0:T(4,128)S(1)} %broadcast_select_fusion.25, f32[1,12,4,512]{3,2,1,0:T(4,128)S(1)} %bitcast.40, ...), kind=kLoop, calls=%fused_computation.20 | loop fusion | flops 3962880 | bytes 2967552 | tf_op jit(solution)/shard_map/concatenate | solution.py:42
  77.6 1.7 fusion.165
  79.3 0.8 fusion.178
  80.2 5.2 %collective-permute-start.7 = (f32[2,12,4,512]{3,2,1,0:T(4,128)S(1)}, f32[2,12,4,512]{3,2,1,0:T(4,128)S(1)}, u32[]{:S(2)}, u32[]{:S(2)}) collective-permute-start(f32[2,12,4,512]{3,2,1,0:T(4,128)S(1)} %scatter-add.29), channel_id=1, source_target_pairs={{2,0},{4,2},{6,4},{8,6},{10,8},{12,10},{14,12},{0,14},{3,1},{5,3},... | collective-permute-start | bytes 589832 | tf_op jit(solution)/shard_map/ppermute | solution.py:25
  85.4 2.0 collective-permute-start.8
  87.4 2.0 collective-permute-start.9
  89.4 2.0 collective-permute-start.6
  91.4 5.3 %collective-permute-start.5 = (f32[2,4,4,512]{3,2,1,0:T(4,128)S(1)}, f32[2,4,4,512]{3,2,1,0:T(4,128)S(1)}, u32[]{:S(2)}, u32[]{:S(2)}) collective-permute-start(f32[2,4,4,512]{3,2,1,0:T(4,128)S(1)} %get-tuple-element.174), channel_id=1, source_target_pairs={{16,0},{32,16},{48,32},{64,48},{80,64},{96,80},{112,96},{128,112},... | collective-permute-start | bytes 196616 | tf_op jit(solution)/shard_map/ppermute | solution.py:25
  97.1 1.4 collective-permute-done.5
  98.7 1.2 select_maximum_fusion.5
  99.9 1.4 add_divide_fusion.2
  101.3 0.8 fusion.180
  102.2 5.2 %collective-permute-start.12 = (f32[2,12,4,512]{3,2,1,0:T(4,128)S(1)}, f32[2,12,4,512]{3,2,1,0:T(4,128)S(1)}, u32[]{:S(2)}, u32[]{:S(2)}) collective-permute-start(f32[2,12,4,512]{3,2,1,0:T(4,128)S(1)} %scatter-add.31), channel_id=1, source_target_pairs={{2,0},{4,2},{6,4},{8,6},{10,8},{12,10},{14,12},{0,14},{3,1},{5,3},... | collective-permute-start | bytes 589832 | tf_op jit(solution)/shard_map/ppermute | solution.py:25
  107.3 2.0 collective-permute-start.13
  109.4 2.0 collective-permute-start.14
  111.4 2.0 collective-permute-start.11
  113.4 5.5 %collective-permute-start.10 = (f32[2,4,4,512]{3,2,1,0:T(4,128)S(1)}, f32[2,4,4,512]{3,2,1,0:T(4,128)S(1)}, u32[]{:S(2)}, u32[]{:S(2)}) collective-permute-start(f32[2,4,4,512]{3,2,1,0:T(4,128)S(1)} %get-tuple-element.172), channel_id=1, source_target_pairs={{16,0},{32,16},{48,32},{64,48},{80,64},{96,80},{112,96},{128,112},... | collective-permute-start | bytes 196616 | tf_op jit(solution)/shard_map/ppermute | solution.py:25
  119.0 4.0 %collective-permute-start.20 = (f32[2,8,4,512]{3,1,2,0:T(8,128)S(1)}, f32[2,8,4,512]{3,1,2,0:T(8,128)S(1)}, u32[]{:S(2)}, u32[]{:S(2)}) collective-permute-start(f32[2,8,4,512]{3,1,2,0:T(8,128)S(1)} %copy.660), channel_id=1, source_target_pairs={{16,0},{32,16},{48,32},{64,48},{80,64},{96,80},{112,96},{128,112},... | collective-permute-start | bytes 393224 | tf_op jit(solution)/shard_map/ppermute | solution.py:25
  123.0 2.0 collective-permute-start.21
  125.0 1.5 collective-permute-done.20
  126.7 4.5 %collective-permute-done.21 = f32[2,8,4,512]{3,1,2,0:T(8,128)S(1)} collective-permute-done((f32[2,8,4,512]{3,1,2,0:T(8,128)S(1)}, f32[2,8,4,512]{3,1,2,0:T(8,128)S(1)}, u32[]{:S(2)}, u32[]{:S(2)}) %collective-permute-start.21) | collective-permute-done | bytes 131104 | tf_op jit(solution)/shard_map/ppermute | solution.py:24
  133.0 1.2 select_maximum_fusion.3
  134.2 1.4 add_divide_fusion.1
  136.4 5.2 %collective-permute-start.17 = (f32[2,12,4,512]{3,2,1,0:T(4,128)S(1)}, f32[2,12,4,512]{3,2,1,0:T(4,128)S(1)}, u32[]{:S(2)}, u32[]{:S(2)}) collective-permute-start(f32[2,12,4,512]{3,2,1,0:T(4,128)S(1)} %scatter-add.35), channel_id=1, source_target_pairs={{2,0},{4,2},{6,4},{8,6},{10,8},{12,10},{14,12},{0,14},{3,1},{5,3},... | collective-permute-start | bytes 589832 | tf_op jit(solution)/shard_map/ppermute | solution.py:25
  141.6 2.0 collective-permute-start.18
  143.6 2.0 collective-permute-start.19
  145.6 2.0 collective-permute-start.16
  147.5 5.2 %collective-permute-start.15 = (f32[2,4,4,512]{3,2,1,0:T(4,128)S(1)}, f32[2,4,4,512]{3,2,1,0:T(4,128)S(1)}, u32[]{:S(2)}, u32[]{:S(2)}) collective-permute-start(f32[2,4,4,512]{3,2,1,0:T(4,128)S(1)} %get-tuple-element.170), channel_id=1, source_target_pairs={{16,0},{32,16},{48,32},{64,48},{80,64},{96,80},{112,96},{128,112},... | collective-permute-start | bytes 196616 | tf_op jit(solution)/shard_map/ppermute | solution.py:25
  153.2 1.4 collective-permute-done.15
  154.9 1.2 select_maximum_fusion.1
  156.1 1.4 add_divide_fusion
  159.1 5.7 %collective-permute-start.22 = (f32[2,8,4,512]{3,1,2,0:T(8,128)}, f32[2,8,4,512]{3,1,2,0:T(8,128)}, u32[]{:S(2)}, u32[]{:S(2)}) collective-permute-start(f32[2,8,4,512]{3,1,2,0:T(8,128)} %copy.680), channel_id=1, source_target_pairs={{16,0},{32,16},{48,32},{64,48},{80,64},{96,80},{112,96},{128,112},... | collective-permute-start | bytes 393224 | tf_op jit(solution)/shard_map/ppermute | solution.py:25
  165.4 2.4 %stack.22 = f32[16,12,4,512]{3,0,2,1:T(8,128)S(1)} concatenate(f32[1,12,4,512]{3,0,2,1:T(1,128)S(1)} %copy.664, f32[1,12,4,512]{3,0,2,1:T(1,128)S(1)} %copy.665, f32[1,12,4,512]{3,0,2,1:T(1,128)S(1)} %copy.666, f32[1,12,4,512]{3,0,2,1:T(1,128)S(1)} %copy.667, f32[1,12,4,512]{3,0,2,1:T(1,128)S(1)} %copy.668, f32[1,12,4,512]{3,0,2,1:T(1,128)S(1)} %copy.669, ...), dimensions={0} | concatenate | bytes 3145728 | tf_op jit(solution)/shard_map/stack | solution.py:95
  168.0 2.0 collective-permute-start.23
  169.9 0.9 broadcast_select_fusion.15
  170.9 5.1 %collective-permute-done.23 = f32[2,8,4,512]{3,1,2,0:T(8,128)S(1)} collective-permute-done((f32[2,8,4,512]{3,1,2,0:T(8,128)S(1)}, f32[2,8,4,512]{3,1,2,0:T(8,128)S(1)}, u32[]{:S(2)}, u32[]{:S(2)}) %collective-permute-start.23) | collective-permute-done | bytes 131104 | tf_op jit(solution)/shard_map/ppermute | solution.py:24
  187.2 4.9 %stack.23 = f32[16,12,4,512]{3,0,2,1:T(8,128)S(1)} concatenate(f32[1,12,4,512]{3,0,2,1:T(1,128)} %copy.684, f32[1,12,4,512]{3,0,2,1:T(1,128)} %copy.685, f32[1,12,4,512]{3,0,2,1:T(1,128)} %copy.686, f32[1,12,4,512]{3,0,2,1:T(1,128)} %copy.687, f32[1,12,4,512]{3,0,2,1:T(1,128)} %copy.688, f32[1,12,4,512]{3,0,2,1:T(1,128)} %copy.689, f32[1,12,4,512]{3,0,2,1:T(1,128)S(1)} %copy.690, ...), dimensions={0} | concatenate | bytes 3145728 | tf_op jit(solution)/shard_map/stack | solution.py:95
  192.8 2.0 collective-permute-start.28
  194.8 5.2 %collective-permute-start.26 = (f32[16,12,1,512]{3,0,2,1:T(8,128)S(1)}, f32[16,12,1,512]{3,0,2,1:T(8,128)S(1)}, u32[]{:S(2)}, u32[]{:S(2)}) collective-permute-start(f32[16,12,1,512]{3,0,2,1:T(8,128)S(1)} %get-tuple-element.120), channel_id=1, source_target_pairs={{2,0},{4,2},{6,4},{8,6},{10,8},{12,10},{14,12},{0,14},{3,1},{5,3},... | collective-permute-start | bytes 1179656 | tf_op jit(solution)/shard_map/ppermute | solution.py:25
  199.9 2.0 collective-permute-start.27
  201.9 2.0 collective-permute-start.25
  203.9 5.2 %collective-permute-start.24 = (f32[16,1,4,512]{3,0,2,1:T(8,128)S(1)}, f32[16,1,4,512]{3,0,2,1:T(8,128)S(1)}, u32[]{:S(2)}, u32[]{:S(2)}) collective-permute-start(f32[16,1,4,512]{3,0,2,1:T(8,128)S(1)} %get-tuple-element.118), channel_id=1, source_target_pairs={{16,0},{32,16},{48,32},{64,48},{80,64},{96,80},{112,96},{128,112},... | collective-permute-start | bytes 393224 | tf_op jit(solution)/shard_map/ppermute | solution.py:25
  209.1 1.5 collective-permute-done.25
  210.7 1.2 collective-permute-done.24
  212.0 2.3 %collective-permute-done.27 = f32[16,12,1,512]{3,0,2,1:T(8,128)S(1)} collective-permute-done((f32[16,12,1,512]{3,0,2,1:T(8,128)S(1)}, f32[16,12,1,512]{3,0,2,1:T(8,128)S(1)}, u32[]{:S(2)}, u32[]{:S(2)}) %collective-permute-start.27) | collective-permute-done | bytes 393248 | tf_op jit(solution)/shard_map/ppermute | solution.py:24
  214.4 2.2 fusion.11
  216.6 1.5 copy.700
  (150 shorter events, 21.7 us)
Async XLA Ops:
  1.6 73.1 %collective-permute-start.2 = (f32[2,12,4,512]{3,2,1,0:T(4,128)S(1)}, f32[2,12,4,512]{3,2,1,0:T(4,128)S(1)}, u32[]{:S(2)}, u32[]{:S(2)}) collective-permute-start(f32[2,12,4,512]{3,2,1,0:T(4,128)S(1)} %pad_maximum_fusion.16), channel_id=1, source_target_pairs={{2,0},{4,2},{6,4},{8,6},{10,8},{12,10},{14,12},{0,14},{3,1},{5,3},... | collective-permute-start | bytes 589832 | tf_op jit(solution)/shard_map/ppermute | solution.py:25
  7.4 67.4 %collective-permute-start.3 = (f32[2,12,4,512]{3,2,1,0:T(4,128)S(1)}, f32[2,12,4,512]{3,2,1,0:T(4,128)S(1)}, u32[]{:S(2)}, u32[]{:S(2)}) collective-permute-start(f32[2,12,4,512]{3,2,1,0:T(4,128)S(1)} %pad_maximum_fusion.16), channel_id=1, source_target_pairs={{0,2},{2,4},{4,6},{6,8},{8,10},{10,12},{12,14},{14,0},{1,3},{3,5},... | collective-permute-start | bytes 589832 | tf_op jit(solution)/shard_map/ppermute | solution.py:24
  10.3 64.2 %collective-permute-start.4 = (f32[2,12,4,4]{3,2,1,0:T(4,128)S(1)}, f32[2,12,4,4]{3,2,1,0:T(4,128)S(1)}, u32[]{:S(2)}, u32[]{:S(2)}) collective-permute-start(f32[2,12,4,4]{3,2,1,0:T(4,128)S(1)} %fusion.276), channel_id=1, source_target_pairs={{0,1},{1,0},{2,3},{3,2},{4,5},{5,4},{6,7},{7,6},{8,9},{9,8},{10,11... | collective-permute-start | bytes 4616 | tf_op jit(solution)/shard_map/ppermute | solution.py:20
  13.1 61.5 %collective-permute-start.1 = (f32[2,4,4,512]{3,2,1,0:T(4,128)S(1)}, f32[2,4,4,512]{3,2,1,0:T(4,128)S(1)}, u32[]{:S(2)}, u32[]{:S(2)}) collective-permute-start(f32[2,4,4,512]{3,2,1,0:T(4,128)S(1)} %get-tuple-element.177), channel_id=1, source_target_pairs={{0,16},{16,32},{32,48},{48,64},{64,80},{80,96},{96,112},{112,128},... | collective-permute-start | bytes 196616 | tf_op jit(solution)/shard_map/ppermute | solution.py:24
  19.1 55.5 %collective-permute-start = (f32[2,4,4,512]{3,2,1,0:T(4,128)S(1)}, f32[2,4,4,512]{3,2,1,0:T(4,128)S(1)}, u32[]{:S(2)}, u32[]{:S(2)}) collective-permute-start(f32[2,4,4,512]{3,2,1,0:T(4,128)S(1)} %get-tuple-element.178), channel_id=1, source_target_pairs={{16,0},{32,16},{48,32},{64,48},{80,64},{96,80},{112,96},{128,112},... | collective-permute-start | bytes 196616 | tf_op jit(solution)/shard_map/ppermute | solution.py:25
  69.6 5.0 %copy-start = (f32[12,4,512]{2,1,0:T(4,128)S(1)}, f32[12,4,512]{2,1,0:T(4,128)}, u32[]{:S(2)}) copy-start(f32[12,4,512]{2,1,0:T(4,128)} %param.27) | copy-start | bytes 294916
  69.6 5.0 %copy-start.1 = (f32[12,4,512]{2,1,0:T(4,128)S(1)}, f32[12,4,512]{2,1,0:T(4,128)}, u32[]{:S(2)}) copy-start(f32[12,4,512]{2,1,0:T(4,128)} %param.29) | copy-start | bytes 294916
  74.9 2.6 %copy-start.2 = (f32[12,4,512]{2,1,0:T(4,128)S(1)}, f32[12,4,512]{2,1,0:T(4,128)}, u32[]{:S(2)}) copy-start(f32[12,4,512]{2,1,0:T(4,128)} %param.30) | copy-start | bytes 294916
  75.0 2.6 %copy-start.3 = (f32[12,4,512]{2,1,0:T(4,128)S(1)}, f32[12,4,512]{2,1,0:T(4,128)}, u32[]{:S(2)}) copy-start(f32[12,4,512]{2,1,0:T(4,128)} %param.28) | copy-start | bytes 294916
  75.0 2.6 %copy-start.4 = (f32[12,4,512]{2,1,0:T(4,128)S(1)}, f32[12,4,512]{2,1,0:T(4,128)}, u32[]{:S(2)}) copy-start(f32[12,4,512]{2,1,0:T(4,128)} %param.26) | copy-start | bytes 294916
  80.2 18.2 %collective-permute-start.7 = (f32[2,12,4,512]{3,2,1,0:T(4,128)S(1)}, f32[2,12,4,512]{3,2,1,0:T(4,128)S(1)}, u32[]{:S(2)}, u32[]{:S(2)}) collective-permute-start(f32[2,12,4,512]{3,2,1,0:T(4,128)S(1)} %scatter-add.29), channel_id=1, source_target_pairs={{2,0},{4,2},{6,4},{8,6},{10,8},{12,10},{14,12},{0,14},{3,1},{5,3},... | collective-permute-start | bytes 589832 | tf_op jit(solution)/shard_map/ppermute | solution.py:25
  85.4 13.2 %collective-permute-start.8 = (f32[2,12,4,512]{3,2,1,0:T(4,128)S(1)}, f32[2,12,4,512]{3,2,1,0:T(4,128)S(1)}, u32[]{:S(2)}, u32[]{:S(2)}) collective-permute-start(f32[2,12,4,512]{3,2,1,0:T(4,128)S(1)} %scatter-add.29), channel_id=1, source_target_pairs={{0,2},{2,4},{4,6},{6,8},{8,10},{10,12},{12,14},{14,0},{1,3},{3,5},... | collective-permute-start | bytes 589832 | tf_op jit(solution)/shard_map/ppermute | solution.py:24
  87.4 9.3 %collective-permute-start.9 = (f32[2,12,4,4]{3,2,1,0:T(4,128)S(1)}, f32[2,12,4,4]{3,2,1,0:T(4,128)S(1)}, u32[]{:S(2)}, u32[]{:S(2)}) collective-permute-start(f32[2,12,4,4]{3,2,1,0:T(4,128)S(1)} %slice_select_fusion.3), channel_id=1, source_target_pairs={{0,1},{1,0},{2,3},{3,2},{4,5},{5,4},{6,7},{7,6},{8,9},{9,8},{10,11... | collective-permute-start | bytes 4616 | tf_op jit(solution)/shard_map/ppermute | solution.py:20
  89.4 7.6 %collective-permute-start.6 = (f32[2,4,4,512]{3,2,1,0:T(4,128)S(1)}, f32[2,4,4,512]{3,2,1,0:T(4,128)S(1)}, u32[]{:S(2)}, u32[]{:S(2)}) collective-permute-start(f32[2,4,4,512]{3,2,1,0:T(4,128)S(1)} %get-tuple-element.173), channel_id=1, source_target_pairs={{0,16},{16,32},{32,48},{48,64},{64,80},{80,96},{96,112},{112,128},... | collective-permute-start | bytes 196616 | tf_op jit(solution)/shard_map/ppermute | solution.py:24
  91.4 7.1 %collective-permute-start.5 = (f32[2,4,4,512]{3,2,1,0:T(4,128)S(1)}, f32[2,4,4,512]{3,2,1,0:T(4,128)S(1)}, u32[]{:S(2)}, u32[]{:S(2)}) collective-permute-start(f32[2,4,4,512]{3,2,1,0:T(4,128)S(1)} %get-tuple-element.174), channel_id=1, source_target_pairs={{16,0},{32,16},{48,32},{64,48},{80,64},{96,80},{112,96},{128,112},... | collective-permute-start | bytes 196616 | tf_op jit(solution)/shard_map/ppermute | solution.py:25
  102.2 30.6 %collective-permute-start.12 = (f32[2,12,4,512]{3,2,1,0:T(4,128)S(1)}, f32[2,12,4,512]{3,2,1,0:T(4,128)S(1)}, u32[]{:S(2)}, u32[]{:S(2)}) collective-permute-start(f32[2,12,4,512]{3,2,1,0:T(4,128)S(1)} %scatter-add.31), channel_id=1, source_target_pairs={{2,0},{4,2},{6,4},{8,6},{10,8},{12,10},{14,12},{0,14},{3,1},{5,3},... | collective-permute-start | bytes 589832 | tf_op jit(solution)/shard_map/ppermute | solution.py:25
  107.3 25.5 %collective-permute-start.13 = (f32[2,12,4,512]{3,2,1,0:T(4,128)S(1)}, f32[2,12,4,512]{3,2,1,0:T(4,128)S(1)}, u32[]{:S(2)}, u32[]{:S(2)}) collective-permute-start(f32[2,12,4,512]{3,2,1,0:T(4,128)S(1)} %scatter-add.31), channel_id=1, source_target_pairs={{0,2},{2,4},{4,6},{6,8},{8,10},{10,12},{12,14},{14,0},{1,3},{3,5},... | collective-permute-start | bytes 589832 | tf_op jit(solution)/shard_map/ppermute | solution.py:24
  109.4 9.6 %collective-permute-start.14 = (f32[2,12,4,4]{3,2,1,0:T(4,128)S(1)}, f32[2,12,4,4]{3,2,1,0:T(4,128)S(1)}, u32[]{:S(2)}, u32[]{:S(2)}) collective-permute-start(f32[2,12,4,4]{3,2,1,0:T(4,128)S(1)} %slice_select_fusion.2), channel_id=1, source_target_pairs={{0,1},{1,0},{2,3},{3,2},{4,5},{5,4},{6,7},{7,6},{8,9},{9,8},{10,11... | collective-permute-start | bytes 4616 | tf_op jit(solution)/shard_map/ppermute | solution.py:20
  111.4 11.6 %collective-permute-start.11 = (f32[2,4,4,512]{3,2,1,0:T(4,128)S(1)}, f32[2,4,4,512]{3,2,1,0:T(4,128)S(1)}, u32[]{:S(2)}, u32[]{:S(2)}) collective-permute-start(f32[2,4,4,512]{3,2,1,0:T(4,128)S(1)} %get-tuple-element.171), channel_id=1, source_target_pairs={{0,16},{16,32},{32,48},{48,64},{64,80},{80,96},{96,112},{112,128},... | collective-permute-start | bytes 196616 | tf_op jit(solution)/shard_map/ppermute | solution.py:24
  113.4 11.6 %collective-permute-start.10 = (f32[2,4,4,512]{3,2,1,0:T(4,128)S(1)}, f32[2,4,4,512]{3,2,1,0:T(4,128)S(1)}, u32[]{:S(2)}, u32[]{:S(2)}) collective-permute-start(f32[2,4,4,512]{3,2,1,0:T(4,128)S(1)} %get-tuple-element.172), channel_id=1, source_target_pairs={{16,0},{32,16},{48,32},{64,48},{80,64},{96,80},{112,96},{128,112},... | collective-permute-start | bytes 196616 | tf_op jit(solution)/shard_map/ppermute | solution.py:25
  119.0 7.5 %collective-permute-start.20 = (f32[2,8,4,512]{3,1,2,0:T(8,128)S(1)}, f32[2,8,4,512]{3,1,2,0:T(8,128)S(1)}, u32[]{:S(2)}, u32[]{:S(2)}) collective-permute-start(f32[2,8,4,512]{3,1,2,0:T(8,128)S(1)} %copy.660), channel_id=1, source_target_pairs={{16,0},{32,16},{48,32},{64,48},{80,64},{96,80},{112,96},{128,112},... | collective-permute-start | bytes 393224 | tf_op jit(solution)/shard_map/ppermute | solution.py:25
  123.0 8.2 %collective-permute-start.21 = (f32[2,8,4,512]{3,1,2,0:T(8,128)S(1)}, f32[2,8,4,512]{3,1,2,0:T(8,128)S(1)}, u32[]{:S(2)}, u32[]{:S(2)}) collective-permute-start(f32[2,8,4,512]{3,1,2,0:T(8,128)S(1)} %copy.662), channel_id=1, source_target_pairs={{0,16},{16,32},{32,48},{48,64},{64,80},{80,96},{96,112},{112,128},... | collective-permute-start | bytes 393224 | tf_op jit(solution)/shard_map/ppermute | solution.py:24
  136.4 18.2 %collective-permute-start.17 = (f32[2,12,4,512]{3,2,1,0:T(4,128)S(1)}, f32[2,12,4,512]{3,2,1,0:T(4,128)S(1)}, u32[]{:S(2)}, u32[]{:S(2)}) collective-permute-start(f32[2,12,4,512]{3,2,1,0:T(4,128)S(1)} %scatter-add.35), channel_id=1, source_target_pairs={{2,0},{4,2},{6,4},{8,6},{10,8},{12,10},{14,12},{0,14},{3,1},{5,3},... | collective-permute-start | bytes 589832 | tf_op jit(solution)/shard_map/ppermute | solution.py:25
  141.6 13.2 %collective-permute-start.18 = (f32[2,12,4,512]{3,2,1,0:T(4,128)S(1)}, f32[2,12,4,512]{3,2,1,0:T(4,128)S(1)}, u32[]{:S(2)}, u32[]{:S(2)}) collective-permute-start(f32[2,12,4,512]{3,2,1,0:T(4,128)S(1)} %scatter-add.35), channel_id=1, source_target_pairs={{0,2},{2,4},{4,6},{6,8},{8,10},{10,12},{12,14},{14,0},{1,3},{3,5},... | collective-permute-start | bytes 589832 | tf_op jit(solution)/shard_map/ppermute | solution.py:24
  143.6 9.1 %collective-permute-start.19 = (f32[2,12,4,4]{3,2,1,0:T(4,128)S(1)}, f32[2,12,4,4]{3,2,1,0:T(4,128)S(1)}, u32[]{:S(2)}, u32[]{:S(2)}) collective-permute-start(f32[2,12,4,4]{3,2,1,0:T(4,128)S(1)} %slice_select_fusion.1), channel_id=1, source_target_pairs={{0,1},{1,0},{2,3},{3,2},{4,5},{5,4},{6,7},{7,6},{8,9},{9,8},{10,11... | collective-permute-start | bytes 4616 | tf_op jit(solution)/shard_map/ppermute | solution.py:20
  145.6 7.6 %collective-permute-start.16 = (f32[2,4,4,512]{3,2,1,0:T(4,128)S(1)}, f32[2,4,4,512]{3,2,1,0:T(4,128)S(1)}, u32[]{:S(2)}, u32[]{:S(2)}) collective-permute-start(f32[2,4,4,512]{3,2,1,0:T(4,128)S(1)} %get-tuple-element.169), channel_id=1, source_target_pairs={{0,16},{16,32},{32,48},{48,64},{64,80},{80,96},{96,112},{112,128},... | collective-permute-start | bytes 196616 | tf_op jit(solution)/shard_map/ppermute | solution.py:24
  147.5 7.1 %collective-permute-start.15 = (f32[2,4,4,512]{3,2,1,0:T(4,128)S(1)}, f32[2,4,4,512]{3,2,1,0:T(4,128)S(1)}, u32[]{:S(2)}, u32[]{:S(2)}) collective-permute-start(f32[2,4,4,512]{3,2,1,0:T(4,128)S(1)} %get-tuple-element.170), channel_id=1, source_target_pairs={{16,0},{32,16},{48,32},{64,48},{80,64},{96,80},{112,96},{128,112},... | collective-permute-start | bytes 196616 | tf_op jit(solution)/shard_map/ppermute | solution.py:25
  159.1 10.9 %collective-permute-start.22 = (f32[2,8,4,512]{3,1,2,0:T(8,128)}, f32[2,8,4,512]{3,1,2,0:T(8,128)}, u32[]{:S(2)}, u32[]{:S(2)}) collective-permute-start(f32[2,8,4,512]{3,1,2,0:T(8,128)} %copy.680), channel_id=1, source_target_pairs={{16,0},{32,16},{48,32},{64,48},{80,64},{96,80},{112,96},{128,112},... | collective-permute-start | bytes 393224 | tf_op jit(solution)/shard_map/ppermute | solution.py:25
  168.0 8.1 %collective-permute-start.23 = (f32[2,8,4,512]{3,1,2,0:T(8,128)S(1)}, f32[2,8,4,512]{3,1,2,0:T(8,128)S(1)}, u32[]{:S(2)}, u32[]{:S(2)}) collective-permute-start(f32[2,8,4,512]{3,1,2,0:T(8,128)S(1)} %copy.682), channel_id=1, source_target_pairs={{0,16},{16,32},{32,48},{48,64},{64,80},{80,96},{96,112},{112,128},... | collective-permute-start | bytes 393224 | tf_op jit(solution)/shard_map/ppermute | solution.py:24
  192.8 16.2 %collective-permute-start.28 = (f32[16,12,4,1]{3,0,2,1:T(8,128)S(1)}, f32[16,12,4,1]{3,0,2,1:T(8,128)S(1)}, u32[]{:S(2)}, u32[]{:S(2)}) collective-permute-start(f32[16,12,4,1]{3,0,2,1:T(8,128)S(1)} %slice_select_fusion), channel_id=1, source_target_pairs={{0,1},{1,0},{2,3},{3,2},{4,5},{5,4},{6,7},{7,6},{8,9},{9,8},{10,11... | collective-permute-start | bytes 9224 | tf_op jit(solution)/shard_map/ppermute | solution.py:20
  194.8 17.1 %collective-permute-start.26 = (f32[16,12,1,512]{3,0,2,1:T(8,128)S(1)}, f32[16,12,1,512]{3,0,2,1:T(8,128)S(1)}, u32[]{:S(2)}, u32[]{:S(2)}) collective-permute-start(f32[16,12,1,512]{3,0,2,1:T(8,128)S(1)} %get-tuple-element.120), channel_id=1, source_target_pairs={{2,0},{4,2},{6,4},{8,6},{10,8},{12,10},{14,12},{0,14},{3,1},{5,3},... | collective-permute-start | bytes 1179656 | tf_op jit(solution)/shard_map/ppermute | solution.py:25
  199.9 14.4 %collective-permute-start.27 = (f32[16,12,1,512]{3,0,2,1:T(8,128)S(1)}, f32[16,12,1,512]{3,0,2,1:T(8,128)S(1)}, u32[]{:S(2)}, u32[]{:S(2)}) collective-permute-start(f32[16,12,1,512]{3,0,2,1:T(8,128)S(1)} %get-tuple-element.119), channel_id=1, source_target_pairs={{0,2},{2,4},{4,6},{6,8},{8,10},{10,12},{12,14},{14,0},{1,3},{3,5},... | collective-permute-start | bytes 1179656 | tf_op jit(solution)/shard_map/ppermute | solution.py:24
  201.9 8.8 %collective-permute-start.25 = (f32[16,1,4,512]{3,0,2,1:T(8,128)S(1)}, f32[16,1,4,512]{3,0,2,1:T(8,128)S(1)}, u32[]{:S(2)}, u32[]{:S(2)}) collective-permute-start(f32[16,1,4,512]{3,0,2,1:T(8,128)S(1)} %get-tuple-element.117), channel_id=1, source_target_pairs={{0,16},{16,32},{32,48},{48,64},{64,80},{80,96},{96,112},{112,128},... | collective-permute-start | bytes 393224 | tf_op jit(solution)/shard_map/ppermute | solution.py:24
  203.9 8.0 %collective-permute-start.24 = (f32[16,1,4,512]{3,0,2,1:T(8,128)S(1)}, f32[16,1,4,512]{3,0,2,1:T(8,128)S(1)}, u32[]{:S(2)}, u32[]{:S(2)}) collective-permute-start(f32[16,1,4,512]{3,0,2,1:T(8,128)S(1)} %get-tuple-element.118), channel_id=1, source_target_pairs={{16,0},{32,16},{48,32},{64,48},{80,64},{96,80},{112,96},{128,112},... | collective-permute-start | bytes 393224 | tf_op jit(solution)/shard_map/ppermute | solution.py:25

commit v2 on v1

v2 whole, which is shorter than its diff:
```python
import functools

import jax
import jax.numpy as jnp
from jax import lax
from jax.experimental import pallas as pl
from jax.experimental.pallas import tpu as pltpu
from jax.sharding import PartitionSpec as P

LAGS = 16
STEPS = 4
EVERY = 2
LANES = 128
HALF = LAGS // 2
WIDE = HALF + 1

stencil_weights = (8.0 / 5.0, -1.0 / 5.0, 8.0 / 315.0, -1.0 / 560.0)
centre_weight = -205.0 / 72.0


def pairs(size):
    near = [(i, i ^ 1) for i in range(size)]
    far = [(i, (i + 1) % size if i % 2 else (i - 1) % size) for i in range(size)]
    return near, far


def swap(a, b, axis):
    near, far = pairs(lax.axis_size(axis))
    return lax.ppermute(a, axis, near), lax.ppermute(b, axis, far)


def cross(a):
    return lax.ppermute(a, "gz", [(0, 1), (1, 0)])


def rows():
    return lax.broadcasted_iota(jnp.int32, (8, LANES), 0)


def lanes():
    return lax.broadcasted_iota(jnp.int32, (8, LANES), 1)


def place(axis):
    index = lax.axis_index(axis)
    return index, lax.rem(index, 2) == 1, index > 0, index < lax.axis_size(axis) - 1


def chunk(j):
    return slice(j * LANES, (j + 1) * LANES)


def kept(flag, value):
    return jnp.where(flag, value, jnp.zeros_like(value))


def call(body, outs, *args, scratch=(), smem=(), far=(), far_outs=()):
    args = [
        a if i in far or i in smem else pltpu.with_memory_space_constraint(a, pltpu.VMEM)
        for i, a in enumerate(args)
    ]
    return pl.pallas_call(
        body,
        out_shape=[
            jax.ShapeDtypeStruct(s, d) if i in far_outs else pltpu.VMEM(s, d)
            for i, (s, d) in enumerate(outs)
        ],
        in_specs=[
            pl.BlockSpec(memory_space=pltpu.SMEM if i in smem else pltpu.VMEM)
            for i in range(len(args))
        ],
        out_specs=[pl.BlockSpec(memory_space=pltpu.VMEM)] * len(outs),
        scratch_shapes=list(scratch),
        compiler_params=pltpu.CompilerParams(vmem_limit_bytes=8 * 2**20),
        name=body.func.__name__ if isinstance(body, functools.partial) else body.__name__,
    )(*args)


def put_sides(tile, a_ref, b_ref, width):
    odd = place("gx")[1]
    size = tile.shape[0]
    for k in range(width):
        low, high = tile[k], tile[size - width + k]
        a_ref[k] = jnp.where(odd, low, high)
        b_ref[k] = jnp.where(odd, high, low)


def put_edge(tile, z_ref, at=0):
    last = place("gz")[0] == 0
    for k in range(tile.shape[0]):
        z_ref[at + k] = jnp.where(last, tile[k, :, -LANES:], tile[k, :, :LANES])


def pack(source, receiver, tile, a_ref, b_ref, z_ref):
    for k in range(tile.shape[0]):
        tile[k, 0:4] = source[k]
        tile[k, 4:8] = receiver[k]
    put_sides(tile, a_ref, b_ref, 4)
    put_edge(tile, z_ref)


def prepare(cell, wavelet, spots, traces, courant, absorbing, source, receiver, coef, before, inject, code_ref, amp_ref):
    size_x, size_y, size_z = courant.shape
    for k in range(size_x):
        before[k, 0:4] = source[k]
        before[k, 4:8] = receiver[k]
        damping = absorbing[k].astype(jnp.float32) / 16.0
        inverse = 1.0 / (1.0 + damping)
        for half in (slice(0, 4), slice(4, 8)):
            coef[0, k, half] = 2.0 * inverse
            coef[1, k, half] = (1.0 - damping) * inverse
            coef[2, k, half] = courant[k] * inverse
    gx, gy, gz = (lax.axis_index(a) for a in ("gx", "gy", "gz"))
    sx, sy, sz = cell[0] - gx * size_x, cell[1] - gy * size_y, cell[2] - gz * size_z
    at_x, at_y = spots[0:1] - gx * size_x, spots[1:2] - gy * size_y
    inside = (at_x >= 0) & (at_x < size_x) & (at_y >= 0) & (at_y < size_y) & (gz == 0)
    code = jnp.where(inside, at_x * 8 + at_y + 4, -1)
    blocks = code.shape[1] // LANES
    for b in range(blocks):
        code_ref[b] = jnp.broadcast_to(code[:, chunk(b)], (8, LANES))
        for t in range(STEPS):
            amp_ref[t, b] = jnp.broadcast_to(traces[t : t + 1, chunk(b)], (8, LANES))
    row, lane = rows(), lanes()

    def each(k, carry):
        sums = [jnp.zeros((8, LANES), jnp.float32) for _ in range(STEPS)]
        for b in range(blocks):
            hit = code_ref[b] == row + k * 8
            for t in range(STEPS):
                sums[t] = sums[t] + jnp.where(hit, amp_ref[t, b], 0.0)
        for t in range(STEPS):
            sheet = jnp.where(lane == 0, jnp.sum(sums[t], axis=1, keepdims=True), 0.0)
            for j in range(size_z // LANES):
                spot = (row == sy) & (sy < 4) & (lane + j * LANES == sz) & (k == sx)
                point = jnp.where(spot, wavelet[t], 0.0)
                inject[t, k, :, chunk(j)] = point + sheet if j == 0 else point
        return carry

    lax.fori_loop(0, size_x, each, 0)


def forward(step, cur, prev, coef, inject, xa, xb, ya, yb, z, new):
    size_x, _, size_z = cur.shape
    count = size_z // LANES
    _, odd_x, below_x, above_x = place("gx")
    _, odd_y, below_y, above_y = place("gy")
    first = lax.axis_index("gz") == 0
    wide = xa.shape[0] if step == 2 else 4
    row, lane = lax.rem(rows(), 4), lanes()

    def at(x, j):
        if x < 0:
            return kept(below_x, jnp.where(odd_x, xa[wide + x, :, chunk(j)], xb[wide + x, :, chunk(j)]))
        if x >= size_x:
            return kept(above_x, jnp.where(odd_x, xb[x - size_x, :, chunk(j)], xa[x - size_x, :, chunk(j)]))
        return cur[x, :, chunk(j)]

    for x in range(size_x):
        own = [cur[x, :, chunk(j)] for j in range(count)]
        beyond = z[x]
        before, after = kept(jnp.logical_not(first), beyond), kept(first, beyond)
        along = [None] * count
        for k, weight in enumerate(stencil_weights, 1):
            up = [pltpu.roll(v, LANES - k, axis=1) for v in (*own, after)]
            down = [pltpu.roll(v, k, axis=1) for v in (before, *own)]
            for j in range(count):
                both = jnp.where(lane < LANES - k, up[j], up[j + 1]) + jnp.where(lane >= k, down[j + 1], down[j])
                both = both + at(x + k, j) + at(x - k, j)
                along[j] = weight * both if along[j] is None else along[j] + weight * both
        for j in range(count):
            s = chunk(j)
            centre = own[j]
            low = kept(below_y, jnp.where(odd_y, ya[x, :, s], yb[x, :, s]))
            high = kept(above_y, jnp.where(odd_y, yb[x, :, s], ya[x, :, s]))
            total = 3.0 * centre_weight * centre + along[j] + stencil_weights[3] * (low + high)
            for k, weight in enumerate(stencil_weights[:3], 1):
                up = jnp.where(row < 4 - k, pltpu.roll(centre, 8 - k, axis=0), pltpu.roll(high, 4 - k, axis=0))
                down = jnp.where(row >= k, pltpu.roll(centre, k, axis=0), pltpu.roll(low, 4 + k, axis=0))
                total = total + weight * (up + down)
            new[x, :, s] = (
                coef[0, x, :, s] * centre - coef[1, x, :, s] * prev[x, :, s] + coef[2, x, :, s] * total
            ) + inject[step, x, :, s]


def margin(ya, yb, x, s, row):
    _, odd, below, above = place("gy")
    low = kept(below, jnp.where(odd, ya[x, :, s], yb[x, :, s]))
    high = kept(above, jnp.where(odd, yb[x, :, s], ya[x, :, s]))
    return jnp.where(lax.rem(row, 4) == 0, high, low)


def put_margins(get, size_x, count, a_ref, b_ref, at):
    odd = place("gx")[1]
    row = rows()
    outer = (lax.rem(row, 4) == 0) | (lax.rem(row, 4) == 3)
    for i in range((WIDE + 1) // 2):
        for j in range(count):
            sides = []
            for start in (0, size_x - WIDE):
                one = get(start + 2 * i, j)
                if 2 * i + 1 < WIDE:
                    one = jnp.where(outer, one, pltpu.roll(get(start + 2 * i + 1, j), 2, axis=0))
                sides.append(one)
            a_ref[at + i, :, chunk(j)] = jnp.where(odd, sides[0], sides[1])
            b_ref[at + i, :, chunk(j)] = jnp.where(odd, sides[1], sides[0])


def around_x(x, s, cur, xa, xb):
    _, odd, below, above = place("gx")
    size_x = cur.shape[0]
    if x < 0:
        return kept(below, jnp.where(odd, xa[WIDE + x, :, s], xb[WIDE + x, :, s]))
    if x >= size_x:
        return kept(above, jnp.where(odd, xb[x - size_x, :, s], xa[x - size_x, :, s]))
    return cur[x, :, s]


def first_step(cur, prev, coef, inject, xa, xb, ya, yb, z, new, a_ref, b_ref, z_ref):
    forward(0, cur, prev, coef, inject, xa, xb, ya, yb, z, new)
    put_sides(new, a_ref, b_ref, 4)
    put_edge(new, z_ref)


def second_step(cur, prev, coef, inject, xa, xb, ya, yb, z, new, a_ref, b_ref, z_ref):
    forward(1, cur, prev, coef, inject, xa, xb, ya, yb, z, new)
    put_sides(new, a_ref, b_ref, WIDE)
    put_edge(new, z_ref)


def put_wide_edge(cur, xa, xb, z_ref, at):
    size_x, _, size_z = cur.shape
    last = lax.axis_index("gz") == 0
    for x in range(-WIDE, size_x + WIDE):
        ends = [around_x(x, s, cur, xa, xb) for s in (slice(size_z - LANES, size_z), slice(0, LANES))]
        z_ref[at + WIDE + x] = jnp.where(last, ends[0], ends[1])


def third_step(cur, prev, coef, inject, xa, xb, ya, yb, z, new, a_ref, b_ref, z_ref):
    forward(2, cur, prev, coef, inject, xa, xb, ya, yb, z, new)
    size_x, _, size_z = cur.shape
    put_sides(new, a_ref, b_ref, 4)
    row = rows()
    put_margins(lambda x, j: margin(ya, yb, x, chunk(j), row), size_x, size_z // LANES, a_ref, b_ref, 4)
    put_edge(new, z_ref)
    put_wide_edge(cur, xa, xb, z_ref, size_x)


def fourth_step(cur, prev, coef, inject, xa, xb, ya, yb, z, new, source, receiver, a_ref, b_ref, ya_ref, yb_ref):
    forward(3, cur, prev, coef, inject, xa, xb, ya, yb, z, new)
    size_x, _, size_z = cur.shape
    put_sides(new, a_ref, b_ref, WIDE)
    odd = place("gy")[1]
    row = lax.rem(rows(), 4)
    for x in range(size_x):
        source[x] = new[x, 0:4]
        receiver[x] = new[x, 4:8]
    for i in range(size_x // 4):
        for j in range(size_z // LANES):
            tops, bottoms = [], []
            for q in range(4):
                value = new[4 * i + q, :, chunk(j)]
                tops.append(value if q == 0 else pltpu.roll(value, 8 - q, axis=0))
                bottoms.append(pltpu.roll(value, 3 - q, axis=0) if q < 3 else value)
            high, low = tops[0], bottoms[0]
            for q in range(1, 4):
                high = jnp.where(row == 3 - q, tops[q], high)
                low = jnp.where(row == 3 - q, bottoms[q], low)
            ya_ref[i, :, chunk(j)] = jnp.where(odd, low, high)
            yb_ref[i, :, chunk(j)] = jnp.where(odd, high, low)


def gather_edges(cur, xa, xb, ya, yb, margins, a_ref, b_ref, z_ref):
    size_x, _, size_z = cur.shape
    _, odd, below, above = place("gy")
    row = lax.rem(rows(), 4)
    for x in range(size_x):
        i, q = divmod(x, 4)
        for j in range(size_z // LANES):
            s = chunk(j)
            low = kept(below, jnp.where(odd, ya[i, :, s], yb[i, :, s]))
            high = kept(above, jnp.where(odd, yb[i, :, s], ya[i, :, s]))
            if q:
                low = pltpu.roll(low, q, axis=0)
            high = pltpu.roll(high, (q + 5) % 8, axis=0)
            margins[x, :, s] = jnp.where(row == 0, high, low)
    put_margins(lambda x, j: margins[x, :, chunk(j)], size_x, size_z // LANES, a_ref, b_ref, 0)
    put_wide_edge(cur, xa, xb, z_ref, 0)


def widen(get_margin, cur, xa, xb, ma, mb, m_at, zw, z_at, first_ref, second_ref, first_z, second_z):
    size_x, _, size_z = cur.shape
    _, odd, below, above = place("gx")
    row = rows()
    own = row < 4
    for x in range(-WIDE, size_x + WIDE):
        e = x + WIDE
        for j in range(size_z // LANES):
            s = chunk(j)
            if 0 <= x < size_x:
                edge = get_margin(x, s)
            else:
                k = e if x < 0 else x - size_x
                i, other = divmod(k, 2)
                near, far = ma[m_at + i, :, s], mb[m_at + i, :, s]
                edge = kept(below, jnp.where(odd, near, far)) if x < 0 else kept(above, jnp.where(odd, far, near))
                if other:
                    edge = pltpu.roll(edge, 6, axis=0)
            both = around_x(x, s, cur, xa, xb)
            first_ref[e, :, s] = jnp.where(own, both, pltpu.roll(edge, 4, axis=0))
            second_ref[e, :, s] = jnp.where(own, pltpu.roll(both, 4, axis=0), edge)
        first_z[e] = zw[z_at + e]
        second_z[e] = pltpu.roll(zw[z_at + e], 4, axis=0)


def early(cur, xa, xb, ya, yb, ma, mb, zw, first_ref, second_ref, first_z, second_z):
    row = rows()
    widen(
        lambda x, s: margin(ya, yb, x, s, row), cur, xa, xb, ma, mb, 4, zw, cur.shape[0],
        first_ref, second_ref, first_z, second_z,
    )


def filtered(s2, r2, s2z, r2z, cur, margins, xa, xb, ma, mb, zw, out, s4, r4, s4z, r4z):
    size_x, _, size_z = cur.shape
    count = size_z // LANES
    widen(lambda x, s: margins[x, :, s], cur, xa, xb, ma, mb, 0, zw, 0, s4, r4, s4z, r4z)
    first = lax.axis_index("gz") == 0
    lane = lanes()

    def each(lag, carry):
        def image(x):
            a, b = x - lag + HALF + WIDE, x + lag - HALF + WIDE
            return [
                s2[a, :, chunk(j)] * r2[b, :, chunk(j)] + s4[a, :, chunk(j)] * r4[b, :, chunk(j)]
                for j in range(count)
            ]

        previous, here = image(-1), image(0)
        for x in range(size_x):
            following = image(x + 1)
            a, b = x - lag + HALF + WIDE, x + lag - HALF + WIDE
            beyond = s2z[a] * r2z[b] + s4z[a] * r4z[b]
            before, after = kept(jnp.logical_not(first), beyond), kept(first, beyond)
            up = [pltpu.roll(v, LANES - 1, axis=1) for v in (*here, after)]
            down = [pltpu.roll(v, 1, axis=1) for v in (before, *here)]
            for j in range(count):
                along = jnp.where(lane < LANES - 1, up[j], up[j + 1]) + jnp.where(lane >= 1, down[j + 1], down[j])
                across = pltpu.roll(here[j], 7, axis=0) + pltpu.roll(here[j], 1, axis=0)
                value = 6.0 * here[j] - (previous[j] + following[j] + across + along)
                out[lag, x, :, chunk(j)] = value[0:4].astype(jnp.bfloat16)
            previous, here = here, following
        return carry

    lax.fori_loop(0, LAGS, each, 0)


def local(
    source_prev,
    source_now,
    receiver_prev,
    receiver_now,
    courant,
    absorbing,
    source_cell,
    wavelet,
    receiver_cells,
    traces,
):
    f32 = jnp.float32
    size_x, size_y, size_z = courant.shape
    tile = ((size_x, 8, size_z), f32)
    wide_x = size_x + 2 * WIDE
    packed = (WIDE + 1) // 2

    def side(n):
        return ((n, 8, size_z), f32)

    def edge(n):
        return ((n, 8, LANES), f32)

    now, a, b, z = call(pack, [tile, side(4), side(4), edge(size_x)], source_now, receiver_now, far=(0, 1))
    halo0 = (*swap(a, b, "gx"), *swap(now, now, "gy"), cross(z))
    blocks = receiver_cells.shape[0] // LANES
    coef, prev, inject = call(
        prepare,
        [((3, *tile[0]), f32), tile, ((STEPS, *tile[0]), f32)],
        source_cell, wavelet, receiver_cells.T, traces, courant, absorbing, source_prev, receiver_prev,
        scratch=[pltpu.VMEM((blocks, 8, LANES), jnp.int32), pltpu.VMEM((STEPS, blocks, 8, LANES), f32)],
        smem=(0, 1),
        far=range(8),
    )
    one, a, b, z = call(first_step, [tile, side(4), side(4), edge(size_x)], now, prev, coef, inject, *halo0)
    halo1 = (*swap(a, b, "gx"), *swap(one, one, "gy"), cross(z))
    two, a, b, z = call(second_step, [tile, side(WIDE), side(WIDE), edge(size_x)], one, now, coef, inject, *halo1)
    halo2 = (*swap(a, b, "gx"), *swap(two, two, "gy"), cross(z))
    three, a, b, z = call(
        third_step,
        [tile, side(4 + packed), side(4 + packed), edge(size_x + wide_x)],
        two, one, coef, inject, *halo2,
    )
    halo3 = (*swap(a, b, "gx"), *swap(three, three, "gy"), cross(z))
    field = ((size_x, size_y, size_z), f32)
    four, source, receiver, a, b, c, d = call(
        fourth_step,
        [tile, field, field, side(WIDE), side(WIDE), side(size_x // 4), side(size_x // 4)],
        three, two, coef, inject, *halo3,
        far_outs=(1, 2),
    )
    halo4 = (*swap(a, b, "gx"), *swap(c, d, "gy"))
    s2, r2, s2z, r2z = call(
        early,
        [side(wide_x), side(wide_x), edge(wide_x), edge(wide_x)],
        two, *halo2[:4], halo3[0], halo3[1], halo3[4],
    )
    margins, a, b, z = call(
        gather_edges, [tile, side(packed), side(packed), edge(wide_x)], four, *halo4
    )
    halo5 = (*swap(a, b, "gx"), cross(z))
    (image,) = call(
        filtered,
        [((LAGS, size_x, size_y, size_z), jnp.bfloat16)],
        s2, r2, s2z, r2z, four, margins, halo4[0], halo4[1], *halo5,
        scratch=[pltpu.VMEM(s, f32) for s, _ in (side(wide_x), side(wide_x), edge(wide_x), edge(wide_x))],
        far_outs=(0,),
    )
    return source, receiver, image


def solution(mesh):
    placed = (
        P(("shot", "gx"), "gy", "gz"),
        P(("shot", "gx"), "gy", "gz"),
        P(("shot", "gx"), "gy", "gz"),
        P(("shot", "gx"), "gy", "gz"),
        P("gx", "gy", "gz"),
        P("gx", "gy", "gz"),
        P("shot"),
        P("shot"),
        P("shot", None),
        P(None, "shot"),
    )
    return jax.shard_map(
        local,
        mesh=mesh,
        in_specs=placed,
        out_specs=(
            P(("shot", "gx"), "gy", "gz"),
            P(("shot", "gx"), "gy", "gz"),
            P(None, ("shot", "gx"), "gy", "gz"),
        ),
        check_vma=False,
    )
```

time: 220 us -> 155 us (0.70)
  other arithmetic: 27.5 us -> 0 us
  local copies, waits for them, and re-layouts: 27 us -> 5.09 us
  starting transfers between devices: 134 us -> 121 us
  Pallas kernels: 0 us -> 9.82 us
  matrix products: 7.41 us -> 0 us
  waiting for transfers between devices: 19.8 us -> 16.9 us
    ppermute x29 -> x27, starting transfers between devices: 134 us -> 121 us  [the longest x22 111 us: swap(): return (lax.ppermute(a, axis, near), lax.ppermute(b, axis, far))]
    mul x32 -> x0, local copies, waits for them, and re-layouts: 10.9 us -> none  [correlate(): widened[0, LAGS - offset:LAGS - offset + length]]
    pallas_call x0 -> x9, Pallas kernels: none -> 9.82 us  [call(): pl.pallas_call(body, out_shape=[jax.ShapeDtypeStruct(s, d) if i in far_ou...]
    another operation x6 -> x0, local copies, waits for them, and re-layouts: 7.78 us -> none  [the longest x2 7.33 us: correlate(): jnp.stack([widened[0, LAGS - offset:LAGS - offset + length] * widened[1,...]
    dot_general x4 -> x0, matrix products: 7.41 us -> none  [local(): jnp.einsum('rx,ry->xy', match_x, match_y, precision=lax.Precision.HIGHEST)]
    concatenate x5 -> x0, other arithmetic: 6.2 us -> none  [extended(): jnp.concatenate([jnp.pad(low, around), array, jnp.pad(high, around)], axi...]
    div x4 -> x0, other arithmetic: 5.81 us -> none  [advance(): (2.0 * current - (1.0 - damping) * earlier + courant * stencil(padded)) /...]
    slice x15 -> x0, local copies, waits for them, and re-layouts: 5.53 us -> none  [the longest x1 1.4 us: local(): inject_upcoming = inject_upcoming.at[0].add(point * wavelet[step_index])]
  transfers between devices with their start and end apart: 29 -> 27, of which waited for: 10 -> 8; matrix products, arithmetic and copies ran while one was open for 11% -> 0% of each run, Pallas kernels for 0% -> 1%
where the time goes in v2:
time: 155 us; the launch traced here: 154 us
  starting transfers between devices  121 us (78%)
  waiting for transfers between devices  16.9 us (11%)
  Pallas kernels  9.82 us (6%)
  local copies, waits for them, and re-layouts  5.09 us (3%)
    ppermute x22, starting transfers between devices, swap(): return (lax.ppermute(a, axis, near), lax.ppermute(b, axis, far))  111 us
    ppermute x22, waiting for transfers between devices, swap(): return (lax.ppermute(a, axis, near), lax.ppermute(b, axis, far))  14.5 us
    pallas_call x9, Pallas kernels, call(): pl.pallas_call(body, out_shape=[jax.ShapeDtypeStruct(s, d) if i in far_ou...  9.82 us
    ppermute x5, starting transfers between devices, cross(): return lax.ppermute(a, 'gz', [(0, 1), (1, 0)])  9.76 us
    unnamed x20, local copies, waits for them, and re-layouts  5.09 us
  transfers between devices with their start and end apart: 27, of which 8 were waited for; matrix products, arithmetic and copies ran while one was open for 0% of the time, Pallas kernels for 1%

profile of v2, /device:TPU:80, one launch (start us, length us, event | category | flops | bytes accessed | tf_op | source)
XLA Modules:
  0.0 153.6 jit_solution(11618070952342620821)
XLA Ops:
  0.7 0.9 copy-done.4
  1.6 0.9 copy-done.5
  2.5 5.8 %collective-permute-start.3 = (f32[12,8,512]{2,1,0:T(8,128)S(1)}, f32[12,8,512]{2,1,0:T(8,128)S(1)}, u32[]{:S(2)}, u32[]{:S(2)}) collective-permute-start(f32[12,8,512]{2,1,0:T(8,128)S(1)} %get-tuple-element.37.cur.prev), channel_id=1, source_target_pairs={{0,14},{2,4},{4,2},{6,8},{8,6},{10,12},{12,10},{14,0},{1,15},{3,5}... | collective-permute-start | bytes 589832 | tf_op jit(solution)/shard_map/ppermute | solution.py:29
  8.3 2.0 %collective-permute-start.2 = (f32[12,8,512]{2,1,0:T(8,128)S(1)}, f32[12,8,512]{2,1,0:T(8,128)S(1)}, u32[]{:S(2)}, u32[]{:S(2)}) collective-permute-start(f32[12,8,512]{2,1,0:T(8,128)S(1)} %get-tuple-element.37.cur.prev), channel_id=1, source_target_pairs={{0,2},{2,0},{4,6},{6,4},{8,10},{10,8},{12,14},{14,12},{1,3},{3,1},... | collective-permute-start | bytes 589832 | tf_op jit(solution)/shard_map/ppermute | solution.py:29
  10.2 6.0 %collective-permute-start = (f32[4,8,512]{2,1,0:T(8,128)S(1)}, f32[4,8,512]{2,1,0:T(8,128)S(1)}, u32[]{:S(2)}, u32[]{:S(2)}) collective-permute-start(f32[4,8,512]{2,1,0:T(8,128)S(1)} %get-tuple-element.41), channel_id=1, source_target_pairs={{0,16},{16,0},{32,48},{48,32},{64,80},{80,64},{96,112},{112,96},{1... | collective-permute-start | bytes 196616 | tf_op jit(solution)/shard_map/ppermute | solution.py:29
  16.3 39.9 %collective-permute-start.1 = (f32[4,8,512]{2,1,0:T(8,128)S(1)}, f32[4,8,512]{2,1,0:T(8,128)S(1)}, u32[]{:S(2)}, u32[]{:S(2)}) collective-permute-start(f32[4,8,512]{2,1,0:T(8,128)S(1)} %get-tuple-element.42), channel_id=1, source_target_pairs={{0,240},{16,32},{32,16},{48,64},{64,48},{80,96},{96,80},{112,128},... | collective-permute-start | bytes 196616 | tf_op jit(solution)/shard_map/ppermute | solution.py:29
  56.2 0.0 copy-start.8
  56.2 0.0 copy-start.9
  56.3 2.0 %collective-permute-start.4 = (f32[12,8,128]{2,1,0:T(8,128)S(1)}, f32[12,8,128]{2,1,0:T(8,128)S(1)}, u32[]{:S(2)}, u32[]{:S(2)}) collective-permute-start(f32[12,8,128]{2,1,0:T(8,128)S(1)} %get-tuple-element.43), channel_id=1, source_target_pairs={{0,1},{1,0},{2,3},{3,2},{4,5},{5,4},{6,7},{7,6},{8,9},{9,8},{10,11... | collective-permute-start | bytes 147464 | tf_op jit(solution)/shard_map/ppermute | solution.py:33
  58.3 0.0 copy-start.2
  58.3 0.9 copy-done.2
  59.2 0.9 copy-done.3
  60.1 0.8 copy-done.6
  60.8 0.7 copy-done.7
  61.5 1.9 %prepare.1 = (f32[3,12,8,512]{3,2,1,0:T(8,128)S(1)}, f32[12,8,512]{2,1,0:T(8,128)S(1)}, f32[4,12,8,512]{3,2,1,0:T(8,128)S(1)}) custom-call(s32[3]{0:T(128)S(1)} %copy-done.8, f32[4]{0:T(128)S(1)} %copy-done.9, s32[2,2048]{1,0:T(2,128)S(1)} %bitcast.1, f32[4,2048]{1,0:T(4,128)S(1)} %copy-done.6, f32[12,4,512]{2,1,0:T(4,128)S(1)} %copy-done, ...), custom_call_target="tpu_custom_call" | custom-call | tf_op jit(solution)/shard_map/prepare/pallas_call | solution.py:62
  63.5 0.0 collective-permute-done.4.z
  63.5 0.0 collective-permute-done.xa
  63.5 0.0 collective-permute-done.1.xb
  63.5 0.0 collective-permute-done.3.yb
  63.5 0.0 collective-permute-done.2.ya
  63.5 0.6 first_step.1
  64.1 4.5 %collective-permute-start.8 = (f32[12,8,512]{2,1,0:T(8,128)S(1)}, f32[12,8,512]{2,1,0:T(8,128)S(1)}, u32[]{:S(2)}, u32[]{:S(2)}) collective-permute-start(f32[12,8,512]{2,1,0:T(8,128)S(1)} %get-tuple-element.44.cur.prev), channel_id=1, source_target_pairs={{0,14},{2,4},{4,2},{6,8},{8,6},{10,12},{12,10},{14,0},{1,15},{3,5}... | collective-permute-start | bytes 589832 | tf_op jit(solution)/shard_map/ppermute | solution.py:29
  68.7 3.2 %collective-permute-start.7 = (f32[12,8,512]{2,1,0:T(8,128)S(1)}, f32[12,8,512]{2,1,0:T(8,128)S(1)}, u32[]{:S(2)}, u32[]{:S(2)}) collective-permute-start(f32[12,8,512]{2,1,0:T(8,128)S(1)} %get-tuple-element.44.cur.prev), channel_id=1, source_target_pairs={{0,2},{2,0},{4,6},{6,4},{8,10},{10,8},{12,14},{14,12},{1,3},{3,1},... | collective-permute-start | bytes 589832 | tf_op jit(solution)/shard_map/ppermute | solution.py:29
  71.9 2.0 %collective-permute-start.5 = (f32[4,8,512]{2,1,0:T(8,128)S(1)}, f32[4,8,512]{2,1,0:T(8,128)S(1)}, u32[]{:S(2)}, u32[]{:S(2)}) collective-permute-start(f32[4,8,512]{2,1,0:T(8,128)S(1)} %get-tuple-element.45), channel_id=1, source_target_pairs={{0,16},{16,0},{32,48},{48,32},{64,80},{80,64},{96,112},{112,96},{1... | collective-permute-start | bytes 196616 | tf_op jit(solution)/shard_map/ppermute | solution.py:29
  73.9 4.0 %collective-permute-start.6 = (f32[4,8,512]{2,1,0:T(8,128)S(1)}, f32[4,8,512]{2,1,0:T(8,128)S(1)}, u32[]{:S(2)}, u32[]{:S(2)}) collective-permute-start(f32[4,8,512]{2,1,0:T(8,128)S(1)} %get-tuple-element.46), channel_id=1, source_target_pairs={{0,240},{16,32},{32,16},{48,64},{64,48},{80,96},{96,80},{112,128},... | collective-permute-start | bytes 196616 | tf_op jit(solution)/shard_map/ppermute | solution.py:29
  77.8 2.0 %collective-permute-start.9 = (f32[12,8,128]{2,1,0:T(8,128)S(1)}, f32[12,8,128]{2,1,0:T(8,128)S(1)}, u32[]{:S(2)}, u32[]{:S(2)}) collective-permute-start(f32[12,8,128]{2,1,0:T(8,128)S(1)} %get-tuple-element.47), channel_id=1, source_target_pairs={{0,1},{1,0},{2,3},{3,2},{4,5},{5,4},{6,7},{7,6},{8,9},{9,8},{10,11... | collective-permute-start | bytes 147464 | tf_op jit(solution)/shard_map/ppermute | solution.py:33
  79.8 1.2 collective-permute-done.9.z
  81.0 0.0 collective-permute-done.5.xa
  81.0 0.3 collective-permute-done.6.xb
  81.3 0.0 collective-permute-done.8.yb
  81.3 0.0 collective-permute-done.7.ya
  81.3 0.6 second_step.1
  81.9 2.3 %collective-permute-start.13 = (f32[12,8,512]{2,1,0:T(8,128)S(1)}, f32[12,8,512]{2,1,0:T(8,128)S(1)}, u32[]{:S(2)}, u32[]{:S(2)}) collective-permute-start(f32[12,8,512]{2,1,0:T(8,128)S(1)} %get-tuple-element.48.cur.prev), channel_id=1, source_target_pairs={{0,14},{2,4},{4,2},{6,8},{8,6},{10,12},{12,10},{14,0},{1,15},{3,5}... | collective-permute-start | bytes 589832 | tf_op jit(solution)/shard_map/ppermute | solution.py:29
  84.3 3.0 %collective-permute-start.12 = (f32[12,8,512]{2,1,0:T(8,128)S(1)}, f32[12,8,512]{2,1,0:T(8,128)S(1)}, u32[]{:S(2)}, u32[]{:S(2)}) collective-permute-start(f32[12,8,512]{2,1,0:T(8,128)S(1)} %get-tuple-element.48.cur.prev), channel_id=1, source_target_pairs={{0,2},{2,0},{4,6},{6,4},{8,10},{10,8},{12,14},{14,12},{1,3},{3,1},... | collective-permute-start | bytes 589832 | tf_op jit(solution)/shard_map/ppermute | solution.py:29
  87.3 2.7 %collective-permute-start.10 = (f32[9,8,512]{2,1,0:T(8,128)S(1)}, f32[9,8,512]{2,1,0:T(8,128)S(1)}, u32[]{:S(2)}, u32[]{:S(2)}) collective-permute-start(f32[9,8,512]{2,1,0:T(8,128)S(1)} %get-tuple-element.49), channel_id=1, source_target_pairs={{0,16},{16,0},{32,48},{48,32},{64,80},{80,64},{96,112},{112,96},{1... | collective-permute-start | bytes 442376 | tf_op jit(solution)/shard_map/ppermute | solution.py:29
  90.0 3.2 %collective-permute-start.11 = (f32[9,8,512]{2,1,0:T(8,128)S(1)}, f32[9,8,512]{2,1,0:T(8,128)S(1)}, u32[]{:S(2)}, u32[]{:S(2)}) collective-permute-start(f32[9,8,512]{2,1,0:T(8,128)S(1)} %get-tuple-element.50), channel_id=1, source_target_pairs={{0,240},{16,32},{32,16},{48,64},{64,48},{80,96},{96,80},{112,128},... | collective-permute-start | bytes 442376 | tf_op jit(solution)/shard_map/ppermute | solution.py:29
  93.2 2.0 %collective-permute-start.14 = (f32[12,8,128]{2,1,0:T(8,128)S(1)}, f32[12,8,128]{2,1,0:T(8,128)S(1)}, u32[]{:S(2)}, u32[]{:S(2)}) collective-permute-start(f32[12,8,128]{2,1,0:T(8,128)S(1)} %get-tuple-element.51), channel_id=1, source_target_pairs={{0,1},{1,0},{2,3},{3,2},{4,5},{5,4},{6,7},{7,6},{8,9},{9,8},{10,11... | collective-permute-start | bytes 147464 | tf_op jit(solution)/shard_map/ppermute | solution.py:33
  95.2 1.2 collective-permute-done.14.z
  96.3 0.0 collective-permute-done.10.xa
  96.4 1.9 %collective-permute-done.11.xb = f32[9,8,512]{2,1,0:T(8,128)S(1)} collective-permute-done((f32[9,8,512]{2,1,0:T(8,128)S(1)}, f32[9,8,512]{2,1,0:T(8,128)S(1)}, u32[]{:S(2)}, u32[]{:S(2)}) %collective-permute-start.11) | collective-permute-done | bytes 147488 | tf_op jit(solution)/shard_map/ppermute | solution.py:29
  98.3 0.0 collective-permute-done.13.yb
  98.3 0.7 third_step.1
  99.0 3.7 %collective-permute-start.18 = (f32[12,8,512]{2,1,0:T(8,128)S(1)}, f32[12,8,512]{2,1,0:T(8,128)S(1)}, u32[]{:S(2)}, u32[]{:S(2)}) collective-permute-start(f32[12,8,512]{2,1,0:T(8,128)S(1)} %get-tuple-element.52.cur), channel_id=1, source_target_pairs={{0,14},{2,4},{4,2},{6,8},{8,6},{10,12},{12,10},{14,0},{1,15},{3,5}... | collective-permute-start | bytes 589832 | tf_op jit(solution)/shard_map/ppermute | solution.py:29
  102.7 2.0 %collective-permute-start.17 = (f32[12,8,512]{2,1,0:T(8,128)S(1)}, f32[12,8,512]{2,1,0:T(8,128)S(1)}, u32[]{:S(2)}, u32[]{:S(2)}) collective-permute-start(f32[12,8,512]{2,1,0:T(8,128)S(1)} %get-tuple-element.52.cur), channel_id=1, source_target_pairs={{0,2},{2,0},{4,6},{6,4},{8,10},{10,8},{12,14},{14,12},{1,3},{3,1},... | collective-permute-start | bytes 589832 | tf_op jit(solution)/shard_map/ppermute | solution.py:29
  104.7 2.0 %collective-permute-start.19 = (f32[42,8,128]{2,1,0:T(8,128)S(1)}, f32[42,8,128]{2,1,0:T(8,128)S(1)}, u32[]{:S(2)}, u32[]{:S(2)}) collective-permute-start(f32[42,8,128]{2,1,0:T(8,128)S(1)} %get-tuple-element.55), channel_id=1, source_target_pairs={{0,1},{1,0},{2,3},{3,2},{4,5},{5,4},{6,7},{7,6},{8,9},{9,8},{10,11... | collective-permute-start | bytes 516104 | tf_op jit(solution)/shard_map/ppermute | solution.py:33
  106.6 2.0 %collective-permute-start.15 = (f32[9,8,512]{2,1,0:T(8,128)S(1)}, f32[9,8,512]{2,1,0:T(8,128)S(1)}, u32[]{:S(2)}, u32[]{:S(2)}) collective-permute-start(f32[9,8,512]{2,1,0:T(8,128)S(1)} %get-tuple-element.53), channel_id=1, source_target_pairs={{0,16},{16,0},{32,48},{48,32},{64,80},{80,64},{96,112},{112,96},{1... | collective-permute-start | bytes 442376 | tf_op jit(solution)/shard_map/ppermute | solution.py:29
  108.6 4.0 %collective-permute-start.16 = (f32[9,8,512]{2,1,0:T(8,128)S(1)}, f32[9,8,512]{2,1,0:T(8,128)S(1)}, u32[]{:S(2)}, u32[]{:S(2)}) collective-permute-start(f32[9,8,512]{2,1,0:T(8,128)S(1)} %get-tuple-element.54), channel_id=1, source_target_pairs={{0,240},{16,32},{32,16},{48,64},{64,48},{80,96},{96,80},{112,128},... | collective-permute-start | bytes 442376 | tf_op jit(solution)/shard_map/ppermute | solution.py:29
  112.6 2.2 %collective-permute-done.15.xa.ma = f32[9,8,512]{2,1,0:T(8,128)S(1)} collective-permute-done((f32[9,8,512]{2,1,0:T(8,128)S(1)}, f32[9,8,512]{2,1,0:T(8,128)S(1)}, u32[]{:S(2)}, u32[]{:S(2)}) %collective-permute-start.15) | collective-permute-done | bytes 147488 | tf_op jit(solution)/shard_map/ppermute | solution.py:29
  114.8 3.2 %collective-permute-done.16.xb.mb = f32[9,8,512]{2,1,0:T(8,128)S(1)} collective-permute-done((f32[9,8,512]{2,1,0:T(8,128)S(1)}, f32[9,8,512]{2,1,0:T(8,128)S(1)}, u32[]{:S(2)}, u32[]{:S(2)}) %collective-permute-start.16) | collective-permute-done | bytes 147488 | tf_op jit(solution)/shard_map/ppermute | solution.py:29
  118.0 1.4 fourth_step.1
  119.4 2.5 %collective-permute-start.20 = (f32[9,8,512]{2,1,0:T(8,128)S(1)}, f32[9,8,512]{2,1,0:T(8,128)S(1)}, u32[]{:S(2)}, u32[]{:S(2)}) collective-permute-start(f32[9,8,512]{2,1,0:T(8,128)S(1)} %get-tuple-element.63), channel_id=1, source_target_pairs={{0,16},{16,0},{32,48},{48,32},{64,80},{80,64},{96,112},{112,96},{1... | collective-permute-start | bytes 442376 | tf_op jit(solution)/shard_map/ppermute | solution.py:29
  121.8 3.4 %collective-permute-start.21 = (f32[9,8,512]{2,1,0:T(8,128)S(1)}, f32[9,8,512]{2,1,0:T(8,128)S(1)}, u32[]{:S(2)}, u32[]{:S(2)}) collective-permute-start(f32[9,8,512]{2,1,0:T(8,128)S(1)} %get-tuple-element.64), channel_id=1, source_target_pairs={{0,240},{16,32},{32,16},{48,64},{64,48},{80,96},{96,80},{112,128},... | collective-permute-start | bytes 442376 | tf_op jit(solution)/shard_map/ppermute | solution.py:29
  125.3 4.0 %collective-permute-start.22 = (f32[3,8,512]{2,1,0:T(8,128)S(1)}, f32[3,8,512]{2,1,0:T(8,128)S(1)}, u32[]{:S(2)}, u32[]{:S(2)}) collective-permute-start(f32[3,8,512]{2,1,0:T(8,128)S(1)} %get-tuple-element.65), channel_id=1, source_target_pairs={{0,2},{2,0},{4,6},{6,4},{8,10},{10,8},{12,14},{14,12},{1,3},{3,1},... | collective-permute-start | bytes 147464 | tf_op jit(solution)/shard_map/ppermute | solution.py:29
  129.2 3.4 %collective-permute-start.23 = (f32[3,8,512]{2,1,0:T(8,128)S(1)}, f32[3,8,512]{2,1,0:T(8,128)S(1)}, u32[]{:S(2)}, u32[]{:S(2)}) collective-permute-start(f32[3,8,512]{2,1,0:T(8,128)S(1)} %get-tuple-element.66), channel_id=1, source_target_pairs={{0,14},{2,4},{4,2},{6,8},{8,6},{10,12},{12,10},{14,0},{1,15},{3,5}... | collective-permute-start | bytes 147464 | tf_op jit(solution)/shard_map/ppermute | solution.py:29
  132.6 0.0 collective-permute-done.22.ya
  132.6 3.8 %collective-permute-done.23.yb = f32[3,8,512]{2,1,0:T(8,128)S(1)} collective-permute-done((f32[3,8,512]{2,1,0:T(8,128)S(1)}, f32[3,8,512]{2,1,0:T(8,128)S(1)}, u32[]{:S(2)}, u32[]{:S(2)}) %collective-permute-start.23) | collective-permute-done | bytes 49184 | tf_op jit(solution)/shard_map/ppermute | solution.py:29
  136.5 0.1 gather_edges.1
  136.5 2.0 %collective-permute-start.26 = (f32[30,8,128]{2,1,0:T(8,128)S(1)}, f32[30,8,128]{2,1,0:T(8,128)S(1)}, u32[]{:S(2)}, u32[]{:S(2)}) collective-permute-start(f32[30,8,128]{2,1,0:T(8,128)S(1)} %get-tuple-element.70), channel_id=1, source_target_pairs={{0,1},{1,0},{2,3},{3,2},{4,5},{5,4},{6,7},{7,6},{8,9},{9,8},{10,11... | collective-permute-start | bytes 368648 | tf_op jit(solution)/shard_map/ppermute | solution.py:33
  138.5 3.1 %collective-permute-start.24 = (f32[5,8,512]{2,1,0:T(8,128)S(1)}, f32[5,8,512]{2,1,0:T(8,128)S(1)}, u32[]{:S(2)}, u32[]{:S(2)}) collective-permute-start(f32[5,8,512]{2,1,0:T(8,128)S(1)} %get-tuple-element.68), channel_id=1, source_target_pairs={{0,16},{16,0},{32,48},{48,32},{64,80},{80,64},{96,112},{112,96},{1... | collective-permute-start | bytes 245768 | tf_op jit(solution)/shard_map/ppermute | solution.py:29
  141.6 4.5 %collective-permute-start.25 = (f32[5,8,512]{2,1,0:T(8,128)S(1)}, f32[5,8,512]{2,1,0:T(8,128)S(1)}, u32[]{:S(2)}, u32[]{:S(2)}) collective-permute-start(f32[5,8,512]{2,1,0:T(8,128)S(1)} %get-tuple-element.69), channel_id=1, source_target_pairs={{0,240},{16,32},{32,16},{48,64},{64,48},{80,96},{96,80},{112,128},... | collective-permute-start | bytes 245768 | tf_op jit(solution)/shard_map/ppermute | solution.py:29
  146.1 0.2 early.1
  146.3 3.0 %collective-permute-done.25.mb = f32[5,8,512]{2,1,0:T(8,128)S(1)} collective-permute-done((f32[5,8,512]{2,1,0:T(8,128)S(1)}, f32[5,8,512]{2,1,0:T(8,128)S(1)}, u32[]{:S(2)}, u32[]{:S(2)}) %collective-permute-start.25) | collective-permute-done | bytes 81952 | tf_op jit(solution)/shard_map/ppermute | solution.py:29
  149.3 0.0 collective-permute-done.26.zw
  149.3 4.3 %filtered.1 = bf16[16,12,4,512]{3,2,1,0:T(4,128)(2,1)} custom-call(f32[30,8,512]{2,1,0:T(8,128)S(1)} %get-tuple-element.58.s2, f32[30,8,512]{2,1,0:T(8,128)S(1)} %get-tuple-element.59.r2, f32[30,8,128]{2,1,0:T(8,128)S(1)} %get-tuple-element.60.s2z, f32[30,8,128]{2,1,0:T(8,128)S(1)} %get-tuple-element.61.r2z, f32[12,8,512]{2,1,0:T(8,128)S(1)} %get-tuple-element.62.cur, ...), custom_call_target="tpu_custom_call" | custom-call | tf_op jit(solution)/shard_map/filtered/pallas_call | solution.py:62
  (19 shorter events, 0.1 us)
Async XLA Ops:
  0.6 57.6 %copy-start.1 = (s32[12,4,512]{2,1,0:T(4,128)S(1)}, s32[12,4,512]{2,1,0:T(4,128)}, u32[]{:S(2)}) copy-start(s32[12,4,512]{2,1,0:T(4,128)} %absorbing.1) | copy-start | bytes 294916
  0.6 57.6 %copy-start = (f32[12,4,512]{2,1,0:T(4,128)S(1)}, f32[12,4,512]{2,1,0:T(4,128)}, u32[]{:S(2)}) copy-start(f32[12,4,512]{2,1,0:T(4,128)} %courant.1) | copy-start | bytes 294916
  0.7 0.9 copy-start.4
  1.6 0.9 copy-start.5
  2.5 61.0 %collective-permute-start.3 = (f32[12,8,512]{2,1,0:T(8,128)S(1)}, f32[12,8,512]{2,1,0:T(8,128)S(1)}, u32[]{:S(2)}, u32[]{:S(2)}) collective-permute-start(f32[12,8,512]{2,1,0:T(8,128)S(1)} %get-tuple-element.37.cur.prev), channel_id=1, source_target_pairs={{0,14},{2,4},{4,2},{6,8},{8,6},{10,12},{12,10},{14,0},{1,15},{3,5}... | collective-permute-start | bytes 589832 | tf_op jit(solution)/shard_map/ppermute | solution.py:29
  8.3 55.2 %collective-permute-start.2 = (f32[12,8,512]{2,1,0:T(8,128)S(1)}, f32[12,8,512]{2,1,0:T(8,128)S(1)}, u32[]{:S(2)}, u32[]{:S(2)}) collective-permute-start(f32[12,8,512]{2,1,0:T(8,128)S(1)} %get-tuple-element.37.cur.prev), channel_id=1, source_target_pairs={{0,2},{2,0},{4,6},{6,4},{8,10},{10,8},{12,14},{14,12},{1,3},{3,1},... | collective-permute-start | bytes 589832 | tf_op jit(solution)/shard_map/ppermute | solution.py:29
  10.2 53.2 %collective-permute-start = (f32[4,8,512]{2,1,0:T(8,128)S(1)}, f32[4,8,512]{2,1,0:T(8,128)S(1)}, u32[]{:S(2)}, u32[]{:S(2)}) collective-permute-start(f32[4,8,512]{2,1,0:T(8,128)S(1)} %get-tuple-element.41), channel_id=1, source_target_pairs={{0,16},{16,0},{32,48},{48,32},{64,80},{80,64},{96,112},{112,96},{1... | collective-permute-start | bytes 196616 | tf_op jit(solution)/shard_map/ppermute | solution.py:29
  16.3 47.2 %collective-permute-start.1 = (f32[4,8,512]{2,1,0:T(8,128)S(1)}, f32[4,8,512]{2,1,0:T(8,128)S(1)}, u32[]{:S(2)}, u32[]{:S(2)}) collective-permute-start(f32[4,8,512]{2,1,0:T(8,128)S(1)} %get-tuple-element.42), channel_id=1, source_target_pairs={{0,240},{16,32},{32,16},{48,64},{64,48},{80,96},{96,80},{112,128},... | collective-permute-start | bytes 196616 | tf_op jit(solution)/shard_map/ppermute | solution.py:29
  56.2 2.0 %copy-start.8 = (s32[3]{0:T(128)S(1)}, s32[3]{0:T(128)}, u32[]{:S(2)}) copy-start(s32[3]{0:T(128)} %cell.1) | copy-start | bytes 40
  56.2 2.0 %copy-start.9 = (f32[4]{0:T(128)S(1)}, f32[4]{0:T(128)}, u32[]{:S(2)}) copy-start(f32[4]{0:T(128)} %wavelet.1) | copy-start | bytes 52
  56.3 7.2 %collective-permute-start.4 = (f32[12,8,128]{2,1,0:T(8,128)S(1)}, f32[12,8,128]{2,1,0:T(8,128)S(1)}, u32[]{:S(2)}, u32[]{:S(2)}) collective-permute-start(f32[12,8,128]{2,1,0:T(8,128)S(1)} %get-tuple-element.43), channel_id=1, source_target_pairs={{0,1},{1,0},{2,3},{3,2},{4,5},{5,4},{6,7},{7,6},{8,9},{9,8},{10,11... | collective-permute-start | bytes 147464 | tf_op jit(solution)/shard_map/ppermute | solution.py:33
  58.3 0.9 copy-start.2
  59.2 0.9 copy-start.3
  60.1 0.8 copy-start.6
  60.8 0.7 copy-start.7
  64.1 17.1 %collective-permute-start.8 = (f32[12,8,512]{2,1,0:T(8,128)S(1)}, f32[12,8,512]{2,1,0:T(8,128)S(1)}, u32[]{:S(2)}, u32[]{:S(2)}) collective-permute-start(f32[12,8,512]{2,1,0:T(8,128)S(1)} %get-tuple-element.44.cur.prev), channel_id=1, source_target_pairs={{0,14},{2,4},{4,2},{6,8},{8,6},{10,12},{12,10},{14,0},{1,15},{3,5}... | collective-permute-start | bytes 589832 | tf_op jit(solution)/shard_map/ppermute | solution.py:29
  68.7 12.6 %collective-permute-start.7 = (f32[12,8,512]{2,1,0:T(8,128)S(1)}, f32[12,8,512]{2,1,0:T(8,128)S(1)}, u32[]{:S(2)}, u32[]{:S(2)}) collective-permute-start(f32[12,8,512]{2,1,0:T(8,128)S(1)} %get-tuple-element.44.cur.prev), channel_id=1, source_target_pairs={{0,2},{2,0},{4,6},{6,4},{8,10},{10,8},{12,14},{14,12},{1,3},{3,1},... | collective-permute-start | bytes 589832 | tf_op jit(solution)/shard_map/ppermute | solution.py:29
  71.9 9.1 %collective-permute-start.5 = (f32[4,8,512]{2,1,0:T(8,128)S(1)}, f32[4,8,512]{2,1,0:T(8,128)S(1)}, u32[]{:S(2)}, u32[]{:S(2)}) collective-permute-start(f32[4,8,512]{2,1,0:T(8,128)S(1)} %get-tuple-element.45), channel_id=1, source_target_pairs={{0,16},{16,0},{32,48},{48,32},{64,80},{80,64},{96,112},{112,96},{1... | collective-permute-start | bytes 196616 | tf_op jit(solution)/shard_map/ppermute | solution.py:29
  73.9 7.4 %collective-permute-start.6 = (f32[4,8,512]{2,1,0:T(8,128)S(1)}, f32[4,8,512]{2,1,0:T(8,128)S(1)}, u32[]{:S(2)}, u32[]{:S(2)}) collective-permute-start(f32[4,8,512]{2,1,0:T(8,128)S(1)} %get-tuple-element.46), channel_id=1, source_target_pairs={{0,240},{16,32},{32,16},{48,64},{64,48},{80,96},{96,80},{112,128},... | collective-permute-start | bytes 196616 | tf_op jit(solution)/shard_map/ppermute | solution.py:29
  77.8 3.2 %collective-permute-start.9 = (f32[12,8,128]{2,1,0:T(8,128)S(1)}, f32[12,8,128]{2,1,0:T(8,128)S(1)}, u32[]{:S(2)}, u32[]{:S(2)}) collective-permute-start(f32[12,8,128]{2,1,0:T(8,128)S(1)} %get-tuple-element.47), channel_id=1, source_target_pairs={{0,1},{1,0},{2,3},{3,2},{4,5},{5,4},{6,7},{7,6},{8,9},{9,8},{10,11... | collective-permute-start | bytes 147464 | tf_op jit(solution)/shard_map/ppermute | solution.py:33
  81.9 16.4 %collective-permute-start.13 = (f32[12,8,512]{2,1,0:T(8,128)S(1)}, f32[12,8,512]{2,1,0:T(8,128)S(1)}, u32[]{:S(2)}, u32[]{:S(2)}) collective-permute-start(f32[12,8,512]{2,1,0:T(8,128)S(1)} %get-tuple-element.48.cur.prev), channel_id=1, source_target_pairs={{0,14},{2,4},{4,2},{6,8},{8,6},{10,12},{12,10},{14,0},{1,15},{3,5}... | collective-permute-start | bytes 589832 | tf_op jit(solution)/shard_map/ppermute | solution.py:29
  84.3 14.0 %collective-permute-start.12 = (f32[12,8,512]{2,1,0:T(8,128)S(1)}, f32[12,8,512]{2,1,0:T(8,128)S(1)}, u32[]{:S(2)}, u32[]{:S(2)}) collective-permute-start(f32[12,8,512]{2,1,0:T(8,128)S(1)} %get-tuple-element.48.cur.prev), channel_id=1, source_target_pairs={{0,2},{2,0},{4,6},{6,4},{8,10},{10,8},{12,14},{14,12},{1,3},{3,1},... | collective-permute-start | bytes 589832 | tf_op jit(solution)/shard_map/ppermute | solution.py:29
  87.3 9.1 %collective-permute-start.10 = (f32[9,8,512]{2,1,0:T(8,128)S(1)}, f32[9,8,512]{2,1,0:T(8,128)S(1)}, u32[]{:S(2)}, u32[]{:S(2)}) collective-permute-start(f32[9,8,512]{2,1,0:T(8,128)S(1)} %get-tuple-element.49), channel_id=1, source_target_pairs={{0,16},{16,0},{32,48},{48,32},{64,80},{80,64},{96,112},{112,96},{1... | collective-permute-start | bytes 442376 | tf_op jit(solution)/shard_map/ppermute | solution.py:29
  90.0 8.3 %collective-permute-start.11 = (f32[9,8,512]{2,1,0:T(8,128)S(1)}, f32[9,8,512]{2,1,0:T(8,128)S(1)}, u32[]{:S(2)}, u32[]{:S(2)}) collective-permute-start(f32[9,8,512]{2,1,0:T(8,128)S(1)} %get-tuple-element.50), channel_id=1, source_target_pairs={{0,240},{16,32},{32,16},{48,64},{64,48},{80,96},{96,80},{112,128},... | collective-permute-start | bytes 442376 | tf_op jit(solution)/shard_map/ppermute | solution.py:29
  93.2 3.2 %collective-permute-start.14 = (f32[12,8,128]{2,1,0:T(8,128)S(1)}, f32[12,8,128]{2,1,0:T(8,128)S(1)}, u32[]{:S(2)}, u32[]{:S(2)}) collective-permute-start(f32[12,8,128]{2,1,0:T(8,128)S(1)} %get-tuple-element.51), channel_id=1, source_target_pairs={{0,1},{1,0},{2,3},{3,2},{4,5},{5,4},{6,7},{7,6},{8,9},{9,8},{10,11... | collective-permute-start | bytes 147464 | tf_op jit(solution)/shard_map/ppermute | solution.py:33
  99.0 19.0 %collective-permute-start.18 = (f32[12,8,512]{2,1,0:T(8,128)S(1)}, f32[12,8,512]{2,1,0:T(8,128)S(1)}, u32[]{:S(2)}, u32[]{:S(2)}) collective-permute-start(f32[12,8,512]{2,1,0:T(8,128)S(1)} %get-tuple-element.52.cur), channel_id=1, source_target_pairs={{0,14},{2,4},{4,2},{6,8},{8,6},{10,12},{12,10},{14,0},{1,15},{3,5}... | collective-permute-start | bytes 589832 | tf_op jit(solution)/shard_map/ppermute | solution.py:29
  102.7 15.3 %collective-permute-start.17 = (f32[12,8,512]{2,1,0:T(8,128)S(1)}, f32[12,8,512]{2,1,0:T(8,128)S(1)}, u32[]{:S(2)}, u32[]{:S(2)}) collective-permute-start(f32[12,8,512]{2,1,0:T(8,128)S(1)} %get-tuple-element.52.cur), channel_id=1, source_target_pairs={{0,2},{2,0},{4,6},{6,4},{8,10},{10,8},{12,14},{14,12},{1,3},{3,1},... | collective-permute-start | bytes 589832 | tf_op jit(solution)/shard_map/ppermute | solution.py:29
  104.7 13.3 %collective-permute-start.19 = (f32[42,8,128]{2,1,0:T(8,128)S(1)}, f32[42,8,128]{2,1,0:T(8,128)S(1)}, u32[]{:S(2)}, u32[]{:S(2)}) collective-permute-start(f32[42,8,128]{2,1,0:T(8,128)S(1)} %get-tuple-element.55), channel_id=1, source_target_pairs={{0,1},{1,0},{2,3},{3,2},{4,5},{5,4},{6,7},{7,6},{8,9},{9,8},{10,11... | collective-permute-start | bytes 516104 | tf_op jit(solution)/shard_map/ppermute | solution.py:33
  106.6 8.2 %collective-permute-start.15 = (f32[9,8,512]{2,1,0:T(8,128)S(1)}, f32[9,8,512]{2,1,0:T(8,128)S(1)}, u32[]{:S(2)}, u32[]{:S(2)}) collective-permute-start(f32[9,8,512]{2,1,0:T(8,128)S(1)} %get-tuple-element.53), channel_id=1, source_target_pairs={{0,16},{16,0},{32,48},{48,32},{64,80},{80,64},{96,112},{112,96},{1... | collective-permute-start | bytes 442376 | tf_op jit(solution)/shard_map/ppermute | solution.py:29
  108.6 9.4 %collective-permute-start.16 = (f32[9,8,512]{2,1,0:T(8,128)S(1)}, f32[9,8,512]{2,1,0:T(8,128)S(1)}, u32[]{:S(2)}, u32[]{:S(2)}) collective-permute-start(f32[9,8,512]{2,1,0:T(8,128)S(1)} %get-tuple-element.54), channel_id=1, source_target_pairs={{0,240},{16,32},{32,16},{48,64},{64,48},{80,96},{96,80},{112,128},... | collective-permute-start | bytes 442376 | tf_op jit(solution)/shard_map/ppermute | solution.py:29
  119.4 17.1 %collective-permute-start.20 = (f32[9,8,512]{2,1,0:T(8,128)S(1)}, f32[9,8,512]{2,1,0:T(8,128)S(1)}, u32[]{:S(2)}, u32[]{:S(2)}) collective-permute-start(f32[9,8,512]{2,1,0:T(8,128)S(1)} %get-tuple-element.63), channel_id=1, source_target_pairs={{0,16},{16,0},{32,48},{48,32},{64,80},{80,64},{96,112},{112,96},{1... | collective-permute-start | bytes 442376 | tf_op jit(solution)/shard_map/ppermute | solution.py:29
  121.8 14.6 %collective-permute-start.21 = (f32[9,8,512]{2,1,0:T(8,128)S(1)}, f32[9,8,512]{2,1,0:T(8,128)S(1)}, u32[]{:S(2)}, u32[]{:S(2)}) collective-permute-start(f32[9,8,512]{2,1,0:T(8,128)S(1)} %get-tuple-element.64), channel_id=1, source_target_pairs={{0,240},{16,32},{32,16},{48,64},{64,48},{80,96},{96,80},{112,128},... | collective-permute-start | bytes 442376 | tf_op jit(solution)/shard_map/ppermute | solution.py:29
  125.3 7.4 %collective-permute-start.22 = (f32[3,8,512]{2,1,0:T(8,128)S(1)}, f32[3,8,512]{2,1,0:T(8,128)S(1)}, u32[]{:S(2)}, u32[]{:S(2)}) collective-permute-start(f32[3,8,512]{2,1,0:T(8,128)S(1)} %get-tuple-element.65), channel_id=1, source_target_pairs={{0,2},{2,0},{4,6},{6,4},{8,10},{10,8},{12,14},{14,12},{1,3},{3,1},... | collective-permute-start | bytes 147464 | tf_op jit(solution)/shard_map/ppermute | solution.py:29
  129.2 7.2 %collective-permute-start.23 = (f32[3,8,512]{2,1,0:T(8,128)S(1)}, f32[3,8,512]{2,1,0:T(8,128)S(1)}, u32[]{:S(2)}, u32[]{:S(2)}) collective-permute-start(f32[3,8,512]{2,1,0:T(8,128)S(1)} %get-tuple-element.66), channel_id=1, source_target_pairs={{0,14},{2,4},{4,2},{6,8},{8,6},{10,12},{12,10},{14,0},{1,15},{3,5}... | collective-permute-start | bytes 147464 | tf_op jit(solution)/shard_map/ppermute | solution.py:29
  136.5 12.8 %collective-permute-start.26 = (f32[30,8,128]{2,1,0:T(8,128)S(1)}, f32[30,8,128]{2,1,0:T(8,128)S(1)}, u32[]{:S(2)}, u32[]{:S(2)}) collective-permute-start(f32[30,8,128]{2,1,0:T(8,128)S(1)} %get-tuple-element.70), channel_id=1, source_target_pairs={{0,1},{1,0},{2,3},{3,2},{4,5},{5,4},{6,7},{7,6},{8,9},{9,8},{10,11... | collective-permute-start | bytes 368648 | tf_op jit(solution)/shard_map/ppermute | solution.py:33
  138.5 7.8 %collective-permute-start.24 = (f32[5,8,512]{2,1,0:T(8,128)S(1)}, f32[5,8,512]{2,1,0:T(8,128)S(1)}, u32[]{:S(2)}, u32[]{:S(2)}) collective-permute-start(f32[5,8,512]{2,1,0:T(8,128)S(1)} %get-tuple-element.68), channel_id=1, source_target_pairs={{0,16},{16,0},{32,48},{48,32},{64,80},{80,64},{96,112},{112,96},{1... | collective-permute-start | bytes 245768 | tf_op jit(solution)/shard_map/ppermute | solution.py:29
  141.6 7.7 %collective-permute-start.25 = (f32[5,8,512]{2,1,0:T(8,128)S(1)}, f32[5,8,512]{2,1,0:T(8,128)S(1)}, u32[]{:S(2)}, u32[]{:S(2)}) collective-permute-start(f32[5,8,512]{2,1,0:T(8,128)S(1)} %get-tuple-element.69), channel_id=1, source_target_pairs={{0,240},{16,32},{32,16},{48,64},{64,48},{80,96},{96,80},{112,128},... | collective-permute-start | bytes 245768 | tf_op jit(solution)/shard_map/ppermute | solution.py:29

commit v3 on v2

--- a/solution.py
+++ b/solution.py
@@ -56,7 +56,7 @@
 
 def call(body, outs, *args, scratch=(), smem=(), far=(), far_outs=()):
     args = [
-        a if i in far or i in smem else pltpu.with_memory_space_constraint(a, pltpu.VMEM)
+        a if i in smem else pltpu.with_memory_space_constraint(a, pltpu.HBM if i in far else pltpu.VMEM)
         for i, a in enumerate(args)
     ]
     return pl.pallas_call(
@@ -85,35 +85,50 @@
         b_ref[k] = jnp.where(odd, high, low)
 
 
-def put_edge(tile, z_ref, at=0):
+def merge(source, receiver, before, behind, courant, absorbing, now, prev, medium, z_ref):
     last = place("gz")[0] == 0
-    for k in range(tile.shape[0]):
-        z_ref[at + k] = jnp.where(last, tile[k, :, -LANES:], tile[k, :, :LANES])
-
-
-def pack(source, receiver, tile, a_ref, b_ref, z_ref):
-    for k in range(tile.shape[0]):
-        tile[k, 0:4] = source[k]
-        tile[k, 4:8] = receiver[k]
+    size_x, _, size_z = source.shape
+    for k in range(size_x):
+        now[k, 0:4] = source[k]
+        now[k, 4:8] = receiver[k]
+        prev[k, 0:4] = before[k]
+        prev[k, 4:8] = behind[k]
+        medium[k, 0:4] = courant[k]
+        medium[k, 4:8] = absorbing[k].astype(jnp.float32)
+    for n, tile in enumerate((now, prev, medium)):
+        for k in range(size_x):
+            z_ref[n * size_x + k] = jnp.where(last, tile[k, :, -LANES:], tile[k, :, :LANES])
+
+
+def pack(now, beyond, tile, a_ref, b_ref):
+    size_x, _, size_z = now.shape
+    for k in range(size_x):
+        tile[k, :, :size_z] = now[k]
+        tile[k, :, size_z:] = beyond[k]
     put_sides(tile, a_ref, b_ref, 4)
-    put_edge(tile, z_ref)
-
-
-def prepare(cell, wavelet, spots, traces, courant, absorbing, source, receiver, coef, before, inject, code_ref, amp_ref):
-    size_x, size_y, size_z = courant.shape
+
+
+def prepare(cell, wavelet, spots, traces, old, medium, beyond, coef, prev, inject, code_ref, amp_ref):
+    size_x, _, size_z = old.shape
+    first = lax.axis_index("gz") == 0
+    count = size_z // LANES
     for k in range(size_x):
-        before[k, 0:4] = source[k]
-        before[k, 4:8] = receiver[k]
-        damping = absorbing[k].astype(jnp.float32) / 16.0
-        inverse = 1.0 / (1.0 + damping)
-        for half in (slice(0, 4), slice(4, 8)):
-            coef[0, k, half] = 2.0 * inverse
-            coef[1, k, half] = (1.0 - damping) * inverse
-            coef[2, k, half] = courant[k] * inverse
+        prev[k, :, :size_z] = old[k]
+        prev[k, :, size_z:] = beyond[size_x + k]
+        for j in range(count + 1):
+            both = medium[k, :, chunk(j)] if j < count else beyond[2 * size_x + k]
+            upper = rows() < 4
+            turned = pltpu.roll(both, 4, axis=0)
+            courant = jnp.where(upper, both, turned)
+            damping = jnp.where(upper, turned, both) / 16.0
+            inverse = 1.0 / (1.0 + damping)
+            coef[0, k, :, chunk(j)] = 2.0 * inverse
+            coef[1, k, :, chunk(j)] = (1.0 - damping) * inverse
+            coef[2, k, :, chunk(j)] = courant * inverse
     gx, gy, gz = (lax.axis_index(a) for a in ("gx", "gy", "gz"))
-    sx, sy, sz = cell[0] - gx * size_x, cell[1] - gy * size_y, cell[2] - gz * size_z
-    at_x, at_y = spots[0:1] - gx * size_x, spots[1:2] - gy * size_y
-    inside = (at_x >= 0) & (at_x < size_x) & (at_y >= 0) & (at_y < size_y) & (gz == 0)
+    sx, sy, sz = cell[0] - gx * size_x, cell[1] - gy * 4, cell[2] - gz * size_z
+    at_x, at_y = spots[0:1] - gx * size_x, spots[1:2] - gy * 4
+    inside = (at_x >= 0) & (at_x < size_x) & (at_y >= 0) & (at_y < 4) & (gz == 0)
     code = jnp.where(inside, at_x * 8 + at_y + 4, -1)
     blocks = code.shape[1] // LANES
     for b in range(blocks):
@@ -130,8 +145,9 @@
                 sums[t] = sums[t] + jnp.where(hit, amp_ref[t, b], 0.0)
         for t in range(STEPS):
             sheet = jnp.where(lane == 0, jnp.sum(sums[t], axis=1, keepdims=True), 0.0)
-            for j in range(size_z // LANES):
-                spot = (row == sy) & (sy < 4) & (lane + j * LANES == sz) & (k == sx)
+            for j in range(count + 1):
+                start = j * LANES if j < count else jnp.where(first, size_z, -LANES)
+                spot = (row == sy) & (sy < 4) & (lane + start == sz) & (k == sx)
                 point = jnp.where(spot, wavelet[t], 0.0)
                 inject[t, k, :, chunk(j)] = point + sheet if j == 0 else point
         return carry
@@ -139,12 +155,13 @@
     lax.fori_loop(0, size_x, each, 0)
 
 
-def forward(step, cur, prev, coef, inject, xa, xb, ya, yb, z, new):
+def forward(step, cur, prev, coef, inject, xa, xb, ya, yb, new):
     size_x, _, size_z = cur.shape
     count = size_z // LANES
     _, odd_x, below_x, above_x = place("gx")
     _, odd_y, below_y, above_y = place("gy")
     first = lax.axis_index("gz") == 0
+    second = jnp.logical_not(first)
     wide = xa.shape[0] if step == 2 else 4
     row, lane = lax.rem(rows(), 4), lanes()
 
@@ -157,14 +174,14 @@
 
     for x in range(size_x):
         own = [cur[x, :, chunk(j)] for j in range(count)]
-        beyond = z[x]
-        before, after = kept(jnp.logical_not(first), beyond), kept(first, beyond)
         along = [None] * count
         for k, weight in enumerate(stencil_weights, 1):
-            up = [pltpu.roll(v, LANES - k, axis=1) for v in (*own, after)]
-            down = [pltpu.roll(v, k, axis=1) for v in (before, *own)]
+            up = [pltpu.roll(v, LANES - k, axis=1) for v in own]
+            down = [pltpu.roll(v, k, axis=1) for v in own]
+            after = [*up[1 : count - 1], kept(first, up[count - 1]), kept(second, up[0])]
+            before = [kept(second, down[count - 1]), *down[: count - 2], kept(first, down[count - 2])]
             for j in range(count):
-                both = jnp.where(lane < LANES - k, up[j], up[j + 1]) + jnp.where(lane >= k, down[j + 1], down[j])
+                both = jnp.where(lane < LANES - k, up[j], after[j]) + jnp.where(lane >= k, down[j], before[j])
                 both = both + at(x + k, j) + at(x - k, j)
                 along[j] = weight * both if along[j] is None else along[j] + weight * both
         for j in range(count):
@@ -215,45 +232,32 @@
     return cur[x, :, s]
 
 
-def first_step(cur, prev, coef, inject, xa, xb, ya, yb, z, new, a_ref, b_ref, z_ref):
-    forward(0, cur, prev, coef, inject, xa, xb, ya, yb, z, new)
+def first_step(cur, prev, coef, inject, xa, xb, ya, yb, new, a_ref, b_ref):
+    forward(0, cur, prev, coef, inject, xa, xb, ya, yb, new)
     put_sides(new, a_ref, b_ref, 4)
-    put_edge(new, z_ref)
-
-
-def second_step(cur, prev, coef, inject, xa, xb, ya, yb, z, new, a_ref, b_ref, z_ref):
-    forward(1, cur, prev, coef, inject, xa, xb, ya, yb, z, new)
+
+
+def second_step(cur, prev, coef, inject, xa, xb, ya, yb, new, a_ref, b_ref):
+    forward(1, cur, prev, coef, inject, xa, xb, ya, yb, new)
     put_sides(new, a_ref, b_ref, WIDE)
-    put_edge(new, z_ref)
-
-
-def put_wide_edge(cur, xa, xb, z_ref, at):
-    size_x, _, size_z = cur.shape
-    last = lax.axis_index("gz") == 0
-    for x in range(-WIDE, size_x + WIDE):
-        ends = [around_x(x, s, cur, xa, xb) for s in (slice(size_z - LANES, size_z), slice(0, LANES))]
-        z_ref[at + WIDE + x] = jnp.where(last, ends[0], ends[1])
-
-
-def third_step(cur, prev, coef, inject, xa, xb, ya, yb, z, new, a_ref, b_ref, z_ref):
-    forward(2, cur, prev, coef, inject, xa, xb, ya, yb, z, new)
+
+
+def third_step(cur, prev, coef, inject, xa, xb, ya, yb, new, a_ref, b_ref):
+    forward(2, cur, prev, coef, inject, xa, xb, ya, yb, new)
     size_x, _, size_z = cur.shape
     put_sides(new, a_ref, b_ref, 4)
     row = rows()
     put_margins(lambda x, j: margin(ya, yb, x, chunk(j), row), size_x, size_z // LANES, a_ref, b_ref, 4)
-    put_edge(new, z_ref)
-    put_wide_edge(cur, xa, xb, z_ref, size_x)
-
-
-def fourth_step(cur, prev, coef, inject, xa, xb, ya, yb, z, new, source, receiver, a_ref, b_ref, ya_ref, yb_ref):
-    forward(3, cur, prev, coef, inject, xa, xb, ya, yb, z, new)
-    size_x, _, size_z = cur.shape
-    put_sides(new, a_ref, b_ref, WIDE)
+
+
+def fourth_step(cur, prev, coef, inject, xa, xb, ya, yb, new, source, receiver, ya_ref, yb_ref):
+    forward(3, cur, prev, coef, inject, xa, xb, ya, yb, new)
+    size_x, _, size_z = source.shape
     odd = place("gy")[1]
     row = lax.rem(rows(), 4)
     for x in range(size_x):
-        source[x] = new[x, 0:4]
-        receiver[x] = new[x, 4:8]
+        source[x] = new[x, 0:4, :size_z]
+        receiver[x] = new[x, 4:8, :size_z]
     for i in range(size_x // 4):
         for j in range(size_z // LANES):
             tops, bottoms = [], []
@@ -269,8 +273,8 @@
             yb_ref[i, :, chunk(j)] = jnp.where(odd, high, low)
 
 
-def gather_edges(cur, xa, xb, ya, yb, margins, a_ref, b_ref, z_ref):
-    size_x, _, size_z = cur.shape
+def gather_edges(cur, ya, yb, margins, a_ref, b_ref):
+    size_x, _, size_z = margins.shape
     _, odd, below, above = place("gy")
     row = lax.rem(rows(), 4)
     for x in range(size_x):
@@ -283,15 +287,15 @@
                 low = pltpu.roll(low, q, axis=0)
             high = pltpu.roll(high, (q + 5) % 8, axis=0)
             margins[x, :, s] = jnp.where(row == 0, high, low)
-    put_margins(lambda x, j: margins[x, :, chunk(j)], size_x, size_z // LANES, a_ref, b_ref, 0)
-    put_wide_edge(cur, xa, xb, z_ref, 0)
-
-
-def widen(get_margin, cur, xa, xb, ma, mb, m_at, zw, z_at, first_ref, second_ref, first_z, second_z):
-    size_x, _, size_z = cur.shape
+    put_sides(cur, a_ref, b_ref, WIDE)
+    put_margins(lambda x, j: margins[x, :, chunk(j)], size_x, size_z // LANES, a_ref, b_ref, WIDE)
+
+
+def widen(get_margin, cur, xa, xb, ma, mb, m_at, first_ref, second_ref, first_z, second_z):
+    size_x = cur.shape[0]
+    size_z = first_ref.shape[2]
     _, odd, below, above = place("gx")
-    row = rows()
-    own = row < 4
+    own = rows() < 4
     for x in range(-WIDE, size_x + WIDE):
         e = x + WIDE
         for j in range(size_z // LANES):
@@ -308,22 +312,23 @@
             both = around_x(x, s, cur, xa, xb)
             first_ref[e, :, s] = jnp.where(own, both, pltpu.roll(edge, 4, axis=0))
             second_ref[e, :, s] = jnp.where(own, pltpu.roll(both, 4, axis=0), edge)
-        first_z[e] = zw[z_at + e]
-        second_z[e] = pltpu.roll(zw[z_at + e], 4, axis=0)
-
-
-def early(cur, xa, xb, ya, yb, ma, mb, zw, first_ref, second_ref, first_z, second_z):
+        beyond = around_x(x, slice(size_z, size_z + LANES), cur, xa, xb)
+        first_z[e] = beyond
+        second_z[e] = pltpu.roll(beyond, 4, axis=0)
+
+
+def early(cur, xa, xb, ya, yb, ma, mb, first_ref, second_ref, first_z, second_z):
     row = rows()
     widen(
-        lambda x, s: margin(ya, yb, x, s, row), cur, xa, xb, ma, mb, 4, zw, cur.shape[0],
+        lambda x, s: margin(ya, yb, x, s, row), cur, xa, xb, ma, mb, 4,
         first_ref, second_ref, first_z, second_z,
     )
 
 
-def filtered(s2, r2, s2z, r2z, cur, margins, xa, xb, ma, mb, zw, out, s4, r4, s4z, r4z):
-    size_x, _, size_z = cur.shape
+def filtered(s2, r2, s2z, r2z, cur, margins, xa, xb, out, s4, r4, s4z, r4z):
+    size_x, _, size_z = margins.shape
     count = size_z // LANES
-    widen(lambda x, s: margins[x, :, s], cur, xa, xb, ma, mb, 0, zw, 0, s4, r4, s4z, r4z)
+    widen(lambda x, s: margins[x, :, s], cur, xa, xb, xa, xb, WIDE, s4, r4, s4z, r4z)
     first = lax.axis_index("gz") == 0
     lane = lanes()
 
@@ -368,59 +373,61 @@
 ):
     f32 = jnp.float32
     size_x, size_y, size_z = courant.shape
-    tile = ((size_x, 8, size_z), f32)
+    deep_z = size_z + LANES
     wide_x = size_x + 2 * WIDE
     packed = (WIDE + 1) // 2
-
-    def side(n):
-        return ((n, 8, size_z), f32)
-
-    def edge(n):
-        return ((n, 8, LANES), f32)
-
-    now, a, b, z = call(pack, [tile, side(4), side(4), edge(size_x)], source_now, receiver_now, far=(0, 1))
-    halo0 = (*swap(a, b, "gx"), *swap(now, now, "gy"), cross(z))
+    tile = ((size_x, 8, deep_z), f32)
+    field = ((size_x, size_y, size_z), f32)
+
+    def side(n, z=size_z):
+        return ((n, 8, z), f32)
+
+    outer = side(wide_x), side(wide_x), side(wide_x, LANES), side(wide_x, LANES)
+    now, old, medium, z = call(
+        merge,
+        [side(size_x), side(size_x), side(size_x), side(3 * size_x, LANES)],
+        source_now, receiver_now, source_prev, receiver_prev, courant, absorbing,
+        far=range(6),
+    )
+    beyond = cross(z)
+    now, a, b = call(pack, [tile, side(4, deep_z), side(4, deep_z)], now, beyond)
+    halo0 = (*swap(a, b, "gx"), *swap(now, now, "gy"))
     blocks = receiver_cells.shape[0] // LANES
     coef, prev, inject = call(
         prepare,
         [((3, *tile[0]), f32), tile, ((STEPS, *tile[0]), f32)],
-        source_cell, wavelet, receiver_cells.T, traces, courant, absorbing, source_prev, receiver_prev,
+        source_cell, wavelet, receiver_cells.T, traces, old, medium, beyond,
         scratch=[pltpu.VMEM((blocks, 8, LANES), jnp.int32), pltpu.VMEM((STEPS, blocks, 8, LANES), f32)],
         smem=(0, 1),
-        far=range(8),
-    )
-    one, a, b, z = call(first_step, [tile, side(4), side(4), edge(size_x)], now, prev, coef, inject, *halo0)
-    halo1 = (*swap(a, b, "gx"), *swap(one, one, "gy"), cross(z))
-    two, a, b, z = call(second_step, [tile, side(WIDE), side(WIDE), edge(size_x)], one, now, coef, inject, *halo1)
-    halo2 = (*swap(a, b, "gx"), *swap(two, two, "gy"), cross(z))
-    three, a, b, z = call(
-        third_step,
-        [tile, side(4 + packed), side(4 + packed), edge(size_x + wide_x)],
-        two, one, coef, inject, *halo2,
-    )
-    halo3 = (*swap(a, b, "gx"), *swap(three, three, "gy"), cross(z))
-    field = ((size_x, size_y, size_z), f32)
-    four, source, receiver, a, b, c, d = call(
+        far=(2, 3),
+    )
+    one, a, b = call(first_step, [tile, side(4, deep_z), side(4, deep_z)], now, prev, coef, inject, *halo0)
+    halo1 = (*swap(a, b, "gx"), *swap(one, one, "gy"))
+    two, a, b = call(second_step, [tile, side(WIDE, deep_z), side(WIDE, deep_z)], one, now, coef, inject, *halo1)
+    halo2 = (*swap(a, b, "gx"), *swap(two, two, "gy"))
+    three, a, b = call(
+        third_step, [tile, side(4 + packed, deep_z), side(4 + packed, deep_z)], two, one, coef, inject, *halo2
+    )
+    halo3 = (*swap(a, b, "gx"), *swap(three, three, "gy"))
+    four, source, receiver, c, d = call(
         fourth_step,
-        [tile, field, field, side(WIDE), side(WIDE), side(size_x // 4), side(size_x // 4)],
+        [tile, field, field, side(size_x // 4), side(size_x // 4)],
         three, two, coef, inject, *halo3,
         far_outs=(1, 2),
     )
-    halo4 = (*swap(a, b, "gx"), *swap(c, d, "gy"))
-    s2, r2, s2z, r2z = call(
-        early,
-        [side(wide_x), side(wide_x), edge(wide_x), edge(wide_x)],
-        two, *halo2[:4], halo3[0], halo3[1], halo3[4],
-    )
-    margins, a, b, z = call(
-        gather_edges, [tile, side(packed), side(packed), edge(wide_x)], four, *halo4
-    )
-    halo5 = (*swap(a, b, "gx"), cross(z))
+    edges = swap(c, d, "gy")
+    margins, a, b = call(
+        gather_edges,
+        [side(size_x), side(WIDE + packed, deep_z), side(WIDE + packed, deep_z)],
+        four, *edges,
+    )
+    halo4 = swap(a, b, "gx")
+    before = call(early, outer, two, *halo2, halo3[0], halo3[1])
     (image,) = call(
         filtered,
         [((LAGS, size_x, size_y, size_z), jnp.bfloat16)],
-        s2, r2, s2z, r2z, four, margins, halo4[0], halo4[1], *halo5,
-        scratch=[pltpu.VMEM(s, f32) for s, _ in (side(wide_x), side(wide_x), edge(wide_x), edge(wide_x))],
+        *before, four, margins, *halo4,
+        scratch=[pltpu.VMEM(s, f32) for s, _ in outer],
         far_outs=(0,),
     )
     return source, receiver, image

time: 155 us -> 145 us (0.935)
  starting transfers between devices: 121 us -> 111 us
  local copies, waits for them, and re-layouts: 5.09 us -> 0.66 us
  waiting for transfers between devices: 16.9 us -> 20 us
  Pallas kernels: 9.82 us -> 11.7 us
    ppermute x5 -> x1, starting transfers between devices: 9.76 us -> 1.95 us  [cross(): return lax.ppermute(a, 'gz', [(0, 1), (1, 0)])]
    unnamed x20 -> x4, local copies, waits for them, and re-layouts: 5.09 us -> 0.66 us
    ppermute x22 -> x20, waiting for transfers between devices: 14.5 us -> 18.6 us  [swap(): return (lax.ppermute(a, axis, near), lax.ppermute(b, axis, far))]
    ppermute x22 -> x20, starting transfers between devices: 111 us -> 109 us  [swap(): return (lax.ppermute(a, axis, near), lax.ppermute(b, axis, far))]
    pallas_call x9 -> x10, Pallas kernels: 9.82 us -> 11.7 us  [call(): pl.pallas_call(body, out_shape=[jax.ShapeDtypeStruct(s, d) if i in far_ou...]
  transfers between devices with their start and end apart: 27 -> 21, of which waited for: 8 -> 8; matrix products, arithmetic and copies ran while one was open for 0% -> 0% of each run, Pallas kernels for 1% -> 2%
where the time goes in v3:
time: 145 us; the launch traced here: 144 us
  starting transfers between devices  111 us (77%)
  waiting for transfers between devices  20 us (14%)
  Pallas kernels  11.7 us (8%)
    ppermute x20, starting transfers between devices, swap(): return (lax.ppermute(a, axis, near), lax.ppermute(b, axis, far))  109 us
    ppermute x20, waiting for transfers between devices, swap(): return (lax.ppermute(a, axis, near), lax.ppermute(b, axis, far))  18.6 us
    pallas_call x10, Pallas kernels, call(): pl.pallas_call(body, out_shape=[jax.ShapeDtypeStruct(s, d) if i in far_ou...  11.7 us
  transfers between devices with their start and end apart: 21, of which 8 were waited for; matrix products, arithmetic and copies ran while one was open for 0% of the time, Pallas kernels for 2%

profile of v3, /device:TPU:80, one launch (start us, length us, event | category | flops | bytes accessed | tf_op | source)
XLA Modules:
  0.0 144.0 jit_solution(7169519962729899098)
XLA Ops:
  0.6 1.2 merge.1
  1.9 2.0 %collective-permute-start = (f32[36,8,128]{2,1,0:T(8,128)S(1)}, f32[36,8,128]{2,1,0:T(8,128)S(1)}, u32[]{:S(2)}, u32[]{:S(2)}) collective-permute-start(f32[36,8,128]{2,1,0:T(8,128)S(1)} %get-tuple-element.35), channel_id=1, source_target_pairs={{0,1},{1,0},{2,3},{3,2},{4,5},{5,4},{6,7},{7,6},{8,9},{9,8},{10,11... | collective-permute-start | bytes 442376 | tf_op jit(solution)/shard_map/ppermute | solution.py:33
  3.8 1.3 collective-permute-done.beyond
  5.2 5.8 %collective-permute-start.4 = (f32[12,8,640]{2,1,0:T(8,128)S(1)}, f32[12,8,640]{2,1,0:T(8,128)S(1)}, u32[]{:S(2)}, u32[]{:S(2)}) collective-permute-start(f32[12,8,640]{2,1,0:T(8,128)S(1)} %get-tuple-element.36.cur.prev), channel_id=1, source_target_pairs={{0,14},{2,4},{4,2},{6,8},{8,6},{10,12},{12,10},{14,0},{1,15},{3,5}... | collective-permute-start | bytes 737288 | tf_op jit(solution)/shard_map/ppermute | solution.py:29
  11.0 2.0 %collective-permute-start.3 = (f32[12,8,640]{2,1,0:T(8,128)S(1)}, f32[12,8,640]{2,1,0:T(8,128)S(1)}, u32[]{:S(2)}, u32[]{:S(2)}) collective-permute-start(f32[12,8,640]{2,1,0:T(8,128)S(1)} %get-tuple-element.36.cur.prev), channel_id=1, source_target_pairs={{0,2},{2,0},{4,6},{6,4},{8,10},{10,8},{12,14},{14,12},{1,3},{3,1},... | collective-permute-start | bytes 737288 | tf_op jit(solution)/shard_map/ppermute | solution.py:29
  12.9 6.0 %collective-permute-start.1 = (f32[4,8,640]{2,1,0:T(8,128)S(1)}, f32[4,8,640]{2,1,0:T(8,128)S(1)}, u32[]{:S(2)}, u32[]{:S(2)}) collective-permute-start(f32[4,8,640]{2,1,0:T(8,128)S(1)} %get-tuple-element.42), channel_id=1, source_target_pairs={{0,16},{16,0},{32,48},{48,32},{64,80},{80,64},{96,112},{112,96},{1... | collective-permute-start | bytes 245768 | tf_op jit(solution)/shard_map/ppermute | solution.py:29
  19.0 39.9 %collective-permute-start.2 = (f32[4,8,640]{2,1,0:T(8,128)S(1)}, f32[4,8,640]{2,1,0:T(8,128)S(1)}, u32[]{:S(2)}, u32[]{:S(2)}) collective-permute-start(f32[4,8,640]{2,1,0:T(8,128)S(1)} %get-tuple-element.43), channel_id=1, source_target_pairs={{0,240},{16,32},{32,16},{48,64},{64,48},{80,96},{96,80},{112,128},... | collective-permute-start | bytes 245768 | tf_op jit(solution)/shard_map/ppermute | solution.py:29
  58.9 0.0 copy-start
  58.9 0.0 copy-start.1
  58.9 0.6 copy-done
  59.6 0.0 copy-done.1
  59.6 2.2 %prepare.1 = (f32[3,12,8,640]{3,2,1,0:T(8,128)S(1)}, f32[12,8,640]{2,1,0:T(8,128)S(1)}, f32[4,12,8,640]{3,2,1,0:T(8,128)S(1)}) custom-call(s32[3]{0:T(128)S(1)} %copy-done, f32[4]{0:T(128)S(1)} %copy-done.1, s32[2,2048]{1,0:T(2,128)} %bitcast.1, f32[4,2048]{1,0:T(4,128)} %traces.1, f32[12,8,512]{2,1,0:T(8,128)S(1)} %get-tuple-element.37.old, ...), custom_call_target="tpu_custom_call" | custom-call | tf_op jit(solution)/shard_map/prepare/pallas_call | solution.py:62
  61.8 0.0 collective-permute-done.1.xa
  61.8 0.0 collective-permute-done.2.xb
  61.8 0.0 collective-permute-done.4.yb
  61.8 0.0 collective-permute-done.3.ya
  61.8 0.7 first_step.1
  62.5 4.5 %collective-permute-start.8 = (f32[12,8,640]{2,1,0:T(8,128)S(1)}, f32[12,8,640]{2,1,0:T(8,128)S(1)}, u32[]{:S(2)}, u32[]{:S(2)}) collective-permute-start(f32[12,8,640]{2,1,0:T(8,128)S(1)} %get-tuple-element.44.cur.prev), channel_id=1, source_target_pairs={{0,14},{2,4},{4,2},{6,8},{8,6},{10,12},{12,10},{14,0},{1,15},{3,5}... | collective-permute-start | bytes 737288 | tf_op jit(solution)/shard_map/ppermute | solution.py:29
  67.0 3.2 %collective-permute-start.7 = (f32[12,8,640]{2,1,0:T(8,128)S(1)}, f32[12,8,640]{2,1,0:T(8,128)S(1)}, u32[]{:S(2)}, u32[]{:S(2)}) collective-permute-start(f32[12,8,640]{2,1,0:T(8,128)S(1)} %get-tuple-element.44.cur.prev), channel_id=1, source_target_pairs={{0,2},{2,0},{4,6},{6,4},{8,10},{10,8},{12,14},{14,12},{1,3},{3,1},... | collective-permute-start | bytes 737288 | tf_op jit(solution)/shard_map/ppermute | solution.py:29
  70.3 2.0 %collective-permute-start.5 = (f32[4,8,640]{2,1,0:T(8,128)S(1)}, f32[4,8,640]{2,1,0:T(8,128)S(1)}, u32[]{:S(2)}, u32[]{:S(2)}) collective-permute-start(f32[4,8,640]{2,1,0:T(8,128)S(1)} %get-tuple-element.45), channel_id=1, source_target_pairs={{0,16},{16,0},{32,48},{48,32},{64,80},{80,64},{96,112},{112,96},{1... | collective-permute-start | bytes 245768 | tf_op jit(solution)/shard_map/ppermute | solution.py:29
  72.2 5.5 %collective-permute-start.6 = (f32[4,8,640]{2,1,0:T(8,128)S(1)}, f32[4,8,640]{2,1,0:T(8,128)S(1)}, u32[]{:S(2)}, u32[]{:S(2)}) collective-permute-start(f32[4,8,640]{2,1,0:T(8,128)S(1)} %get-tuple-element.46), channel_id=1, source_target_pairs={{0,240},{16,32},{32,16},{48,64},{64,48},{80,96},{96,80},{112,128},... | collective-permute-start | bytes 245768 | tf_op jit(solution)/shard_map/ppermute | solution.py:29
  77.7 0.0 collective-permute-done.5.xa
  77.7 2.4 %collective-permute-done.6.xb = f32[4,8,640]{2,1,0:T(8,128)S(1)} collective-permute-done((f32[4,8,640]{2,1,0:T(8,128)S(1)}, f32[4,8,640]{2,1,0:T(8,128)S(1)}, u32[]{:S(2)}, u32[]{:S(2)}) %collective-permute-start.6) | collective-permute-done | bytes 81952 | tf_op jit(solution)/shard_map/ppermute | solution.py:29
  80.1 0.0 collective-permute-done.8.yb
  80.1 0.0 collective-permute-done.7.ya
  80.1 0.7 second_step.1
  80.8 2.3 %collective-permute-start.12 = (f32[12,8,640]{2,1,0:T(8,128)S(1)}, f32[12,8,640]{2,1,0:T(8,128)S(1)}, u32[]{:S(2)}, u32[]{:S(2)}) collective-permute-start(f32[12,8,640]{2,1,0:T(8,128)S(1)} %get-tuple-element.47.cur.prev), channel_id=1, source_target_pairs={{0,14},{2,4},{4,2},{6,8},{8,6},{10,12},{12,10},{14,0},{1,15},{3,5}... | collective-permute-start | bytes 737288 | tf_op jit(solution)/shard_map/ppermute | solution.py:29
  83.2 3.0 %collective-permute-start.11 = (f32[12,8,640]{2,1,0:T(8,128)S(1)}, f32[12,8,640]{2,1,0:T(8,128)S(1)}, u32[]{:S(2)}, u32[]{:S(2)}) collective-permute-start(f32[12,8,640]{2,1,0:T(8,128)S(1)} %get-tuple-element.47.cur.prev), channel_id=1, source_target_pairs={{0,2},{2,0},{4,6},{6,4},{8,10},{10,8},{12,14},{14,12},{1,3},{3,1},... | collective-permute-start | bytes 737288 | tf_op jit(solution)/shard_map/ppermute | solution.py:29
  86.2 2.4 %collective-permute-start.9 = (f32[9,8,640]{2,1,0:T(8,128)S(1)}, f32[9,8,640]{2,1,0:T(8,128)S(1)}, u32[]{:S(2)}, u32[]{:S(2)}) collective-permute-start(f32[9,8,640]{2,1,0:T(8,128)S(1)} %get-tuple-element.48), channel_id=1, source_target_pairs={{0,16},{16,0},{32,48},{48,32},{64,80},{80,64},{96,112},{112,96},{1... | collective-permute-start | bytes 552968 | tf_op jit(solution)/shard_map/ppermute | solution.py:29
  88.6 4.7 %collective-permute-start.10 = (f32[9,8,640]{2,1,0:T(8,128)S(1)}, f32[9,8,640]{2,1,0:T(8,128)S(1)}, u32[]{:S(2)}, u32[]{:S(2)}) collective-permute-start(f32[9,8,640]{2,1,0:T(8,128)S(1)} %get-tuple-element.49), channel_id=1, source_target_pairs={{0,240},{16,32},{32,16},{48,64},{64,48},{80,96},{96,80},{112,128},... | collective-permute-start | bytes 552968 | tf_op jit(solution)/shard_map/ppermute | solution.py:29
  93.3 0.3 collective-permute-done.9.xa
  93.6 3.7 %collective-permute-done.10.xb = f32[9,8,640]{2,1,0:T(8,128)S(1)} collective-permute-done((f32[9,8,640]{2,1,0:T(8,128)S(1)}, f32[9,8,640]{2,1,0:T(8,128)S(1)}, u32[]{:S(2)}, u32[]{:S(2)}) %collective-permute-start.10) | collective-permute-done | bytes 184352 | tf_op jit(solution)/shard_map/ppermute | solution.py:29
  97.3 0.0 collective-permute-done.12.yb
  97.3 0.0 collective-permute-done.11.ya
  97.3 0.7 third_step.1
  98.0 3.7 %collective-permute-start.16 = (f32[12,8,640]{2,1,0:T(8,128)S(1)}, f32[12,8,640]{2,1,0:T(8,128)S(1)}, u32[]{:S(2)}, u32[]{:S(2)}) collective-permute-start(f32[12,8,640]{2,1,0:T(8,128)S(1)} %get-tuple-element.50.cur), channel_id=1, source_target_pairs={{0,14},{2,4},{4,2},{6,8},{8,6},{10,12},{12,10},{14,0},{1,15},{3,5}... | collective-permute-start | bytes 737288 | tf_op jit(solution)/shard_map/ppermute | solution.py:29
  101.8 2.0 %collective-permute-start.15 = (f32[12,8,640]{2,1,0:T(8,128)S(1)}, f32[12,8,640]{2,1,0:T(8,128)S(1)}, u32[]{:S(2)}, u32[]{:S(2)}) collective-permute-start(f32[12,8,640]{2,1,0:T(8,128)S(1)} %get-tuple-element.50.cur), channel_id=1, source_target_pairs={{0,2},{2,0},{4,6},{6,4},{8,10},{10,8},{12,14},{14,12},{1,3},{3,1},... | collective-permute-start | bytes 737288 | tf_op jit(solution)/shard_map/ppermute | solution.py:29
  103.7 2.3 %collective-permute-start.13 = (f32[9,8,640]{2,1,0:T(8,128)S(1)}, f32[9,8,640]{2,1,0:T(8,128)S(1)}, u32[]{:S(2)}, u32[]{:S(2)}) collective-permute-start(f32[9,8,640]{2,1,0:T(8,128)S(1)} %get-tuple-element.51), channel_id=1, source_target_pairs={{0,16},{16,0},{32,48},{48,32},{64,80},{80,64},{96,112},{112,96},{1... | collective-permute-start | bytes 552968 | tf_op jit(solution)/shard_map/ppermute | solution.py:29
  106.0 5.2 %collective-permute-start.14 = (f32[9,8,640]{2,1,0:T(8,128)S(1)}, f32[9,8,640]{2,1,0:T(8,128)S(1)}, u32[]{:S(2)}, u32[]{:S(2)}) collective-permute-start(f32[9,8,640]{2,1,0:T(8,128)S(1)} %get-tuple-element.52), channel_id=1, source_target_pairs={{0,240},{16,32},{32,16},{48,64},{64,48},{80,96},{96,80},{112,128},... | collective-permute-start | bytes 552968 | tf_op jit(solution)/shard_map/ppermute | solution.py:29
  111.2 0.0 collective-permute-done.13.xa.ma
  111.2 3.5 %collective-permute-done.14.xb.mb = f32[9,8,640]{2,1,0:T(8,128)S(1)} collective-permute-done((f32[9,8,640]{2,1,0:T(8,128)S(1)}, f32[9,8,640]{2,1,0:T(8,128)S(1)}, u32[]{:S(2)}, u32[]{:S(2)}) %collective-permute-start.14) | collective-permute-done | bytes 184352 | tf_op jit(solution)/shard_map/ppermute | solution.py:29
  114.7 0.0 collective-permute-done.16.yb
  114.7 0.0 collective-permute-done.15.ya
  114.7 1.5 %fourth_step.1 = (f32[12,8,640]{2,1,0:T(8,128)S(1)}, f32[12,4,512]{2,1,0:T(4,128)}, f32[12,4,512]{2,1,0:T(4,128)}, f32[3,8,512]{2,1,0:T(8,128)S(1)}, f32[3,8,512]{2,1,0:T(8,128)S(1)}) custom-call(f32[12,8,640]{2,1,0:T(8,128)S(1)} %get-tuple-element.50.cur, f32[12,8,640]{2,1,0:T(8,128)S(1)} %get-tuple-element.47.cur.prev, ...), custom_call_target="tpu_custom_call" | custom-call | tf_op jit(solution)/shard_map/fourth_step/pallas_call | solution.py:62
  116.1 3.9 %collective-permute-start.17 = (f32[3,8,512]{2,1,0:T(8,128)S(1)}, f32[3,8,512]{2,1,0:T(8,128)S(1)}, u32[]{:S(2)}, u32[]{:S(2)}) collective-permute-start(f32[3,8,512]{2,1,0:T(8,128)S(1)} %get-tuple-element.60), channel_id=1, source_target_pairs={{0,2},{2,0},{4,6},{6,4},{8,10},{10,8},{12,14},{14,12},{1,3},{3,1},... | collective-permute-start | bytes 147464 | tf_op jit(solution)/shard_map/ppermute | solution.py:29
  120.1 3.4 %collective-permute-start.18 = (f32[3,8,512]{2,1,0:T(8,128)S(1)}, f32[3,8,512]{2,1,0:T(8,128)S(1)}, u32[]{:S(2)}, u32[]{:S(2)}) collective-permute-start(f32[3,8,512]{2,1,0:T(8,128)S(1)} %get-tuple-element.61), channel_id=1, source_target_pairs={{0,14},{2,4},{4,2},{6,8},{8,6},{10,12},{12,10},{14,0},{1,15},{3,5}... | collective-permute-start | bytes 147464 | tf_op jit(solution)/shard_map/ppermute | solution.py:29
  123.5 0.0 collective-permute-done.17.ya
  123.5 3.8 %collective-permute-done.18.yb = f32[3,8,512]{2,1,0:T(8,128)S(1)} collective-permute-done((f32[3,8,512]{2,1,0:T(8,128)S(1)}, f32[3,8,512]{2,1,0:T(8,128)S(1)}, u32[]{:S(2)}, u32[]{:S(2)}) %collective-permute-start.18) | collective-permute-done | bytes 49184 | tf_op jit(solution)/shard_map/ppermute | solution.py:29
  127.3 0.1 gather_edges.1
  127.4 2.4 %collective-permute-start.19 = (f32[14,8,640]{2,1,0:T(8,128)S(1)}, f32[14,8,640]{2,1,0:T(8,128)S(1)}, u32[]{:S(2)}, u32[]{:S(2)}) collective-permute-start(f32[14,8,640]{2,1,0:T(8,128)S(1)} %get-tuple-element.63), channel_id=1, source_target_pairs={{0,16},{16,0},{32,48},{48,32},{64,80},{80,64},{96,112},{112,96},{1... | collective-permute-start | bytes 860168 | tf_op jit(solution)/shard_map/ppermute | solution.py:29
  129.8 4.7 %collective-permute-start.20 = (f32[14,8,640]{2,1,0:T(8,128)S(1)}, f32[14,8,640]{2,1,0:T(8,128)S(1)}, u32[]{:S(2)}, u32[]{:S(2)}) collective-permute-start(f32[14,8,640]{2,1,0:T(8,128)S(1)} %get-tuple-element.64), channel_id=1, source_target_pairs={{0,240},{16,32},{32,16},{48,64},{64,48},{80,96},{96,80},{112,128},... | collective-permute-start | bytes 860168 | tf_op jit(solution)/shard_map/ppermute | solution.py:29
  134.5 0.2 early.1
  134.7 1.3 collective-permute-done.19.xa
  135.9 3.7 %collective-permute-done.20.xb = f32[14,8,640]{2,1,0:T(8,128)S(1)} collective-permute-done((f32[14,8,640]{2,1,0:T(8,128)S(1)}, f32[14,8,640]{2,1,0:T(8,128)S(1)}, u32[]{:S(2)}, u32[]{:S(2)}) %collective-permute-start.20) | collective-permute-done | bytes 286752 | tf_op jit(solution)/shard_map/ppermute | solution.py:29
  139.6 4.5 %filtered.1 = bf16[16,12,4,512]{3,2,1,0:T(4,128)(2,1)} custom-call(f32[30,8,512]{2,1,0:T(8,128)S(1)} %get-tuple-element.55.s2, f32[30,8,512]{2,1,0:T(8,128)S(1)} %get-tuple-element.56.r2, f32[30,8,128]{2,1,0:T(8,128)S(1)} %get-tuple-element.57.s2z, f32[30,8,128]{2,1,0:T(8,128)S(1)} %get-tuple-element.58.r2z, f32[12,8,640]{2,1,0:T(8,128)S(1)} %get-tuple-element.59.cur, ...), custom_call_target="tpu_custom_call" | custom-call | tf_op jit(solution)/shard_map/filtered/pallas_call | solution.py:62
  (1 shorter events, 0.0 us)
Async XLA Ops:
  1.9 3.3 %collective-permute-start = (f32[36,8,128]{2,1,0:T(8,128)S(1)}, f32[36,8,128]{2,1,0:T(8,128)S(1)}, u32[]{:S(2)}, u32[]{:S(2)}) collective-permute-start(f32[36,8,128]{2,1,0:T(8,128)S(1)} %get-tuple-element.35), channel_id=1, source_target_pairs={{0,1},{1,0},{2,3},{3,2},{4,5},{5,4},{6,7},{7,6},{8,9},{9,8},{10,11... | collective-permute-start | bytes 442376 | tf_op jit(solution)/shard_map/ppermute | solution.py:33
  5.2 56.6 %collective-permute-start.4 = (f32[12,8,640]{2,1,0:T(8,128)S(1)}, f32[12,8,640]{2,1,0:T(8,128)S(1)}, u32[]{:S(2)}, u32[]{:S(2)}) collective-permute-start(f32[12,8,640]{2,1,0:T(8,128)S(1)} %get-tuple-element.36.cur.prev), channel_id=1, source_target_pairs={{0,14},{2,4},{4,2},{6,8},{8,6},{10,12},{12,10},{14,0},{1,15},{3,5}... | collective-permute-start | bytes 737288 | tf_op jit(solution)/shard_map/ppermute | solution.py:29
  11.0 50.8 %collective-permute-start.3 = (f32[12,8,640]{2,1,0:T(8,128)S(1)}, f32[12,8,640]{2,1,0:T(8,128)S(1)}, u32[]{:S(2)}, u32[]{:S(2)}) collective-permute-start(f32[12,8,640]{2,1,0:T(8,128)S(1)} %get-tuple-element.36.cur.prev), channel_id=1, source_target_pairs={{0,2},{2,0},{4,6},{6,4},{8,10},{10,8},{12,14},{14,12},{1,3},{3,1},... | collective-permute-start | bytes 737288 | tf_op jit(solution)/shard_map/ppermute | solution.py:29
  12.9 48.8 %collective-permute-start.1 = (f32[4,8,640]{2,1,0:T(8,128)S(1)}, f32[4,8,640]{2,1,0:T(8,128)S(1)}, u32[]{:S(2)}, u32[]{:S(2)}) collective-permute-start(f32[4,8,640]{2,1,0:T(8,128)S(1)} %get-tuple-element.42), channel_id=1, source_target_pairs={{0,16},{16,0},{32,48},{48,32},{64,80},{80,64},{96,112},{112,96},{1... | collective-permute-start | bytes 245768 | tf_op jit(solution)/shard_map/ppermute | solution.py:29
  19.0 42.8 %collective-permute-start.2 = (f32[4,8,640]{2,1,0:T(8,128)S(1)}, f32[4,8,640]{2,1,0:T(8,128)S(1)}, u32[]{:S(2)}, u32[]{:S(2)}) collective-permute-start(f32[4,8,640]{2,1,0:T(8,128)S(1)} %get-tuple-element.43), channel_id=1, source_target_pairs={{0,240},{16,32},{32,16},{48,64},{64,48},{80,96},{96,80},{112,128},... | collective-permute-start | bytes 245768 | tf_op jit(solution)/shard_map/ppermute | solution.py:29
  58.9 0.7 copy-start
  58.9 0.7 copy-start.1
  62.5 17.6 %collective-permute-start.8 = (f32[12,8,640]{2,1,0:T(8,128)S(1)}, f32[12,8,640]{2,1,0:T(8,128)S(1)}, u32[]{:S(2)}, u32[]{:S(2)}) collective-permute-start(f32[12,8,640]{2,1,0:T(8,128)S(1)} %get-tuple-element.44.cur.prev), channel_id=1, source_target_pairs={{0,14},{2,4},{4,2},{6,8},{8,6},{10,12},{12,10},{14,0},{1,15},{3,5}... | collective-permute-start | bytes 737288 | tf_op jit(solution)/shard_map/ppermute | solution.py:29
  67.0 13.1 %collective-permute-start.7 = (f32[12,8,640]{2,1,0:T(8,128)S(1)}, f32[12,8,640]{2,1,0:T(8,128)S(1)}, u32[]{:S(2)}, u32[]{:S(2)}) collective-permute-start(f32[12,8,640]{2,1,0:T(8,128)S(1)} %get-tuple-element.44.cur.prev), channel_id=1, source_target_pairs={{0,2},{2,0},{4,6},{6,4},{8,10},{10,8},{12,14},{14,12},{1,3},{3,1},... | collective-permute-start | bytes 737288 | tf_op jit(solution)/shard_map/ppermute | solution.py:29
  70.3 7.4 %collective-permute-start.5 = (f32[4,8,640]{2,1,0:T(8,128)S(1)}, f32[4,8,640]{2,1,0:T(8,128)S(1)}, u32[]{:S(2)}, u32[]{:S(2)}) collective-permute-start(f32[4,8,640]{2,1,0:T(8,128)S(1)} %get-tuple-element.45), channel_id=1, source_target_pairs={{0,16},{16,0},{32,48},{48,32},{64,80},{80,64},{96,112},{112,96},{1... | collective-permute-start | bytes 245768 | tf_op jit(solution)/shard_map/ppermute | solution.py:29
  72.2 7.9 %collective-permute-start.6 = (f32[4,8,640]{2,1,0:T(8,128)S(1)}, f32[4,8,640]{2,1,0:T(8,128)S(1)}, u32[]{:S(2)}, u32[]{:S(2)}) collective-permute-start(f32[4,8,640]{2,1,0:T(8,128)S(1)} %get-tuple-element.46), channel_id=1, source_target_pairs={{0,240},{16,32},{32,16},{48,64},{64,48},{80,96},{96,80},{112,128},... | collective-permute-start | bytes 245768 | tf_op jit(solution)/shard_map/ppermute | solution.py:29
  80.8 16.5 %collective-permute-start.12 = (f32[12,8,640]{2,1,0:T(8,128)S(1)}, f32[12,8,640]{2,1,0:T(8,128)S(1)}, u32[]{:S(2)}, u32[]{:S(2)}) collective-permute-start(f32[12,8,640]{2,1,0:T(8,128)S(1)} %get-tuple-element.47.cur.prev), channel_id=1, source_target_pairs={{0,14},{2,4},{4,2},{6,8},{8,6},{10,12},{12,10},{14,0},{1,15},{3,5}... | collective-permute-start | bytes 737288 | tf_op jit(solution)/shard_map/ppermute | solution.py:29
  83.2 14.1 %collective-permute-start.11 = (f32[12,8,640]{2,1,0:T(8,128)S(1)}, f32[12,8,640]{2,1,0:T(8,128)S(1)}, u32[]{:S(2)}, u32[]{:S(2)}) collective-permute-start(f32[12,8,640]{2,1,0:T(8,128)S(1)} %get-tuple-element.47.cur.prev), channel_id=1, source_target_pairs={{0,2},{2,0},{4,6},{6,4},{8,10},{10,8},{12,14},{14,12},{1,3},{3,1},... | collective-permute-start | bytes 737288 | tf_op jit(solution)/shard_map/ppermute | solution.py:29
  86.2 7.5 %collective-permute-start.9 = (f32[9,8,640]{2,1,0:T(8,128)S(1)}, f32[9,8,640]{2,1,0:T(8,128)S(1)}, u32[]{:S(2)}, u32[]{:S(2)}) collective-permute-start(f32[9,8,640]{2,1,0:T(8,128)S(1)} %get-tuple-element.48), channel_id=1, source_target_pairs={{0,16},{16,0},{32,48},{48,32},{64,80},{80,64},{96,112},{112,96},{1... | collective-permute-start | bytes 552968 | tf_op jit(solution)/shard_map/ppermute | solution.py:29
  88.6 8.7 %collective-permute-start.10 = (f32[9,8,640]{2,1,0:T(8,128)S(1)}, f32[9,8,640]{2,1,0:T(8,128)S(1)}, u32[]{:S(2)}, u32[]{:S(2)}) collective-permute-start(f32[9,8,640]{2,1,0:T(8,128)S(1)} %get-tuple-element.49), channel_id=1, source_target_pairs={{0,240},{16,32},{32,16},{48,64},{64,48},{80,96},{96,80},{112,128},... | collective-permute-start | bytes 552968 | tf_op jit(solution)/shard_map/ppermute | solution.py:29
  98.0 16.6 %collective-permute-start.16 = (f32[12,8,640]{2,1,0:T(8,128)S(1)}, f32[12,8,640]{2,1,0:T(8,128)S(1)}, u32[]{:S(2)}, u32[]{:S(2)}) collective-permute-start(f32[12,8,640]{2,1,0:T(8,128)S(1)} %get-tuple-element.50.cur), channel_id=1, source_target_pairs={{0,14},{2,4},{4,2},{6,8},{8,6},{10,12},{12,10},{14,0},{1,15},{3,5}... | collective-permute-start | bytes 737288 | tf_op jit(solution)/shard_map/ppermute | solution.py:29
  101.8 12.9 %collective-permute-start.15 = (f32[12,8,640]{2,1,0:T(8,128)S(1)}, f32[12,8,640]{2,1,0:T(8,128)S(1)}, u32[]{:S(2)}, u32[]{:S(2)}) collective-permute-start(f32[12,8,640]{2,1,0:T(8,128)S(1)} %get-tuple-element.50.cur), channel_id=1, source_target_pairs={{0,2},{2,0},{4,6},{6,4},{8,10},{10,8},{12,14},{14,12},{1,3},{3,1},... | collective-permute-start | bytes 737288 | tf_op jit(solution)/shard_map/ppermute | solution.py:29
  103.7 7.5 %collective-permute-start.13 = (f32[9,8,640]{2,1,0:T(8,128)S(1)}, f32[9,8,640]{2,1,0:T(8,128)S(1)}, u32[]{:S(2)}, u32[]{:S(2)}) collective-permute-start(f32[9,8,640]{2,1,0:T(8,128)S(1)} %get-tuple-element.51), channel_id=1, source_target_pairs={{0,16},{16,0},{32,48},{48,32},{64,80},{80,64},{96,112},{112,96},{1... | collective-permute-start | bytes 552968 | tf_op jit(solution)/shard_map/ppermute | solution.py:29
  106.0 8.7 %collective-permute-start.14 = (f32[9,8,640]{2,1,0:T(8,128)S(1)}, f32[9,8,640]{2,1,0:T(8,128)S(1)}, u32[]{:S(2)}, u32[]{:S(2)}) collective-permute-start(f32[9,8,640]{2,1,0:T(8,128)S(1)} %get-tuple-element.52), channel_id=1, source_target_pairs={{0,240},{16,32},{32,16},{48,64},{64,48},{80,96},{96,80},{112,128},... | collective-permute-start | bytes 552968 | tf_op jit(solution)/shard_map/ppermute | solution.py:29
  116.1 7.3 %collective-permute-start.17 = (f32[3,8,512]{2,1,0:T(8,128)S(1)}, f32[3,8,512]{2,1,0:T(8,128)S(1)}, u32[]{:S(2)}, u32[]{:S(2)}) collective-permute-start(f32[3,8,512]{2,1,0:T(8,128)S(1)} %get-tuple-element.60), channel_id=1, source_target_pairs={{0,2},{2,0},{4,6},{6,4},{8,10},{10,8},{12,14},{14,12},{1,3},{3,1},... | collective-permute-start | bytes 147464 | tf_op jit(solution)/shard_map/ppermute | solution.py:29
  120.1 7.2 %collective-permute-start.18 = (f32[3,8,512]{2,1,0:T(8,128)S(1)}, f32[3,8,512]{2,1,0:T(8,128)S(1)}, u32[]{:S(2)}, u32[]{:S(2)}) collective-permute-start(f32[3,8,512]{2,1,0:T(8,128)S(1)} %get-tuple-element.61), channel_id=1, source_target_pairs={{0,14},{2,4},{4,2},{6,8},{8,6},{10,12},{12,10},{14,0},{1,15},{3,5}... | collective-permute-start | bytes 147464 | tf_op jit(solution)/shard_map/ppermute | solution.py:29
  127.4 8.6 %collective-permute-start.19 = (f32[14,8,640]{2,1,0:T(8,128)S(1)}, f32[14,8,640]{2,1,0:T(8,128)S(1)}, u32[]{:S(2)}, u32[]{:S(2)}) collective-permute-start(f32[14,8,640]{2,1,0:T(8,128)S(1)} %get-tuple-element.63), channel_id=1, source_target_pairs={{0,16},{16,0},{32,48},{48,32},{64,80},{80,64},{96,112},{112,96},{1... | collective-permute-start | bytes 860168 | tf_op jit(solution)/shard_map/ppermute | solution.py:29
  129.8 9.8 %collective-permute-start.20 = (f32[14,8,640]{2,1,0:T(8,128)S(1)}, f32[14,8,640]{2,1,0:T(8,128)S(1)}, u32[]{:S(2)}, u32[]{:S(2)}) collective-permute-start(f32[14,8,640]{2,1,0:T(8,128)S(1)} %get-tuple-element.64), channel_id=1, source_target_pairs={{0,240},{16,32},{32,16},{48,64},{64,48},{80,96},{96,80},{112,128},... | collective-permute-start | bytes 860168 | tf_op jit(solution)/shard_map/ppermute | solution.py:29

commit v4 on v3

--- a/solution.py
+++ b/solution.py
@@ -30,7 +30,7 @@
 
 
 def cross(a):
-    return lax.ppermute(a, "gz", [(0, 1), (1, 0)])
+    return lax.all_gather(a, "gz")
 
 
 def rows():
@@ -54,7 +54,7 @@
     return jnp.where(flag, value, jnp.zeros_like(value))
 
 
-def call(body, outs, *args, scratch=(), smem=(), far=(), far_outs=()):
+def call(body, outs, *args, scratch=(), smem=(), far=(), far_outs=(), left=()):
     args = [
         a if i in smem else pltpu.with_memory_space_constraint(a, pltpu.HBM if i in far else pltpu.VMEM)
         for i, a in enumerate(args)
@@ -69,7 +69,9 @@
             pl.BlockSpec(memory_space=pltpu.SMEM if i in smem else pltpu.VMEM)
             for i in range(len(args))
         ],
-        out_specs=[pl.BlockSpec(memory_space=pltpu.VMEM)] * len(outs),
+        out_specs=[
+            pl.BlockSpec(memory_space=pltpu.HBM if i in left else pltpu.VMEM) for i in range(len(outs))
+        ],
         scratch_shapes=list(scratch),
         compiler_params=pltpu.CompilerParams(vmem_limit_bytes=8 * 2**20),
         name=body.func.__name__ if isinstance(body, functools.partial) else body.__name__,
@@ -102,9 +104,10 @@
 
 def pack(now, beyond, tile, a_ref, b_ref):
     size_x, _, size_z = now.shape
+    other = 1 - lax.axis_index("gz")
     for k in range(size_x):
         tile[k, :, :size_z] = now[k]
-        tile[k, :, size_z:] = beyond[k]
+        tile[k, :, size_z:] = beyond[other, k]
     put_sides(tile, a_ref, b_ref, 4)
 
 
@@ -112,11 +115,12 @@
     size_x, _, size_z = old.shape
     first = lax.axis_index("gz") == 0
     count = size_z // LANES
+    other = 1 - lax.axis_index("gz")
     for k in range(size_x):
         prev[k, :, :size_z] = old[k]
-        prev[k, :, size_z:] = beyond[size_x + k]
+        prev[k, :, size_z:] = beyond[other, size_x + k]
         for j in range(count + 1):
-            both = medium[k, :, chunk(j)] if j < count else beyond[2 * size_x + k]
+            both = medium[k, :, chunk(j)] if j < count else beyond[other, 2 * size_x + k]
             upper = rows() < 4
             turned = pltpu.roll(both, 4, axis=0)
             courant = jnp.where(upper, both, turned)
@@ -250,14 +254,12 @@
     put_margins(lambda x, j: margin(ya, yb, x, chunk(j), row), size_x, size_z // LANES, a_ref, b_ref, 4)
 
 
-def fourth_step(cur, prev, coef, inject, xa, xb, ya, yb, new, source, receiver, ya_ref, yb_ref):
+def fourth_step(cur, prev, coef, inject, xa, xb, ya, yb, new, ya_ref, yb_ref):
     forward(3, cur, prev, coef, inject, xa, xb, ya, yb, new)
-    size_x, _, size_z = source.shape
+    size_x = new.shape[0]
+    size_z = ya_ref.shape[2]
     odd = place("gy")[1]
     row = lax.rem(rows(), 4)
-    for x in range(size_x):
-        source[x] = new[x, 0:4, :size_z]
-        receiver[x] = new[x, 4:8, :size_z]
     for i in range(size_x // 4):
         for j in range(size_z // LANES):
             tops, bottoms = [], []
@@ -317,46 +319,65 @@
         second_z[e] = pltpu.roll(beyond, 4, axis=0)
 
 
-def early(cur, xa, xb, ya, yb, ma, mb, first_ref, second_ref, first_z, second_z):
+def laplace(first, second, first_z, second_z, lag, emit):
+    size_x = first.shape[0] - 2 * WIDE
+    count = first.shape[2] // LANES
+    core = lax.axis_index("gz") == 0
+    lane = lanes()
+
+    def image(x):
+        a, b = x - lag + HALF + WIDE, x + lag - HALF + WIDE
+        return [first[a, :, chunk(j)] * second[b, :, chunk(j)] for j in range(count)]
+
+    previous, here = image(-1), image(0)
+    for x in range(size_x):
+        following = image(x + 1)
+        beyond = first_z[x - lag + HALF + WIDE] * second_z[x + lag - HALF + WIDE]
+        before, after = kept(jnp.logical_not(core), beyond), kept(core, beyond)
+        up = [pltpu.roll(v, LANES - 1, axis=1) for v in (*here, after)]
+        down = [pltpu.roll(v, 1, axis=1) for v in (before, *here)]
+        for j in range(count):
+            along = jnp.where(lane < LANES - 1, up[j], up[j + 1]) + jnp.where(lane >= 1, down[j + 1], down[j])
+            across = pltpu.roll(here[j], 7, axis=0) + pltpu.roll(here[j], 1, axis=0)
+            emit(x, chunk(j), 6.0 * here[j] - (previous[j] + following[j] + across + along))
+        previous, here = here, following
+
+
+def early(cur, xa, xb, ya, yb, ma, mb, last, partial, source, receiver, *wide):
     row = rows()
-    widen(
-        lambda x, s: margin(ya, yb, x, s, row), cur, xa, xb, ma, mb, 4,
-        first_ref, second_ref, first_z, second_z,
-    )
-
-
-def filtered(s2, r2, s2z, r2z, cur, margins, xa, xb, out, s4, r4, s4z, r4z):
-    size_x, _, size_z = margins.shape
-    count = size_z // LANES
-    widen(lambda x, s: margins[x, :, s], cur, xa, xb, xa, xb, WIDE, s4, r4, s4z, r4z)
-    first = lax.axis_index("gz") == 0
-    lane = lanes()
+    size_x, _, size_z = source.shape
+    for x in range(size_x):
+        source[x] = last[x, 0:4, :size_z]
+        receiver[x] = last[x, 4:8, :size_z]
+    widen(lambda x, s: margin(ya, yb, x, s, row), cur, xa, xb, ma, mb, 4, *wide)
 
     def each(lag, carry):
-        def image(x):
-            a, b = x - lag + HALF + WIDE, x + lag - HALF + WIDE
-            return [
-                s2[a, :, chunk(j)] * r2[b, :, chunk(j)] + s4[a, :, chunk(j)] * r4[b, :, chunk(j)]
-                for j in range(count)
-            ]
-
-        previous, here = image(-1), image(0)
-        for x in range(size_x):
-            following = image(x + 1)
-            a, b = x - lag + HALF + WIDE, x + lag - HALF + WIDE
-            beyond = s2z[a] * r2z[b] + s4z[a] * r4z[b]
-            before, after = kept(jnp.logical_not(first), beyond), kept(first, beyond)
-            up = [pltpu.roll(v, LANES - 1, axis=1) for v in (*here, after)]
-            down = [pltpu.roll(v, 1, axis=1) for v in (before, *here)]
-            for j in range(count):
-                along = jnp.where(lane < LANES - 1, up[j], up[j + 1]) + jnp.where(lane >= 1, down[j + 1], down[j])
-                across = pltpu.roll(here[j], 7, axis=0) + pltpu.roll(here[j], 1, axis=0)
-                value = 6.0 * here[j] - (previous[j] + following[j] + across + along)
-                out[lag, x, :, chunk(j)] = value[0:4].astype(jnp.bfloat16)
-            previous, here = here, following
+        def emit(x, s, value):
+            partial[lag, x, :, s] = value[0:4]
+
+        laplace(*wide, lag, emit)
         return carry
 
     lax.fori_loop(0, LAGS, each, 0)
+
+
+def filtered(partial, cur, margins, xa, xb, out, held, done, *wide):
+    widen(lambda x, s: margins[x, :, s], cur, xa, xb, xa, xb, WIDE, *wide)
+
+    def each(lag, carry):
+        def emit(x, s, value):
+            held[lag, x, :, s] = (partial[lag, x, :, s] + value[0:4]).astype(jnp.bfloat16)
+
+        laplace(*wide, lag, emit)
+        pltpu.make_async_copy(held.at[lag], out.at[lag], done.at[lag]).start()
+        return carry
+
+    def finish(lag, carry):
+        pltpu.make_async_copy(held.at[lag], out.at[lag], done.at[lag]).wait()
+        return carry
+
+    lax.fori_loop(0, LAGS, each, 0)
+    lax.fori_loop(0, LAGS, finish, 0)
 
 
 def local(
@@ -409,11 +430,8 @@
         third_step, [tile, side(4 + packed, deep_z), side(4 + packed, deep_z)], two, one, coef, inject, *halo2
     )
     halo3 = (*swap(a, b, "gx"), *swap(three, three, "gy"))
-    four, source, receiver, c, d = call(
-        fourth_step,
-        [tile, field, field, side(size_x // 4), side(size_x // 4)],
-        three, two, coef, inject, *halo3,
-        far_outs=(1, 2),
+    four, c, d = call(
+        fourth_step, [tile, side(size_x // 4), side(size_x // 4)], three, two, coef, inject, *halo3
     )
     edges = swap(c, d, "gy")
     margins, a, b = call(
@@ -422,13 +440,20 @@
         four, *edges,
     )
     halo4 = swap(a, b, "gx")
-    before = call(early, outer, two, *halo2, halo3[0], halo3[1])
+    picture = (LAGS, size_x, size_y, size_z)
+    wide = [pltpu.VMEM(s, f32) for s, _ in outer]
+    partial, source, receiver = call(
+        early, [(picture, f32), field, field], two, *halo2, halo3[0], halo3[1], four,
+        scratch=wide,
+        far_outs=(1, 2),
+    )
     (image,) = call(
         filtered,
-        [((LAGS, size_x, size_y, size_z), jnp.bfloat16)],
-        *before, four, margins, *halo4,
-        scratch=[pltpu.VMEM(s, f32) for s, _ in outer],
+        [(picture, jnp.bfloat16)],
+        partial, four, margins, *halo4,
+        scratch=[pltpu.VMEM(picture, jnp.bfloat16), pltpu.SemaphoreType.DMA((LAGS,)), *wide],
         far_outs=(0,),
+        left=(0,),
     )
     return source, receiver, image
 

time: 145 us -> 143 us (0.986)
  starting transfers between devices: 111 us -> 107 us
  waiting for transfers between devices: 20 us -> 16.8 us
  Pallas kernels: 11.7 us -> 14.4 us
  blocking collectives: 0 us -> 2.07 us
    pallas_call x10, Pallas kernels: 11.7 us -> 14.4 us  [call(): pl.pallas_call(body, out_shape=[jax.ShapeDtypeStruct(s, d) if i in far_ou...]
    all_gather x0 -> x1, blocking collectives: none -> 2.07 us  [cross(): return lax.all_gather(a, 'gz')]
    ppermute x1 -> x0, starting transfers between devices: 1.95 us -> none  [cross(): return lax.ppermute(a, 'gz', [(0, 1), (1, 0)])]
    ppermute x20, starting transfers between devices: 109 us -> 107 us  [swap(): return (lax.ppermute(a, axis, near), lax.ppermute(b, axis, far))]
    ppermute x20, waiting for transfers between devices: 18.6 us -> 16.8 us  [swap(): return (lax.ppermute(a, axis, near), lax.ppermute(b, axis, far))]
  transfers between devices with their start and end apart: 21 -> 20, of which waited for: 8 -> 7; matrix products, arithmetic and copies ran while one was open for 0% -> 0% of each run, Pallas kernels for 2% -> 4%
where the time goes in v4:
time: 143 us; the launch traced here: 142 us
  starting transfers between devices  107 us (75%)
  waiting for transfers between devices  16.8 us (12%)
  Pallas kernels  14.4 us (10%)
  blocking collectives  2.07 us (1%)
    ppermute x20, starting transfers between devices, swap(): return (lax.ppermute(a, axis, near), lax.ppermute(b, axis, far))  107 us
    ppermute x20, waiting for transfers between devices, swap(): return (lax.ppermute(a, axis, near), lax.ppermute(b, axis, far))  16.8 us
    pallas_call x10, Pallas kernels, call(): pl.pallas_call(body, out_shape=[jax.ShapeDtypeStruct(s, d) if i in far_ou...  14.4 us
  transfers between devices with their start and end apart: 20, of which 7 were waited for; matrix products, arithmetic and copies ran while one was open for 0% of the time, Pallas kernels for 4%

profile of v4, /device:TPU:80, one launch (start us, length us, event | category | flops | bytes accessed | tf_op | source)
XLA Modules:
  0.0 142.4 jit_solution(4704785769428802418)
XLA Ops:
  0.6 1.2 merge.1
  1.9 2.1 %all-gather = f32[72,8,128]{2,1,0:T(8,128)S(1)} all-gather(f32[36,8,128]{2,1,0:T(8,128)S(1)} %get-tuple-element.32), channel_id=2, replica_groups=mesh['shot'=2,'gx'=16,'gy'=8,'gz'=2] {'gz'}, dimensions={0}, use_global_device_ids=true | all-gather | bytes 442368 | tf_op jit(solution)/shard_map/all_gather | solution.py:33
  4.0 5.8 %collective-permute-start.3 = (f32[12,8,640]{2,1,0:T(8,128)S(1)}, f32[12,8,640]{2,1,0:T(8,128)S(1)}, u32[]{:S(2)}, u32[]{:S(2)}) collective-permute-start(f32[12,8,640]{2,1,0:T(8,128)S(1)} %get-tuple-element.33.cur.prev), channel_id=1, source_target_pairs={{0,14},{2,4},{4,2},{6,8},{8,6},{10,12},{12,10},{14,0},{1,15},{3,5}... | collective-permute-start | bytes 737288 | tf_op jit(solution)/shard_map/ppermute | solution.py:29
  9.7 2.0 %collective-permute-start.2 = (f32[12,8,640]{2,1,0:T(8,128)S(1)}, f32[12,8,640]{2,1,0:T(8,128)S(1)}, u32[]{:S(2)}, u32[]{:S(2)}) collective-permute-start(f32[12,8,640]{2,1,0:T(8,128)S(1)} %get-tuple-element.33.cur.prev), channel_id=1, source_target_pairs={{0,2},{2,0},{4,6},{6,4},{8,10},{10,8},{12,14},{14,12},{1,3},{3,1},... | collective-permute-start | bytes 737288 | tf_op jit(solution)/shard_map/ppermute | solution.py:29
  11.7 6.0 %collective-permute-start = (f32[4,8,640]{2,1,0:T(8,128)S(1)}, f32[4,8,640]{2,1,0:T(8,128)S(1)}, u32[]{:S(2)}, u32[]{:S(2)}) collective-permute-start(f32[4,8,640]{2,1,0:T(8,128)S(1)} %get-tuple-element.39), channel_id=1, source_target_pairs={{0,16},{16,0},{32,48},{48,32},{64,80},{80,64},{96,112},{112,96},{1... | collective-permute-start | bytes 245768 | tf_op jit(solution)/shard_map/ppermute | solution.py:29
  17.7 39.9 %collective-permute-start.1 = (f32[4,8,640]{2,1,0:T(8,128)S(1)}, f32[4,8,640]{2,1,0:T(8,128)S(1)}, u32[]{:S(2)}, u32[]{:S(2)}) collective-permute-start(f32[4,8,640]{2,1,0:T(8,128)S(1)} %get-tuple-element.40), channel_id=1, source_target_pairs={{0,240},{16,32},{32,16},{48,64},{64,48},{80,96},{96,80},{112,128},... | collective-permute-start | bytes 245768 | tf_op jit(solution)/shard_map/ppermute | solution.py:29
  57.7 0.0 copy-start
  57.7 0.6 copy-done
  58.3 0.0 copy-start.1
  58.3 0.7 copy-done.1
  59.0 2.2 %prepare.1 = (f32[3,12,8,640]{3,2,1,0:T(8,128)S(1)}, f32[12,8,640]{2,1,0:T(8,128)S(1)}, f32[4,12,8,640]{3,2,1,0:T(8,128)S(1)}) custom-call(s32[3]{0:T(128)S(1)} %copy-done, f32[4]{0:T(128)S(1)} %copy-done.1, s32[2,2048]{1,0:T(2,128)} %bitcast.4, f32[4,2048]{1,0:T(4,128)} %traces.1, f32[12,8,512]{2,1,0:T(8,128)S(1)} %get-tuple-element.34.old, ...), custom_call_target="tpu_custom_call" | custom-call | tf_op jit(solution)/shard_map/prepare/pallas_call | solution.py:62
  61.2 0.0 collective-permute-done.xa
  61.2 0.0 collective-permute-done.1.xb
  61.2 0.0 collective-permute-done.3.yb
  61.2 0.0 collective-permute-done.2.ya
  61.2 0.7 first_step.1
  61.9 4.5 %collective-permute-start.7 = (f32[12,8,640]{2,1,0:T(8,128)S(1)}, f32[12,8,640]{2,1,0:T(8,128)S(1)}, u32[]{:S(2)}, u32[]{:S(2)}) collective-permute-start(f32[12,8,640]{2,1,0:T(8,128)S(1)} %get-tuple-element.41.cur.prev), channel_id=1, source_target_pairs={{0,14},{2,4},{4,2},{6,8},{8,6},{10,12},{12,10},{14,0},{1,15},{3,5}... | collective-permute-start | bytes 737288 | tf_op jit(solution)/shard_map/ppermute | solution.py:29
  66.4 3.2 %collective-permute-start.6 = (f32[12,8,640]{2,1,0:T(8,128)S(1)}, f32[12,8,640]{2,1,0:T(8,128)S(1)}, u32[]{:S(2)}, u32[]{:S(2)}) collective-permute-start(f32[12,8,640]{2,1,0:T(8,128)S(1)} %get-tuple-element.41.cur.prev), channel_id=1, source_target_pairs={{0,2},{2,0},{4,6},{6,4},{8,10},{10,8},{12,14},{14,12},{1,3},{3,1},... | collective-permute-start | bytes 737288 | tf_op jit(solution)/shard_map/ppermute | solution.py:29
  69.7 2.0 %collective-permute-start.4 = (f32[4,8,640]{2,1,0:T(8,128)S(1)}, f32[4,8,640]{2,1,0:T(8,128)S(1)}, u32[]{:S(2)}, u32[]{:S(2)}) collective-permute-start(f32[4,8,640]{2,1,0:T(8,128)S(1)} %get-tuple-element.42), channel_id=1, source_target_pairs={{0,16},{16,0},{32,48},{48,32},{64,80},{80,64},{96,112},{112,96},{1... | collective-permute-start | bytes 245768 | tf_op jit(solution)/shard_map/ppermute | solution.py:29
  71.6 4.8 %collective-permute-start.5 = (f32[4,8,640]{2,1,0:T(8,128)S(1)}, f32[4,8,640]{2,1,0:T(8,128)S(1)}, u32[]{:S(2)}, u32[]{:S(2)}) collective-permute-start(f32[4,8,640]{2,1,0:T(8,128)S(1)} %get-tuple-element.43), channel_id=1, source_target_pairs={{0,240},{16,32},{32,16},{48,64},{64,48},{80,96},{96,80},{112,128},... | collective-permute-start | bytes 245768 | tf_op jit(solution)/shard_map/ppermute | solution.py:29
  76.5 0.0 collective-permute-done.4.xa
  76.5 2.7 %collective-permute-done.5.xb = f32[4,8,640]{2,1,0:T(8,128)S(1)} collective-permute-done((f32[4,8,640]{2,1,0:T(8,128)S(1)}, f32[4,8,640]{2,1,0:T(8,128)S(1)}, u32[]{:S(2)}, u32[]{:S(2)}) %collective-permute-start.5) | collective-permute-done | bytes 81952 | tf_op jit(solution)/shard_map/ppermute | solution.py:29
  79.2 0.0 collective-permute-done.7.yb
  79.2 0.0 collective-permute-done.6.ya
  79.2 0.7 second_step.1
  79.9 2.3 %collective-permute-start.11 = (f32[12,8,640]{2,1,0:T(8,128)S(1)}, f32[12,8,640]{2,1,0:T(8,128)S(1)}, u32[]{:S(2)}, u32[]{:S(2)}) collective-permute-start(f32[12,8,640]{2,1,0:T(8,128)S(1)} %get-tuple-element.44.cur.prev), channel_id=1, source_target_pairs={{0,14},{2,4},{4,2},{6,8},{8,6},{10,12},{12,10},{14,0},{1,15},{3,5}... | collective-permute-start | bytes 737288 | tf_op jit(solution)/shard_map/ppermute | solution.py:29
  82.3 3.0 %collective-permute-start.10 = (f32[12,8,640]{2,1,0:T(8,128)S(1)}, f32[12,8,640]{2,1,0:T(8,128)S(1)}, u32[]{:S(2)}, u32[]{:S(2)}) collective-permute-start(f32[12,8,640]{2,1,0:T(8,128)S(1)} %get-tuple-element.44.cur.prev), channel_id=1, source_target_pairs={{0,2},{2,0},{4,6},{6,4},{8,10},{10,8},{12,14},{14,12},{1,3},{3,1},... | collective-permute-start | bytes 737288 | tf_op jit(solution)/shard_map/ppermute | solution.py:29
  85.3 2.7 %collective-permute-start.8 = (f32[9,8,640]{2,1,0:T(8,128)S(1)}, f32[9,8,640]{2,1,0:T(8,128)S(1)}, u32[]{:S(2)}, u32[]{:S(2)}) collective-permute-start(f32[9,8,640]{2,1,0:T(8,128)S(1)} %get-tuple-element.45), channel_id=1, source_target_pairs={{0,16},{16,0},{32,48},{48,32},{64,80},{80,64},{96,112},{112,96},{1... | collective-permute-start | bytes 552968 | tf_op jit(solution)/shard_map/ppermute | solution.py:29
  88.0 4.0 %collective-permute-start.9 = (f32[9,8,640]{2,1,0:T(8,128)S(1)}, f32[9,8,640]{2,1,0:T(8,128)S(1)}, u32[]{:S(2)}, u32[]{:S(2)}) collective-permute-start(f32[9,8,640]{2,1,0:T(8,128)S(1)} %get-tuple-element.46), channel_id=1, source_target_pairs={{0,240},{16,32},{32,16},{48,64},{64,48},{80,96},{96,80},{112,128},... | collective-permute-start | bytes 552968 | tf_op jit(solution)/shard_map/ppermute | solution.py:29
  92.1 0.7 collective-permute-done.8.xa
  92.7 4.0 %collective-permute-done.9.xb = f32[9,8,640]{2,1,0:T(8,128)S(1)} collective-permute-done((f32[9,8,640]{2,1,0:T(8,128)S(1)}, f32[9,8,640]{2,1,0:T(8,128)S(1)}, u32[]{:S(2)}, u32[]{:S(2)}) %collective-permute-start.9) | collective-permute-done | bytes 184352 | tf_op jit(solution)/shard_map/ppermute | solution.py:29
  96.7 0.0 collective-permute-done.11.yb
  96.7 0.0 collective-permute-done.10.ya
  96.7 0.7 third_step.1
  97.4 3.7 %collective-permute-start.15 = (f32[12,8,640]{2,1,0:T(8,128)S(1)}, f32[12,8,640]{2,1,0:T(8,128)S(1)}, u32[]{:S(2)}, u32[]{:S(2)}) collective-permute-start(f32[12,8,640]{2,1,0:T(8,128)S(1)} %get-tuple-element.49.cur), channel_id=1, source_target_pairs={{0,14},{2,4},{4,2},{6,8},{8,6},{10,12},{12,10},{14,0},{1,15},{3,5}... | collective-permute-start | bytes 737288 | tf_op jit(solution)/shard_map/ppermute | solution.py:29
  101.2 2.0 %collective-permute-start.14 = (f32[12,8,640]{2,1,0:T(8,128)S(1)}, f32[12,8,640]{2,1,0:T(8,128)S(1)}, u32[]{:S(2)}, u32[]{:S(2)}) collective-permute-start(f32[12,8,640]{2,1,0:T(8,128)S(1)} %get-tuple-element.49.cur), channel_id=1, source_target_pairs={{0,2},{2,0},{4,6},{6,4},{8,10},{10,8},{12,14},{14,12},{1,3},{3,1},... | collective-permute-start | bytes 737288 | tf_op jit(solution)/shard_map/ppermute | solution.py:29
  103.1 2.0 %collective-permute-start.12 = (f32[9,8,640]{2,1,0:T(8,128)S(1)}, f32[9,8,640]{2,1,0:T(8,128)S(1)}, u32[]{:S(2)}, u32[]{:S(2)}) collective-permute-start(f32[9,8,640]{2,1,0:T(8,128)S(1)} %get-tuple-element.47), channel_id=1, source_target_pairs={{0,16},{16,0},{32,48},{48,32},{64,80},{80,64},{96,112},{112,96},{1... | collective-permute-start | bytes 552968 | tf_op jit(solution)/shard_map/ppermute | solution.py:29
  105.1 4.8 %collective-permute-start.13 = (f32[9,8,640]{2,1,0:T(8,128)S(1)}, f32[9,8,640]{2,1,0:T(8,128)S(1)}, u32[]{:S(2)}, u32[]{:S(2)}) collective-permute-start(f32[9,8,640]{2,1,0:T(8,128)S(1)} %get-tuple-element.48), channel_id=1, source_target_pairs={{0,240},{16,32},{32,16},{48,64},{64,48},{80,96},{96,80},{112,128},... | collective-permute-start | bytes 552968 | tf_op jit(solution)/shard_map/ppermute | solution.py:29
  109.9 0.7 collective-permute-done.12.xa.ma
  110.6 3.2 %collective-permute-done.13.xb.mb = f32[9,8,640]{2,1,0:T(8,128)S(1)} collective-permute-done((f32[9,8,640]{2,1,0:T(8,128)S(1)}, f32[9,8,640]{2,1,0:T(8,128)S(1)}, u32[]{:S(2)}, u32[]{:S(2)}) %collective-permute-start.13) | collective-permute-done | bytes 184352 | tf_op jit(solution)/shard_map/ppermute | solution.py:29
  113.8 0.0 collective-permute-done.15.yb
  113.8 0.0 collective-permute-done.14.ya
  113.8 0.7 fourth_step.1
  114.5 4.0 %collective-permute-start.16 = (f32[3,8,512]{2,1,0:T(8,128)S(1)}, f32[3,8,512]{2,1,0:T(8,128)S(1)}, u32[]{:S(2)}, u32[]{:S(2)}) collective-permute-start(f32[3,8,512]{2,1,0:T(8,128)S(1)} %get-tuple-element.54), channel_id=1, source_target_pairs={{0,2},{2,0},{4,6},{6,4},{8,10},{10,8},{12,14},{14,12},{1,3},{3,1},... | collective-permute-start | bytes 147464 | tf_op jit(solution)/shard_map/ppermute | solution.py:29
  118.5 3.4 %collective-permute-start.17 = (f32[3,8,512]{2,1,0:T(8,128)S(1)}, f32[3,8,512]{2,1,0:T(8,128)S(1)}, u32[]{:S(2)}, u32[]{:S(2)}) collective-permute-start(f32[3,8,512]{2,1,0:T(8,128)S(1)} %get-tuple-element.55), channel_id=1, source_target_pairs={{0,14},{2,4},{4,2},{6,8},{8,6},{10,12},{12,10},{14,0},{1,15},{3,5}... | collective-permute-start | bytes 147464 | tf_op jit(solution)/shard_map/ppermute | solution.py:29
  121.8 0.0 collective-permute-done.16.ya
  121.9 3.8 %collective-permute-done.17.yb = f32[3,8,512]{2,1,0:T(8,128)S(1)} collective-permute-done((f32[3,8,512]{2,1,0:T(8,128)S(1)}, f32[3,8,512]{2,1,0:T(8,128)S(1)}, u32[]{:S(2)}, u32[]{:S(2)}) %collective-permute-start.17) | collective-permute-done | bytes 49184 | tf_op jit(solution)/shard_map/ppermute | solution.py:29
  125.7 0.1 gather_edges.1
  125.7 2.7 %collective-permute-start.18 = (f32[14,8,640]{2,1,0:T(8,128)S(1)}, f32[14,8,640]{2,1,0:T(8,128)S(1)}, u32[]{:S(2)}, u32[]{:S(2)}) collective-permute-start(f32[14,8,640]{2,1,0:T(8,128)S(1)} %get-tuple-element.57), channel_id=1, source_target_pairs={{0,16},{16,0},{32,48},{48,32},{64,80},{80,64},{96,112},{112,96},{1... | collective-permute-start | bytes 860168 | tf_op jit(solution)/shard_map/ppermute | solution.py:29
  128.5 4.0 %collective-permute-start.19 = (f32[14,8,640]{2,1,0:T(8,128)S(1)}, f32[14,8,640]{2,1,0:T(8,128)S(1)}, u32[]{:S(2)}, u32[]{:S(2)}) collective-permute-start(f32[14,8,640]{2,1,0:T(8,128)S(1)} %get-tuple-element.58), channel_id=1, source_target_pairs={{0,240},{16,32},{32,16},{48,64},{64,48},{80,96},{96,80},{112,128},... | collective-permute-start | bytes 860168 | tf_op jit(solution)/shard_map/ppermute | solution.py:29
  132.5 4.0 %early.1 = (f32[16,12,4,512]{3,2,1,0:T(4,128)S(1)}, f32[12,4,512]{2,1,0:T(4,128)}, f32[12,4,512]{2,1,0:T(4,128)}) custom-call(f32[12,8,640]{2,1,0:T(8,128)S(1)} %get-tuple-element.44.cur.prev, f32[9,8,640]{2,1,0:T(8,128)S(1)} %collective-permute-done.8.xa, f32[9,8,640]{2,1,0:T(8,128)S(1)} %collective-permute-done.9.xb, ...), custom_call_target="tpu_custom_call" | custom-call | tf_op jit(solution)/shard_map/early/pallas_call | solution.py:62
  136.5 0.0 collective-permute-done.18.xa
  136.5 1.7 %collective-permute-done.19.xb = f32[14,8,640]{2,1,0:T(8,128)S(1)} collective-permute-done((f32[14,8,640]{2,1,0:T(8,128)S(1)}, f32[14,8,640]{2,1,0:T(8,128)S(1)}, u32[]{:S(2)}, u32[]{:S(2)}) %collective-permute-start.19) | collective-permute-done | bytes 286752 | tf_op jit(solution)/shard_map/ppermute | solution.py:29
  138.3 4.1 %filtered.1 = bf16[16,12,4,512]{3,2,1,0:T(4,128)(2,1)} custom-call(f32[16,12,4,512]{3,2,1,0:T(4,128)S(1)} %get-tuple-element.53.partial, f32[12,8,640]{2,1,0:T(8,128)S(1)} %get-tuple-element.50.last.cur, f32[12,8,512]{2,1,0:T(8,128)S(1)} %get-tuple-element.56.margins, f32[14,8,640]{2,1,0:T(8,128)S(1)} %collective-permute-done.18.xa, ...), custom_call_target="tpu_custom_call" | custom-call | tf_op jit(solution)/shard_map/filtered/pallas_call | solution.py:62
  (1 shorter events, 0.0 us)
Async XLA Ops:
  4.0 57.2 %collective-permute-start.3 = (f32[12,8,640]{2,1,0:T(8,128)S(1)}, f32[12,8,640]{2,1,0:T(8,128)S(1)}, u32[]{:S(2)}, u32[]{:S(2)}) collective-permute-start(f32[12,8,640]{2,1,0:T(8,128)S(1)} %get-tuple-element.33.cur.prev), channel_id=1, source_target_pairs={{0,14},{2,4},{4,2},{6,8},{8,6},{10,12},{12,10},{14,0},{1,15},{3,5}... | collective-permute-start | bytes 737288 | tf_op jit(solution)/shard_map/ppermute | solution.py:29
  9.7 51.5 %collective-permute-start.2 = (f32[12,8,640]{2,1,0:T(8,128)S(1)}, f32[12,8,640]{2,1,0:T(8,128)S(1)}, u32[]{:S(2)}, u32[]{:S(2)}) collective-permute-start(f32[12,8,640]{2,1,0:T(8,128)S(1)} %get-tuple-element.33.cur.prev), channel_id=1, source_target_pairs={{0,2},{2,0},{4,6},{6,4},{8,10},{10,8},{12,14},{14,12},{1,3},{3,1},... | collective-permute-start | bytes 737288 | tf_op jit(solution)/shard_map/ppermute | solution.py:29
  11.7 49.5 %collective-permute-start = (f32[4,8,640]{2,1,0:T(8,128)S(1)}, f32[4,8,640]{2,1,0:T(8,128)S(1)}, u32[]{:S(2)}, u32[]{:S(2)}) collective-permute-start(f32[4,8,640]{2,1,0:T(8,128)S(1)} %get-tuple-element.39), channel_id=1, source_target_pairs={{0,16},{16,0},{32,48},{48,32},{64,80},{80,64},{96,112},{112,96},{1... | collective-permute-start | bytes 245768 | tf_op jit(solution)/shard_map/ppermute | solution.py:29
  17.7 43.5 %collective-permute-start.1 = (f32[4,8,640]{2,1,0:T(8,128)S(1)}, f32[4,8,640]{2,1,0:T(8,128)S(1)}, u32[]{:S(2)}, u32[]{:S(2)}) collective-permute-start(f32[4,8,640]{2,1,0:T(8,128)S(1)} %get-tuple-element.40), channel_id=1, source_target_pairs={{0,240},{16,32},{32,16},{48,64},{64,48},{80,96},{96,80},{112,128},... | collective-permute-start | bytes 245768 | tf_op jit(solution)/shard_map/ppermute | solution.py:29
  57.7 0.7 copy-start
  58.3 0.7 copy-start.1
  61.9 17.3 %collective-permute-start.7 = (f32[12,8,640]{2,1,0:T(8,128)S(1)}, f32[12,8,640]{2,1,0:T(8,128)S(1)}, u32[]{:S(2)}, u32[]{:S(2)}) collective-permute-start(f32[12,8,640]{2,1,0:T(8,128)S(1)} %get-tuple-element.41.cur.prev), channel_id=1, source_target_pairs={{0,14},{2,4},{4,2},{6,8},{8,6},{10,12},{12,10},{14,0},{1,15},{3,5}... | collective-permute-start | bytes 737288 | tf_op jit(solution)/shard_map/ppermute | solution.py:29
  66.4 12.8 %collective-permute-start.6 = (f32[12,8,640]{2,1,0:T(8,128)S(1)}, f32[12,8,640]{2,1,0:T(8,128)S(1)}, u32[]{:S(2)}, u32[]{:S(2)}) collective-permute-start(f32[12,8,640]{2,1,0:T(8,128)S(1)} %get-tuple-element.41.cur.prev), channel_id=1, source_target_pairs={{0,2},{2,0},{4,6},{6,4},{8,10},{10,8},{12,14},{14,12},{1,3},{3,1},... | collective-permute-start | bytes 737288 | tf_op jit(solution)/shard_map/ppermute | solution.py:29
  69.7 6.8 %collective-permute-start.4 = (f32[4,8,640]{2,1,0:T(8,128)S(1)}, f32[4,8,640]{2,1,0:T(8,128)S(1)}, u32[]{:S(2)}, u32[]{:S(2)}) collective-permute-start(f32[4,8,640]{2,1,0:T(8,128)S(1)} %get-tuple-element.42), channel_id=1, source_target_pairs={{0,16},{16,0},{32,48},{48,32},{64,80},{80,64},{96,112},{112,96},{1... | collective-permute-start | bytes 245768 | tf_op jit(solution)/shard_map/ppermute | solution.py:29
  71.6 7.6 %collective-permute-start.5 = (f32[4,8,640]{2,1,0:T(8,128)S(1)}, f32[4,8,640]{2,1,0:T(8,128)S(1)}, u32[]{:S(2)}, u32[]{:S(2)}) collective-permute-start(f32[4,8,640]{2,1,0:T(8,128)S(1)} %get-tuple-element.43), channel_id=1, source_target_pairs={{0,240},{16,32},{32,16},{48,64},{64,48},{80,96},{96,80},{112,128},... | collective-permute-start | bytes 245768 | tf_op jit(solution)/shard_map/ppermute | solution.py:29
  79.9 16.8 %collective-permute-start.11 = (f32[12,8,640]{2,1,0:T(8,128)S(1)}, f32[12,8,640]{2,1,0:T(8,128)S(1)}, u32[]{:S(2)}, u32[]{:S(2)}) collective-permute-start(f32[12,8,640]{2,1,0:T(8,128)S(1)} %get-tuple-element.44.cur.prev), channel_id=1, source_target_pairs={{0,14},{2,4},{4,2},{6,8},{8,6},{10,12},{12,10},{14,0},{1,15},{3,5}... | collective-permute-start | bytes 737288 | tf_op jit(solution)/shard_map/ppermute | solution.py:29
  82.3 14.4 %collective-permute-start.10 = (f32[12,8,640]{2,1,0:T(8,128)S(1)}, f32[12,8,640]{2,1,0:T(8,128)S(1)}, u32[]{:S(2)}, u32[]{:S(2)}) collective-permute-start(f32[12,8,640]{2,1,0:T(8,128)S(1)} %get-tuple-element.44.cur.prev), channel_id=1, source_target_pairs={{0,2},{2,0},{4,6},{6,4},{8,10},{10,8},{12,14},{14,12},{1,3},{3,1},... | collective-permute-start | bytes 737288 | tf_op jit(solution)/shard_map/ppermute | solution.py:29
  85.3 7.5 %collective-permute-start.8 = (f32[9,8,640]{2,1,0:T(8,128)S(1)}, f32[9,8,640]{2,1,0:T(8,128)S(1)}, u32[]{:S(2)}, u32[]{:S(2)}) collective-permute-start(f32[9,8,640]{2,1,0:T(8,128)S(1)} %get-tuple-element.45), channel_id=1, source_target_pairs={{0,16},{16,0},{32,48},{48,32},{64,80},{80,64},{96,112},{112,96},{1... | collective-permute-start | bytes 552968 | tf_op jit(solution)/shard_map/ppermute | solution.py:29
  88.0 8.7 %collective-permute-start.9 = (f32[9,8,640]{2,1,0:T(8,128)S(1)}, f32[9,8,640]{2,1,0:T(8,128)S(1)}, u32[]{:S(2)}, u32[]{:S(2)}) collective-permute-start(f32[9,8,640]{2,1,0:T(8,128)S(1)} %get-tuple-element.46), channel_id=1, source_target_pairs={{0,240},{16,32},{32,16},{48,64},{64,48},{80,96},{96,80},{112,128},... | collective-permute-start | bytes 552968 | tf_op jit(solution)/shard_map/ppermute | solution.py:29
  97.4 16.3 %collective-permute-start.15 = (f32[12,8,640]{2,1,0:T(8,128)S(1)}, f32[12,8,640]{2,1,0:T(8,128)S(1)}, u32[]{:S(2)}, u32[]{:S(2)}) collective-permute-start(f32[12,8,640]{2,1,0:T(8,128)S(1)} %get-tuple-element.49.cur), channel_id=1, source_target_pairs={{0,14},{2,4},{4,2},{6,8},{8,6},{10,12},{12,10},{14,0},{1,15},{3,5}... | collective-permute-start | bytes 737288 | tf_op jit(solution)/shard_map/ppermute | solution.py:29
  101.2 12.6 %collective-permute-start.14 = (f32[12,8,640]{2,1,0:T(8,128)S(1)}, f32[12,8,640]{2,1,0:T(8,128)S(1)}, u32[]{:S(2)}, u32[]{:S(2)}) collective-permute-start(f32[12,8,640]{2,1,0:T(8,128)S(1)} %get-tuple-element.49.cur), channel_id=1, source_target_pairs={{0,2},{2,0},{4,6},{6,4},{8,10},{10,8},{12,14},{14,12},{1,3},{3,1},... | collective-permute-start | bytes 737288 | tf_op jit(solution)/shard_map/ppermute | solution.py:29
  103.1 7.5 %collective-permute-start.12 = (f32[9,8,640]{2,1,0:T(8,128)S(1)}, f32[9,8,640]{2,1,0:T(8,128)S(1)}, u32[]{:S(2)}, u32[]{:S(2)}) collective-permute-start(f32[9,8,640]{2,1,0:T(8,128)S(1)} %get-tuple-element.47), channel_id=1, source_target_pairs={{0,16},{16,0},{32,48},{48,32},{64,80},{80,64},{96,112},{112,96},{1... | collective-permute-start | bytes 552968 | tf_op jit(solution)/shard_map/ppermute | solution.py:29
  105.1 8.7 %collective-permute-start.13 = (f32[9,8,640]{2,1,0:T(8,128)S(1)}, f32[9,8,640]{2,1,0:T(8,128)S(1)}, u32[]{:S(2)}, u32[]{:S(2)}) collective-permute-start(f32[9,8,640]{2,1,0:T(8,128)S(1)} %get-tuple-element.48), channel_id=1, source_target_pairs={{0,240},{16,32},{32,16},{48,64},{64,48},{80,96},{96,80},{112,128},... | collective-permute-start | bytes 552968 | tf_op jit(solution)/shard_map/ppermute | solution.py:29
  114.5 7.4 %collective-permute-start.16 = (f32[3,8,512]{2,1,0:T(8,128)S(1)}, f32[3,8,512]{2,1,0:T(8,128)S(1)}, u32[]{:S(2)}, u32[]{:S(2)}) collective-permute-start(f32[3,8,512]{2,1,0:T(8,128)S(1)} %get-tuple-element.54), channel_id=1, source_target_pairs={{0,2},{2,0},{4,6},{6,4},{8,10},{10,8},{12,14},{14,12},{1,3},{3,1},... | collective-permute-start | bytes 147464 | tf_op jit(solution)/shard_map/ppermute | solution.py:29
  118.5 7.2 %collective-permute-start.17 = (f32[3,8,512]{2,1,0:T(8,128)S(1)}, f32[3,8,512]{2,1,0:T(8,128)S(1)}, u32[]{:S(2)}, u32[]{:S(2)}) collective-permute-start(f32[3,8,512]{2,1,0:T(8,128)S(1)} %get-tuple-element.55), channel_id=1, source_target_pairs={{0,14},{2,4},{4,2},{6,8},{8,6},{10,12},{12,10},{14,0},{1,15},{3,5}... | collective-permute-start | bytes 147464 | tf_op jit(solution)/shard_map/ppermute | solution.py:29
  125.7 10.8 %collective-permute-start.18 = (f32[14,8,640]{2,1,0:T(8,128)S(1)}, f32[14,8,640]{2,1,0:T(8,128)S(1)}, u32[]{:S(2)}, u32[]{:S(2)}) collective-permute-start(f32[14,8,640]{2,1,0:T(8,128)S(1)} %get-tuple-element.57), channel_id=1, source_target_pairs={{0,16},{16,0},{32,48},{48,32},{64,80},{80,64},{96,112},{112,96},{1... | collective-permute-start | bytes 860168 | tf_op jit(solution)/shard_map/ppermute | solution.py:29
  128.5 9.8 %collective-permute-start.19 = (f32[14,8,640]{2,1,0:T(8,128)S(1)}, f32[14,8,640]{2,1,0:T(8,128)S(1)}, u32[]{:S(2)}, u32[]{:S(2)}) collective-permute-start(f32[14,8,640]{2,1,0:T(8,128)S(1)} %get-tuple-element.58), channel_id=1, source_target_pairs={{0,240},{16,32},{32,16},{48,64},{64,48},{80,96},{96,80},{112,128},... | collective-permute-start | bytes 860168 | tf_op jit(solution)/shard_map/ppermute | solution.py:29

commit v5 on v4

--- a/solution.py
+++ b/solution.py
@@ -56,7 +56,7 @@
 
 def call(body, outs, *args, scratch=(), smem=(), far=(), far_outs=(), left=()):
     args = [
-        a if i in smem else pltpu.with_memory_space_constraint(a, pltpu.HBM if i in far else pltpu.VMEM)
+        pltpu.with_memory_space_constraint(a, pltpu.HBM if i in far else pltpu.VMEM)
         for i, a in enumerate(args)
     ]
     return pl.pallas_call(
@@ -293,14 +293,15 @@
     put_margins(lambda x, j: margins[x, :, chunk(j)], size_x, size_z // LANES, a_ref, b_ref, WIDE)
 
 
-def widen(get_margin, cur, xa, xb, ma, mb, m_at, first_ref, second_ref, first_z, second_z):
+def widen(get_margin, cur, xa, xb, ma, mb, m_at, both_ref, rim_ref, first, second, first_rim, second_rim):
     size_x = cur.shape[0]
-    size_z = first_ref.shape[2]
     _, odd, below, above = place("gx")
-    own = rows() < 4
+    row = rows()
     for x in range(-WIDE, size_x + WIDE):
         e = x + WIDE
-        for j in range(size_z // LANES):
+        for j in range(both_ref.shape[2] // LANES):
+            both_ref[e, :, chunk(j)] = around_x(x, chunk(j), cur, xa, xb)
+        for j in range(rim_ref.shape[2] // LANES):
             s = chunk(j)
             if 0 <= x < size_x:
                 edge = get_margin(x, s)
@@ -311,72 +312,91 @@
                 edge = kept(below, jnp.where(odd, near, far)) if x < 0 else kept(above, jnp.where(odd, far, near))
                 if other:
                     edge = pltpu.roll(edge, 6, axis=0)
-            both = around_x(x, s, cur, xa, xb)
-            first_ref[e, :, s] = jnp.where(own, both, pltpu.roll(edge, 4, axis=0))
-            second_ref[e, :, s] = jnp.where(own, pltpu.roll(both, 4, axis=0), edge)
-        beyond = around_x(x, slice(size_z, size_z + LANES), cur, xa, xb)
-        first_z[e] = beyond
-        second_z[e] = pltpu.roll(beyond, 4, axis=0)
-
-
-def laplace(first, second, first_z, second_z, lag, emit):
+            rim_ref[e, :, s] = jnp.where(
+                lax.rem(row, 4) == 3, pltpu.roll(edge, 3, axis=0), pltpu.roll(edge, 5, axis=0)
+            )
+    own = row < 4
+    for source, one, two in ((both_ref, first, second), (rim_ref, first_rim, second_rim)):
+        for e in range(size_x + 2 * WIDE):
+            for j in range(source.shape[2] // LANES):
+                s = chunk(j)
+                here = source[e, :, s]
+                turned = pltpu.roll(here, 4, axis=0)
+                if e >= HALF:
+                    one[e, :, s] = jnp.where(own, here, pltpu.roll(source[e - HALF, :, s], 4, axis=0))
+                if e + HALF < size_x + 2 * WIDE:
+                    two[e, :, s] = jnp.where(own, turned, source[e + HALF, :, s])
+
+
+def laplace(first, second, first_rim, second_rim, lag, emit):
     size_x = first.shape[0] - 2 * WIDE
-    count = first.shape[2] // LANES
+    count = first_rim.shape[2] // LANES
     core = lax.axis_index("gz") == 0
-    lane = lanes()
+    lane, row = lanes(), lax.rem(rows(), 4)
+
+    def product(one, two, x, j):
+        return one[x - lag + HALF + WIDE, :, chunk(j)] * two[x + lag - HALF + WIDE, :, chunk(j)]
 
     def image(x):
-        a, b = x - lag + HALF + WIDE, x + lag - HALF + WIDE
-        return [first[a, :, chunk(j)] * second[b, :, chunk(j)] for j in range(count)]
+        return [product(first, second, x, j) for j in range(count)]
 
     previous, here = image(-1), image(0)
     for x in range(size_x):
         following = image(x + 1)
-        beyond = first_z[x - lag + HALF + WIDE] * second_z[x + lag - HALF + WIDE]
+        beyond = product(first, second, x, count)
         before, after = kept(jnp.logical_not(core), beyond), kept(core, beyond)
         up = [pltpu.roll(v, LANES - 1, axis=1) for v in (*here, after)]
         down = [pltpu.roll(v, 1, axis=1) for v in (before, *here)]
         for j in range(count):
+            rim = product(first_rim, second_rim, x, j)
             along = jnp.where(lane < LANES - 1, up[j], up[j + 1]) + jnp.where(lane >= 1, down[j + 1], down[j])
-            across = pltpu.roll(here[j], 7, axis=0) + pltpu.roll(here[j], 1, axis=0)
+            across = jnp.where(row == 3, rim, pltpu.roll(here[j], 7, axis=0)) + jnp.where(
+                row == 0, rim, pltpu.roll(here[j], 1, axis=0)
+            )
             emit(x, chunk(j), 6.0 * here[j] - (previous[j] + following[j] + across + along))
         previous, here = here, following
 
 
-def early(cur, xa, xb, ya, yb, ma, mb, last, partial, source, receiver, *wide):
+def early(cur, xa, xb, ya, yb, ma, mb, last, partial, source, receiver, both, rim, *wide):
     row = rows()
     size_x, _, size_z = source.shape
     for x in range(size_x):
         source[x] = last[x, 0:4, :size_z]
         receiver[x] = last[x, 4:8, :size_z]
-    widen(lambda x, s: margin(ya, yb, x, s, row), cur, xa, xb, ma, mb, 4, *wide)
+    widen(lambda x, s: margin(ya, yb, x, s, row), cur, xa, xb, ma, mb, 4, both, rim, *wide)
 
     def each(lag, carry):
         def emit(x, s, value):
-            partial[lag, x, :, s] = value[0:4]
+            partial[lag, x, :, s] = value
 
         laplace(*wide, lag, emit)
         return carry
 
-    lax.fori_loop(0, LAGS, each, 0)
-
-
-def filtered(partial, cur, margins, xa, xb, out, held, done, *wide):
-    widen(lambda x, s: margins[x, :, s], cur, xa, xb, xa, xb, WIDE, *wide)
+    lax.fori_loop(0, HALF, each, 0)
+
+
+def filtered(partial, cur, margins, xa, xb, out, held, done, both, rim, *wide):
+    widen(lambda x, s: margins[x, :, s], cur, xa, xb, xa, xb, WIDE, both, rim, *wide)
+
+    def copy(lag):
+        return pltpu.make_async_copy(held.at[lag], out.at[lag], done.at[lag])
 
     def each(lag, carry):
         def emit(x, s, value):
-            held[lag, x, :, s] = (partial[lag, x, :, s] + value[0:4]).astype(jnp.bfloat16)
+            total = (partial[lag, x, :, s] + value).astype(jnp.bfloat16)
+            held[lag, x, :, s] = total[0:4]
+            held[lag + HALF, x, :, s] = total[4:8]
 
         laplace(*wide, lag, emit)
-        pltpu.make_async_copy(held.at[lag], out.at[lag], done.at[lag]).start()
+        copy(lag).start()
+        copy(lag + HALF).start()
         return carry
 
     def finish(lag, carry):
-        pltpu.make_async_copy(held.at[lag], out.at[lag], done.at[lag]).wait()
+        copy(lag).wait()
         return carry
 
-    lax.fori_loop(0, LAGS, each, 0)
+    lax.fori_loop(0, HALF, each, 0)
     lax.fori_loop(0, LAGS, finish, 0)
 
 
@@ -403,7 +423,7 @@
     def side(n, z=size_z):
         return ((n, 8, z), f32)
 
-    outer = side(wide_x), side(wide_x), side(wide_x, LANES), side(wide_x, LANES)
+    deep, flat = side(wide_x, deep_z), side(wide_x)
     now, old, medium, z = call(
         merge,
         [side(size_x), side(size_x), side(size_x), side(3 * size_x, LANES)],
@@ -420,7 +440,7 @@
         source_cell, wavelet, receiver_cells.T, traces, old, medium, beyond,
         scratch=[pltpu.VMEM((blocks, 8, LANES), jnp.int32), pltpu.VMEM((STEPS, blocks, 8, LANES), f32)],
         smem=(0, 1),
-        far=(2, 3),
+        far=range(4),
     )
     one, a, b = call(first_step, [tile, side(4, deep_z), side(4, deep_z)], now, prev, coef, inject, *halo0)
     halo1 = (*swap(a, b, "gx"), *swap(one, one, "gy"))
@@ -441,9 +461,9 @@
     )
     halo4 = swap(a, b, "gx")
     picture = (LAGS, size_x, size_y, size_z)
-    wide = [pltpu.VMEM(s, f32) for s, _ in outer]
+    wide = [pltpu.VMEM(s, f32) for s, _ in (deep, flat, deep, deep, flat, flat)]
     partial, source, receiver = call(
-        early, [(picture, f32), field, field], two, *halo2, halo3[0], halo3[1], four,
+        early, [((HALF, size_x, 8, size_z), f32), field, field], two, *halo2, halo3[0], halo3[1], four,
         scratch=wide,
         far_outs=(1, 2),
     )

time: 143 us -> 141 us (0.986)
  starting transfers between devices: 107 us -> 110 us
  Pallas kernels: 14.4 us -> 11.6 us
    ppermute x20, starting transfers between devices: 107 us -> 110 us  [swap(): return (lax.ppermute(a, axis, near), lax.ppermute(b, axis, far))]
    pallas_call x10, Pallas kernels: 14.4 us -> 11.6 us  [call(): pl.pallas_call(body, out_shape=[jax.ShapeDtypeStruct(s, d) if i in far_ou...]
  transfers between devices with their start and end apart: 20 -> 20, of which waited for: 7 -> 7; matrix products, arithmetic and copies ran while one was open for 0% -> 0% of each run, Pallas kernels for 4% -> 3%
where the time goes in v5:
time: 141 us; the launch traced here: 140 us
  starting transfers between devices  110 us (78%)
  waiting for transfers between devices  15.6 us (11%)
  Pallas kernels  11.6 us (8%)
  blocking collectives  2.07 us (1%)
    ppermute x20, starting transfers between devices, swap(): return (lax.ppermute(a, axis, near), lax.ppermute(b, axis, far))  110 us
    ppermute x20, waiting for transfers between devices, swap(): return (lax.ppermute(a, axis, near), lax.ppermute(b, axis, far))  15.6 us
    pallas_call x10, Pallas kernels, call(): pl.pallas_call(body, out_shape=[jax.ShapeDtypeStruct(s, d) if i in far_ou...  11.6 us
  transfers between devices with their start and end apart: 20, of which 7 were waited for; matrix products, arithmetic and copies ran while one was open for 0% of the time, Pallas kernels for 3%

profile of v5, /device:TPU:80, one launch (start us, length us, event | category | flops | bytes accessed | tf_op | source)
XLA Modules:
  0.0 140.0 jit_solution(3941991737875600073)
XLA Ops:
  0.6 1.2 merge.1
  1.9 2.1 %all-gather = f32[72,8,128]{2,1,0:T(8,128)S(1)} all-gather(f32[36,8,128]{2,1,0:T(8,128)S(1)} %get-tuple-element.32), channel_id=2, replica_groups=mesh['shot'=2,'gx'=16,'gy'=8,'gz'=2] {'gz'}, dimensions={0}, use_global_device_ids=true | all-gather | bytes 442368 | tf_op jit(solution)/shard_map/all_gather | solution.py:33
  4.0 5.8 %collective-permute-start.3 = (f32[12,8,640]{2,1,0:T(8,128)S(1)}, f32[12,8,640]{2,1,0:T(8,128)S(1)}, u32[]{:S(2)}, u32[]{:S(2)}) collective-permute-start(f32[12,8,640]{2,1,0:T(8,128)S(1)} %get-tuple-element.33.cur.prev), channel_id=1, source_target_pairs={{0,14},{2,4},{4,2},{6,8},{8,6},{10,12},{12,10},{14,0},{1,15},{3,5}... | collective-permute-start | bytes 737288 | tf_op jit(solution)/shard_map/ppermute | solution.py:29
  9.7 2.0 %collective-permute-start.2 = (f32[12,8,640]{2,1,0:T(8,128)S(1)}, f32[12,8,640]{2,1,0:T(8,128)S(1)}, u32[]{:S(2)}, u32[]{:S(2)}) collective-permute-start(f32[12,8,640]{2,1,0:T(8,128)S(1)} %get-tuple-element.33.cur.prev), channel_id=1, source_target_pairs={{0,2},{2,0},{4,6},{6,4},{8,10},{10,8},{12,14},{14,12},{1,3},{3,1},... | collective-permute-start | bytes 737288 | tf_op jit(solution)/shard_map/ppermute | solution.py:29
  11.7 6.0 %collective-permute-start = (f32[4,8,640]{2,1,0:T(8,128)S(1)}, f32[4,8,640]{2,1,0:T(8,128)S(1)}, u32[]{:S(2)}, u32[]{:S(2)}) collective-permute-start(f32[4,8,640]{2,1,0:T(8,128)S(1)} %get-tuple-element.39), channel_id=1, source_target_pairs={{0,16},{16,0},{32,48},{48,32},{64,80},{80,64},{96,112},{112,96},{1... | collective-permute-start | bytes 245768 | tf_op jit(solution)/shard_map/ppermute | solution.py:29
  17.7 39.9 %collective-permute-start.1 = (f32[4,8,640]{2,1,0:T(8,128)S(1)}, f32[4,8,640]{2,1,0:T(8,128)S(1)}, u32[]{:S(2)}, u32[]{:S(2)}) collective-permute-start(f32[4,8,640]{2,1,0:T(8,128)S(1)} %get-tuple-element.40), channel_id=1, source_target_pairs={{0,240},{16,32},{32,16},{48,64},{64,48},{80,96},{96,80},{112,128},... | collective-permute-start | bytes 245768 | tf_op jit(solution)/shard_map/ppermute | solution.py:29
  57.7 2.2 %prepare.1 = (f32[3,12,8,640]{3,2,1,0:T(8,128)S(1)}, f32[12,8,640]{2,1,0:T(8,128)S(1)}, f32[4,12,8,640]{3,2,1,0:T(8,128)S(1)}) custom-call(s32[3]{0:T(128)} %cell.1, f32[4]{0:T(128)} %wavelet.1, s32[2,2048]{1,0:T(2,128)} %bitcast.4, f32[4,2048]{1,0:T(4,128)} %traces.1, f32[12,8,512]{2,1,0:T(8,128)S(1)} %get-tuple-element.34.old, ...), custom_call_target="tpu_custom_call" | custom-call | tf_op jit(solution)/shard_map/prepare/pallas_call | solution.py:62
  59.9 0.0 collective-permute-done.xa
  59.9 0.3 collective-permute-done.1.xb
  60.1 0.0 collective-permute-done.3.yb
  60.1 0.0 collective-permute-done.2.ya
  60.1 0.7 first_step.1
  60.8 4.5 %collective-permute-start.7 = (f32[12,8,640]{2,1,0:T(8,128)S(1)}, f32[12,8,640]{2,1,0:T(8,128)S(1)}, u32[]{:S(2)}, u32[]{:S(2)}) collective-permute-start(f32[12,8,640]{2,1,0:T(8,128)S(1)} %get-tuple-element.41.cur.prev), channel_id=1, source_target_pairs={{0,14},{2,4},{4,2},{6,8},{8,6},{10,12},{12,10},{14,0},{1,15},{3,5}... | collective-permute-start | bytes 737288 | tf_op jit(solution)/shard_map/ppermute | solution.py:29
  65.3 3.2 %collective-permute-start.6 = (f32[12,8,640]{2,1,0:T(8,128)S(1)}, f32[12,8,640]{2,1,0:T(8,128)S(1)}, u32[]{:S(2)}, u32[]{:S(2)}) collective-permute-start(f32[12,8,640]{2,1,0:T(8,128)S(1)} %get-tuple-element.41.cur.prev), channel_id=1, source_target_pairs={{0,2},{2,0},{4,6},{6,4},{8,10},{10,8},{12,14},{14,12},{1,3},{3,1},... | collective-permute-start | bytes 737288 | tf_op jit(solution)/shard_map/ppermute | solution.py:29
  68.5 2.0 %collective-permute-start.4 = (f32[4,8,640]{2,1,0:T(8,128)S(1)}, f32[4,8,640]{2,1,0:T(8,128)S(1)}, u32[]{:S(2)}, u32[]{:S(2)}) collective-permute-start(f32[4,8,640]{2,1,0:T(8,128)S(1)} %get-tuple-element.42), channel_id=1, source_target_pairs={{0,16},{16,0},{32,48},{48,32},{64,80},{80,64},{96,112},{112,96},{1... | collective-permute-start | bytes 245768 | tf_op jit(solution)/shard_map/ppermute | solution.py:29
  70.5 6.0 %collective-permute-start.5 = (f32[4,8,640]{2,1,0:T(8,128)S(1)}, f32[4,8,640]{2,1,0:T(8,128)S(1)}, u32[]{:S(2)}, u32[]{:S(2)}) collective-permute-start(f32[4,8,640]{2,1,0:T(8,128)S(1)} %get-tuple-element.43), channel_id=1, source_target_pairs={{0,240},{16,32},{32,16},{48,64},{64,48},{80,96},{96,80},{112,128},... | collective-permute-start | bytes 245768 | tf_op jit(solution)/shard_map/ppermute | solution.py:29
  76.5 0.0 collective-permute-done.4.xa
  76.5 2.4 %collective-permute-done.5.xb = f32[4,8,640]{2,1,0:T(8,128)S(1)} collective-permute-done((f32[4,8,640]{2,1,0:T(8,128)S(1)}, f32[4,8,640]{2,1,0:T(8,128)S(1)}, u32[]{:S(2)}, u32[]{:S(2)}) %collective-permute-start.5) | collective-permute-done | bytes 81952 | tf_op jit(solution)/shard_map/ppermute | solution.py:29
  78.9 0.0 collective-permute-done.7.yb
  78.9 0.0 collective-permute-done.6.ya
  78.9 0.7 second_step.1
  79.6 2.3 %collective-permute-start.11 = (f32[12,8,640]{2,1,0:T(8,128)S(1)}, f32[12,8,640]{2,1,0:T(8,128)S(1)}, u32[]{:S(2)}, u32[]{:S(2)}) collective-permute-start(f32[12,8,640]{2,1,0:T(8,128)S(1)} %get-tuple-element.44.cur.prev), channel_id=1, source_target_pairs={{0,14},{2,4},{4,2},{6,8},{8,6},{10,12},{12,10},{14,0},{1,15},{3,5}... | collective-permute-start | bytes 737288 | tf_op jit(solution)/shard_map/ppermute | solution.py:29
  81.9 3.0 %collective-permute-start.10 = (f32[12,8,640]{2,1,0:T(8,128)S(1)}, f32[12,8,640]{2,1,0:T(8,128)S(1)}, u32[]{:S(2)}, u32[]{:S(2)}) collective-permute-start(f32[12,8,640]{2,1,0:T(8,128)S(1)} %get-tuple-element.44.cur.prev), channel_id=1, source_target_pairs={{0,2},{2,0},{4,6},{6,4},{8,10},{10,8},{12,14},{14,12},{1,3},{3,1},... | collective-permute-start | bytes 737288 | tf_op jit(solution)/shard_map/ppermute | solution.py:29
  84.9 2.0 %collective-permute-start.8 = (f32[9,8,640]{2,1,0:T(8,128)S(1)}, f32[9,8,640]{2,1,0:T(8,128)S(1)}, u32[]{:S(2)}, u32[]{:S(2)}) collective-permute-start(f32[9,8,640]{2,1,0:T(8,128)S(1)} %get-tuple-element.45), channel_id=1, source_target_pairs={{0,16},{16,0},{32,48},{48,32},{64,80},{80,64},{96,112},{112,96},{1... | collective-permute-start | bytes 552968 | tf_op jit(solution)/shard_map/ppermute | solution.py:29
  86.9 5.2 %collective-permute-start.9 = (f32[9,8,640]{2,1,0:T(8,128)S(1)}, f32[9,8,640]{2,1,0:T(8,128)S(1)}, u32[]{:S(2)}, u32[]{:S(2)}) collective-permute-start(f32[9,8,640]{2,1,0:T(8,128)S(1)} %get-tuple-element.46), channel_id=1, source_target_pairs={{0,240},{16,32},{32,16},{48,64},{64,48},{80,96},{96,80},{112,128},... | collective-permute-start | bytes 552968 | tf_op jit(solution)/shard_map/ppermute | solution.py:29
  92.1 0.3 collective-permute-done.8.xa
  92.4 3.2 %collective-permute-done.9.xb = f32[9,8,640]{2,1,0:T(8,128)S(1)} collective-permute-done((f32[9,8,640]{2,1,0:T(8,128)S(1)}, f32[9,8,640]{2,1,0:T(8,128)S(1)}, u32[]{:S(2)}, u32[]{:S(2)}) %collective-permute-start.9) | collective-permute-done | bytes 184352 | tf_op jit(solution)/shard_map/ppermute | solution.py:29
  95.6 0.0 collective-permute-done.11.yb
  95.6 0.0 collective-permute-done.10.ya
  95.6 0.7 third_step.1
  96.3 3.8 %collective-permute-start.15 = (f32[12,8,640]{2,1,0:T(8,128)S(1)}, f32[12,8,640]{2,1,0:T(8,128)S(1)}, u32[]{:S(2)}, u32[]{:S(2)}) collective-permute-start(f32[12,8,640]{2,1,0:T(8,128)S(1)} %get-tuple-element.49.cur), channel_id=1, source_target_pairs={{0,14},{2,4},{4,2},{6,8},{8,6},{10,12},{12,10},{14,0},{1,15},{3,5}... | collective-permute-start | bytes 737288 | tf_op jit(solution)/shard_map/ppermute | solution.py:29
  100.1 2.0 %collective-permute-start.14 = (f32[12,8,640]{2,1,0:T(8,128)S(1)}, f32[12,8,640]{2,1,0:T(8,128)S(1)}, u32[]{:S(2)}, u32[]{:S(2)}) collective-permute-start(f32[12,8,640]{2,1,0:T(8,128)S(1)} %get-tuple-element.49.cur), channel_id=1, source_target_pairs={{0,2},{2,0},{4,6},{6,4},{8,10},{10,8},{12,14},{14,12},{1,3},{3,1},... | collective-permute-start | bytes 737288 | tf_op jit(solution)/shard_map/ppermute | solution.py:29
  102.1 2.7 %collective-permute-start.12 = (f32[9,8,640]{2,1,0:T(8,128)S(1)}, f32[9,8,640]{2,1,0:T(8,128)S(1)}, u32[]{:S(2)}, u32[]{:S(2)}) collective-permute-start(f32[9,8,640]{2,1,0:T(8,128)S(1)} %get-tuple-element.47), channel_id=1, source_target_pairs={{0,16},{16,0},{32,48},{48,32},{64,80},{80,64},{96,112},{112,96},{1... | collective-permute-start | bytes 552968 | tf_op jit(solution)/shard_map/ppermute | solution.py:29
  104.8 5.2 %collective-permute-start.13 = (f32[9,8,640]{2,1,0:T(8,128)S(1)}, f32[9,8,640]{2,1,0:T(8,128)S(1)}, u32[]{:S(2)}, u32[]{:S(2)}) collective-permute-start(f32[9,8,640]{2,1,0:T(8,128)S(1)} %get-tuple-element.48), channel_id=1, source_target_pairs={{0,240},{16,32},{32,16},{48,64},{64,48},{80,96},{96,80},{112,128},... | collective-permute-start | bytes 552968 | tf_op jit(solution)/shard_map/ppermute | solution.py:29
  109.9 0.0 collective-permute-done.12.xa.ma
  109.9 3.5 %collective-permute-done.13.xb.mb = f32[9,8,640]{2,1,0:T(8,128)S(1)} collective-permute-done((f32[9,8,640]{2,1,0:T(8,128)S(1)}, f32[9,8,640]{2,1,0:T(8,128)S(1)}, u32[]{:S(2)}, u32[]{:S(2)}) %collective-permute-start.13) | collective-permute-done | bytes 184352 | tf_op jit(solution)/shard_map/ppermute | solution.py:29
  113.4 0.0 collective-permute-done.15.yb
  113.4 0.0 collective-permute-done.14.ya
  113.4 0.7 fourth_step.1
  114.2 4.0 %collective-permute-start.16 = (f32[3,8,512]{2,1,0:T(8,128)S(1)}, f32[3,8,512]{2,1,0:T(8,128)S(1)}, u32[]{:S(2)}, u32[]{:S(2)}) collective-permute-start(f32[3,8,512]{2,1,0:T(8,128)S(1)} %get-tuple-element.54), channel_id=1, source_target_pairs={{0,2},{2,0},{4,6},{6,4},{8,10},{10,8},{12,14},{14,12},{1,3},{3,1},... | collective-permute-start | bytes 147464 | tf_op jit(solution)/shard_map/ppermute | solution.py:29
  118.1 3.4 %collective-permute-start.17 = (f32[3,8,512]{2,1,0:T(8,128)S(1)}, f32[3,8,512]{2,1,0:T(8,128)S(1)}, u32[]{:S(2)}, u32[]{:S(2)}) collective-permute-start(f32[3,8,512]{2,1,0:T(8,128)S(1)} %get-tuple-element.55), channel_id=1, source_target_pairs={{0,14},{2,4},{4,2},{6,8},{8,6},{10,12},{12,10},{14,0},{1,15},{3,5}... | collective-permute-start | bytes 147464 | tf_op jit(solution)/shard_map/ppermute | solution.py:29
  121.5 0.0 collective-permute-done.16.ya
  121.5 3.8 %collective-permute-done.17.yb = f32[3,8,512]{2,1,0:T(8,128)S(1)} collective-permute-done((f32[3,8,512]{2,1,0:T(8,128)S(1)}, f32[3,8,512]{2,1,0:T(8,128)S(1)}, u32[]{:S(2)}, u32[]{:S(2)}) %collective-permute-start.17) | collective-permute-done | bytes 49184 | tf_op jit(solution)/shard_map/ppermute | solution.py:29
  125.3 0.1 gather_edges.1
  125.4 2.0 %collective-permute-start.18 = (f32[14,8,640]{2,1,0:T(8,128)S(1)}, f32[14,8,640]{2,1,0:T(8,128)S(1)}, u32[]{:S(2)}, u32[]{:S(2)}) collective-permute-start(f32[14,8,640]{2,1,0:T(8,128)S(1)} %get-tuple-element.57), channel_id=1, source_target_pairs={{0,16},{16,0},{32,48},{48,32},{64,80},{80,64},{96,112},{112,96},{1... | collective-permute-start | bytes 860168 | tf_op jit(solution)/shard_map/ppermute | solution.py:29
  127.4 5.1 %collective-permute-start.19 = (f32[14,8,640]{2,1,0:T(8,128)S(1)}, f32[14,8,640]{2,1,0:T(8,128)S(1)}, u32[]{:S(2)}, u32[]{:S(2)}) collective-permute-start(f32[14,8,640]{2,1,0:T(8,128)S(1)} %get-tuple-element.58), channel_id=1, source_target_pairs={{0,240},{16,32},{32,16},{48,64},{64,48},{80,96},{96,80},{112,128},... | collective-permute-start | bytes 860168 | tf_op jit(solution)/shard_map/ppermute | solution.py:29
  132.5 2.5 %early.1 = (f32[8,12,8,512]{3,2,1,0:T(8,128)S(1)}, f32[12,4,512]{2,1,0:T(4,128)}, f32[12,4,512]{2,1,0:T(4,128)}) custom-call(f32[12,8,640]{2,1,0:T(8,128)S(1)} %get-tuple-element.44.cur.prev, f32[9,8,640]{2,1,0:T(8,128)S(1)} %collective-permute-done.8.xa, f32[9,8,640]{2,1,0:T(8,128)S(1)} %collective-permute-done.9.xb, ...), custom_call_target="tpu_custom_call" | custom-call | tf_op jit(solution)/shard_map/early/pallas_call | solution.py:62
  135.1 0.0 collective-permute-done.18.xa
  135.1 2.1 %collective-permute-done.19.xb = f32[14,8,640]{2,1,0:T(8,128)S(1)} collective-permute-done((f32[14,8,640]{2,1,0:T(8,128)S(1)}, f32[14,8,640]{2,1,0:T(8,128)S(1)}, u32[]{:S(2)}, u32[]{:S(2)}) %collective-permute-start.19) | collective-permute-done | bytes 286752 | tf_op jit(solution)/shard_map/ppermute | solution.py:29
  137.2 2.8 %filtered.1 = bf16[16,12,4,512]{3,2,1,0:T(4,128)(2,1)} custom-call(f32[8,12,8,512]{3,2,1,0:T(8,128)S(1)} %get-tuple-element.53.partial, f32[12,8,640]{2,1,0:T(8,128)S(1)} %get-tuple-element.50.last.cur, f32[12,8,512]{2,1,0:T(8,128)S(1)} %get-tuple-element.56.margins, f32[14,8,640]{2,1,0:T(8,128)S(1)} %collective-permute-done.18.xa, ...), custom_call_target="tpu_custom_call" | custom-call | tf_op jit(solution)/shard_map/filtered/pallas_call | solution.py:62
  (1 shorter events, 0.0 us)
Async XLA Ops:
  4.0 56.2 %collective-permute-start.3 = (f32[12,8,640]{2,1,0:T(8,128)S(1)}, f32[12,8,640]{2,1,0:T(8,128)S(1)}, u32[]{:S(2)}, u32[]{:S(2)}) collective-permute-start(f32[12,8,640]{2,1,0:T(8,128)S(1)} %get-tuple-element.33.cur.prev), channel_id=1, source_target_pairs={{0,14},{2,4},{4,2},{6,8},{8,6},{10,12},{12,10},{14,0},{1,15},{3,5}... | collective-permute-start | bytes 737288 | tf_op jit(solution)/shard_map/ppermute | solution.py:29
  9.7 50.4 %collective-permute-start.2 = (f32[12,8,640]{2,1,0:T(8,128)S(1)}, f32[12,8,640]{2,1,0:T(8,128)S(1)}, u32[]{:S(2)}, u32[]{:S(2)}) collective-permute-start(f32[12,8,640]{2,1,0:T(8,128)S(1)} %get-tuple-element.33.cur.prev), channel_id=1, source_target_pairs={{0,2},{2,0},{4,6},{6,4},{8,10},{10,8},{12,14},{14,12},{1,3},{3,1},... | collective-permute-start | bytes 737288 | tf_op jit(solution)/shard_map/ppermute | solution.py:29
  11.7 48.2 %collective-permute-start = (f32[4,8,640]{2,1,0:T(8,128)S(1)}, f32[4,8,640]{2,1,0:T(8,128)S(1)}, u32[]{:S(2)}, u32[]{:S(2)}) collective-permute-start(f32[4,8,640]{2,1,0:T(8,128)S(1)} %get-tuple-element.39), channel_id=1, source_target_pairs={{0,16},{16,0},{32,48},{48,32},{64,80},{80,64},{96,112},{112,96},{1... | collective-permute-start | bytes 245768 | tf_op jit(solution)/shard_map/ppermute | solution.py:29
  17.7 42.4 %collective-permute-start.1 = (f32[4,8,640]{2,1,0:T(8,128)S(1)}, f32[4,8,640]{2,1,0:T(8,128)S(1)}, u32[]{:S(2)}, u32[]{:S(2)}) collective-permute-start(f32[4,8,640]{2,1,0:T(8,128)S(1)} %get-tuple-element.40), channel_id=1, source_target_pairs={{0,240},{16,32},{32,16},{48,64},{64,48},{80,96},{96,80},{112,128},... | collective-permute-start | bytes 245768 | tf_op jit(solution)/shard_map/ppermute | solution.py:29
  60.8 18.1 %collective-permute-start.7 = (f32[12,8,640]{2,1,0:T(8,128)S(1)}, f32[12,8,640]{2,1,0:T(8,128)S(1)}, u32[]{:S(2)}, u32[]{:S(2)}) collective-permute-start(f32[12,8,640]{2,1,0:T(8,128)S(1)} %get-tuple-element.41.cur.prev), channel_id=1, source_target_pairs={{0,14},{2,4},{4,2},{6,8},{8,6},{10,12},{12,10},{14,0},{1,15},{3,5}... | collective-permute-start | bytes 737288 | tf_op jit(solution)/shard_map/ppermute | solution.py:29
  65.3 13.6 %collective-permute-start.6 = (f32[12,8,640]{2,1,0:T(8,128)S(1)}, f32[12,8,640]{2,1,0:T(8,128)S(1)}, u32[]{:S(2)}, u32[]{:S(2)}) collective-permute-start(f32[12,8,640]{2,1,0:T(8,128)S(1)} %get-tuple-element.41.cur.prev), channel_id=1, source_target_pairs={{0,2},{2,0},{4,6},{6,4},{8,10},{10,8},{12,14},{14,12},{1,3},{3,1},... | collective-permute-start | bytes 737288 | tf_op jit(solution)/shard_map/ppermute | solution.py:29
  68.5 7.9 %collective-permute-start.4 = (f32[4,8,640]{2,1,0:T(8,128)S(1)}, f32[4,8,640]{2,1,0:T(8,128)S(1)}, u32[]{:S(2)}, u32[]{:S(2)}) collective-permute-start(f32[4,8,640]{2,1,0:T(8,128)S(1)} %get-tuple-element.42), channel_id=1, source_target_pairs={{0,16},{16,0},{32,48},{48,32},{64,80},{80,64},{96,112},{112,96},{1... | collective-permute-start | bytes 245768 | tf_op jit(solution)/shard_map/ppermute | solution.py:29
  70.5 8.4 %collective-permute-start.5 = (f32[4,8,640]{2,1,0:T(8,128)S(1)}, f32[4,8,640]{2,1,0:T(8,128)S(1)}, u32[]{:S(2)}, u32[]{:S(2)}) collective-permute-start(f32[4,8,640]{2,1,0:T(8,128)S(1)} %get-tuple-element.43), channel_id=1, source_target_pairs={{0,240},{16,32},{32,16},{48,64},{64,48},{80,96},{96,80},{112,128},... | collective-permute-start | bytes 245768 | tf_op jit(solution)/shard_map/ppermute | solution.py:29
  79.6 16.0 %collective-permute-start.11 = (f32[12,8,640]{2,1,0:T(8,128)S(1)}, f32[12,8,640]{2,1,0:T(8,128)S(1)}, u32[]{:S(2)}, u32[]{:S(2)}) collective-permute-start(f32[12,8,640]{2,1,0:T(8,128)S(1)} %get-tuple-element.44.cur.prev), channel_id=1, source_target_pairs={{0,14},{2,4},{4,2},{6,8},{8,6},{10,12},{12,10},{14,0},{1,15},{3,5}... | collective-permute-start | bytes 737288 | tf_op jit(solution)/shard_map/ppermute | solution.py:29
  81.9 13.6 %collective-permute-start.10 = (f32[12,8,640]{2,1,0:T(8,128)S(1)}, f32[12,8,640]{2,1,0:T(8,128)S(1)}, u32[]{:S(2)}, u32[]{:S(2)}) collective-permute-start(f32[12,8,640]{2,1,0:T(8,128)S(1)} %get-tuple-element.44.cur.prev), channel_id=1, source_target_pairs={{0,2},{2,0},{4,6},{6,4},{8,10},{10,8},{12,14},{14,12},{1,3},{3,1},... | collective-permute-start | bytes 737288 | tf_op jit(solution)/shard_map/ppermute | solution.py:29
  84.9 7.5 %collective-permute-start.8 = (f32[9,8,640]{2,1,0:T(8,128)S(1)}, f32[9,8,640]{2,1,0:T(8,128)S(1)}, u32[]{:S(2)}, u32[]{:S(2)}) collective-permute-start(f32[9,8,640]{2,1,0:T(8,128)S(1)} %get-tuple-element.45), channel_id=1, source_target_pairs={{0,16},{16,0},{32,48},{48,32},{64,80},{80,64},{96,112},{112,96},{1... | collective-permute-start | bytes 552968 | tf_op jit(solution)/shard_map/ppermute | solution.py:29
  86.9 8.7 %collective-permute-start.9 = (f32[9,8,640]{2,1,0:T(8,128)S(1)}, f32[9,8,640]{2,1,0:T(8,128)S(1)}, u32[]{:S(2)}, u32[]{:S(2)}) collective-permute-start(f32[9,8,640]{2,1,0:T(8,128)S(1)} %get-tuple-element.46), channel_id=1, source_target_pairs={{0,240},{16,32},{32,16},{48,64},{64,48},{80,96},{96,80},{112,128},... | collective-permute-start | bytes 552968 | tf_op jit(solution)/shard_map/ppermute | solution.py:29
  96.3 17.1 %collective-permute-start.15 = (f32[12,8,640]{2,1,0:T(8,128)S(1)}, f32[12,8,640]{2,1,0:T(8,128)S(1)}, u32[]{:S(2)}, u32[]{:S(2)}) collective-permute-start(f32[12,8,640]{2,1,0:T(8,128)S(1)} %get-tuple-element.49.cur), channel_id=1, source_target_pairs={{0,14},{2,4},{4,2},{6,8},{8,6},{10,12},{12,10},{14,0},{1,15},{3,5}... | collective-permute-start | bytes 737288 | tf_op jit(solution)/shard_map/ppermute | solution.py:29
  100.1 13.3 %collective-permute-start.14 = (f32[12,8,640]{2,1,0:T(8,128)S(1)}, f32[12,8,640]{2,1,0:T(8,128)S(1)}, u32[]{:S(2)}, u32[]{:S(2)}) collective-permute-start(f32[12,8,640]{2,1,0:T(8,128)S(1)} %get-tuple-element.49.cur), channel_id=1, source_target_pairs={{0,2},{2,0},{4,6},{6,4},{8,10},{10,8},{12,14},{14,12},{1,3},{3,1},... | collective-permute-start | bytes 737288 | tf_op jit(solution)/shard_map/ppermute | solution.py:29
  102.1 7.9 %collective-permute-start.12 = (f32[9,8,640]{2,1,0:T(8,128)S(1)}, f32[9,8,640]{2,1,0:T(8,128)S(1)}, u32[]{:S(2)}, u32[]{:S(2)}) collective-permute-start(f32[9,8,640]{2,1,0:T(8,128)S(1)} %get-tuple-element.47), channel_id=1, source_target_pairs={{0,16},{16,0},{32,48},{48,32},{64,80},{80,64},{96,112},{112,96},{1... | collective-permute-start | bytes 552968 | tf_op jit(solution)/shard_map/ppermute | solution.py:29
  104.8 8.7 %collective-permute-start.13 = (f32[9,8,640]{2,1,0:T(8,128)S(1)}, f32[9,8,640]{2,1,0:T(8,128)S(1)}, u32[]{:S(2)}, u32[]{:S(2)}) collective-permute-start(f32[9,8,640]{2,1,0:T(8,128)S(1)} %get-tuple-element.48), channel_id=1, source_target_pairs={{0,240},{16,32},{32,16},{48,64},{64,48},{80,96},{96,80},{112,128},... | collective-permute-start | bytes 552968 | tf_op jit(solution)/shard_map/ppermute | solution.py:29
  114.2 7.4 %collective-permute-start.16 = (f32[3,8,512]{2,1,0:T(8,128)S(1)}, f32[3,8,512]{2,1,0:T(8,128)S(1)}, u32[]{:S(2)}, u32[]{:S(2)}) collective-permute-start(f32[3,8,512]{2,1,0:T(8,128)S(1)} %get-tuple-element.54), channel_id=1, source_target_pairs={{0,2},{2,0},{4,6},{6,4},{8,10},{10,8},{12,14},{14,12},{1,3},{3,1},... | collective-permute-start | bytes 147464 | tf_op jit(solution)/shard_map/ppermute | solution.py:29
  118.1 7.2 %collective-permute-start.17 = (f32[3,8,512]{2,1,0:T(8,128)S(1)}, f32[3,8,512]{2,1,0:T(8,128)S(1)}, u32[]{:S(2)}, u32[]{:S(2)}) collective-permute-start(f32[3,8,512]{2,1,0:T(8,128)S(1)} %get-tuple-element.55), channel_id=1, source_target_pairs={{0,14},{2,4},{4,2},{6,8},{8,6},{10,12},{12,10},{14,0},{1,15},{3,5}... | collective-permute-start | bytes 147464 | tf_op jit(solution)/shard_map/ppermute | solution.py:29
  125.4 9.7 %collective-permute-start.18 = (f32[14,8,640]{2,1,0:T(8,128)S(1)}, f32[14,8,640]{2,1,0:T(8,128)S(1)}, u32[]{:S(2)}, u32[]{:S(2)}) collective-permute-start(f32[14,8,640]{2,1,0:T(8,128)S(1)} %get-tuple-element.57), channel_id=1, source_target_pairs={{0,16},{16,0},{32,48},{48,32},{64,80},{80,64},{96,112},{112,96},{1... | collective-permute-start | bytes 860168 | tf_op jit(solution)/shard_map/ppermute | solution.py:29
  127.4 9.8 %collective-permute-start.19 = (f32[14,8,640]{2,1,0:T(8,128)S(1)}, f32[14,8,640]{2,1,0:T(8,128)S(1)}, u32[]{:S(2)}, u32[]{:S(2)}) collective-permute-start(f32[14,8,640]{2,1,0:T(8,128)S(1)} %get-tuple-element.58), channel_id=1, source_target_pairs={{0,240},{16,32},{32,16},{48,64},{64,48},{80,96},{96,80},{112,128},... | collective-permute-start | bytes 860168 | tf_op jit(solution)/shard_map/ppermute | solution.py:29

commit v6 on v5

--- a/solution.py
+++ b/solution.py
@@ -20,7 +20,7 @@
 
 def pairs(size):
     near = [(i, i ^ 1) for i in range(size)]
-    far = [(i, (i + 1) % size if i % 2 else (i - 1) % size) for i in range(size)]
+    far = [(i, i + 1 if i % 2 else i - 1) for i in range(1, size - 1)]
     return near, far
 
 

time: 141 us -> 129 us (0.915)
  the two profiles are of different devices: /device:TPU:80 before, /device:TPU:326 now
where the time goes in v6:
time: 129 us; the launch traced here: 128 us
  starting transfers between devices  94.5 us (73%)
  waiting for transfers between devices  19 us (15%)
  Pallas kernels  11.6 us (9%)
  blocking collectives  2.07 us (2%)
    ppermute x20, starting transfers between devices, swap(): return (lax.ppermute(a, axis, near), lax.ppermute(b, axis, far))  94.5 us
    ppermute x20, waiting for transfers between devices, swap(): return (lax.ppermute(a, axis, near), lax.ppermute(b, axis, far))  19 us
    pallas_call x10, Pallas kernels, call(): pl.pallas_call(body, out_shape=[jax.ShapeDtypeStruct(s, d) if i in far_ou...  11.6 us
  transfers between devices with their start and end apart: 20, of which 10 were waited for; matrix products, arithmetic and copies ran while one was open for 0% of the time, Pallas kernels for 4%

profile of v6, /device:TPU:326, one launch (start us, length us, event | category | flops | bytes accessed | tf_op | source)
XLA Modules:
  0.0 128.0 jit_solution(15769004579413431019)
XLA Ops:
  0.6 1.2 merge.1
  1.9 2.1 %all-gather = f32[72,8,128]{2,1,0:T(8,128)S(1)} all-gather(f32[36,8,128]{2,1,0:T(8,128)S(1)} %get-tuple-element.32), channel_id=2, replica_groups=mesh['shot'=2,'gx'=16,'gy'=8,'gz'=2] {'gz'}, dimensions={0}, use_global_device_ids=true | all-gather | bytes 442368 | tf_op jit(solution)/shard_map/all_gather | solution.py:33
  4.0 4.8 %collective-permute-start.3 = (f32[12,8,640]{2,1,0:T(8,128)S(1)}, f32[12,8,640]{2,1,0:T(8,128)S(1)}, u32[]{:S(2)}, u32[]{:S(2)}) collective-permute-start(f32[12,8,640]{2,1,0:T(8,128)S(1)} %get-tuple-element.33.cur.prev), channel_id=1, source_target_pairs={{2,4},{4,2},{6,8},{8,6},{10,12},{12,10},{3,5},{5,3},{7,9},{9,7},{1... | collective-permute-start | bytes 737288 | tf_op jit(solution)/shard_map/ppermute | solution.py:29
  8.7 2.0 %collective-permute-start.2 = (f32[12,8,640]{2,1,0:T(8,128)S(1)}, f32[12,8,640]{2,1,0:T(8,128)S(1)}, u32[]{:S(2)}, u32[]{:S(2)}) collective-permute-start(f32[12,8,640]{2,1,0:T(8,128)S(1)} %get-tuple-element.33.cur.prev), channel_id=1, source_target_pairs={{0,2},{2,0},{4,6},{6,4},{8,10},{10,8},{12,14},{14,12},{1,3},{3,1},... | collective-permute-start | bytes 737288 | tf_op jit(solution)/shard_map/ppermute | solution.py:29
  10.7 2.0 %collective-permute-start = (f32[4,8,640]{2,1,0:T(8,128)S(1)}, f32[4,8,640]{2,1,0:T(8,128)S(1)}, u32[]{:S(2)}, u32[]{:S(2)}) collective-permute-start(f32[4,8,640]{2,1,0:T(8,128)S(1)} %get-tuple-element.39), channel_id=1, source_target_pairs={{0,16},{16,0},{32,48},{48,32},{64,80},{80,64},{96,112},{112,96},{1... | collective-permute-start | bytes 245768 | tf_op jit(solution)/shard_map/ppermute | solution.py:29
  12.7 10.1 %collective-permute-start.1 = (f32[4,8,640]{2,1,0:T(8,128)S(1)}, f32[4,8,640]{2,1,0:T(8,128)S(1)}, u32[]{:S(2)}, u32[]{:S(2)}) collective-permute-start(f32[4,8,640]{2,1,0:T(8,128)S(1)} %get-tuple-element.40), channel_id=1, source_target_pairs={{16,32},{32,16},{48,64},{64,48},{80,96},{96,80},{112,128},{128,112... | collective-permute-start | bytes 245768 | tf_op jit(solution)/shard_map/ppermute | solution.py:29
  22.8 2.2 %prepare.1 = (f32[3,12,8,640]{3,2,1,0:T(8,128)S(1)}, f32[12,8,640]{2,1,0:T(8,128)S(1)}, f32[4,12,8,640]{3,2,1,0:T(8,128)S(1)}) custom-call(s32[3]{0:T(128)} %cell.1, f32[4]{0:T(128)} %wavelet.1, s32[2,2048]{1,0:T(2,128)} %bitcast.4, f32[4,2048]{1,0:T(4,128)} %traces.1, f32[12,8,512]{2,1,0:T(8,128)S(1)} %get-tuple-element.34.old, ...), custom_call_target="tpu_custom_call" | custom-call | tf_op jit(solution)/shard_map/prepare/pallas_call | solution.py:62
  25.0 0.0 collective-permute-done.xa
  25.0 0.2 collective-permute-done.1.xb
  25.2 0.0 collective-permute-done.3.yb
  25.2 0.0 collective-permute-done.2.ya
  25.2 0.7 first_step.1
  25.9 3.4 %collective-permute-start.7 = (f32[12,8,640]{2,1,0:T(8,128)S(1)}, f32[12,8,640]{2,1,0:T(8,128)S(1)}, u32[]{:S(2)}, u32[]{:S(2)}) collective-permute-start(f32[12,8,640]{2,1,0:T(8,128)S(1)} %get-tuple-element.41.cur.prev), channel_id=1, source_target_pairs={{2,4},{4,2},{6,8},{8,6},{10,12},{12,10},{3,5},{5,3},{7,9},{9,7},{1... | collective-permute-start | bytes 737288 | tf_op jit(solution)/shard_map/ppermute | solution.py:29
  29.3 29.4 %collective-permute-start.6 = (f32[12,8,640]{2,1,0:T(8,128)S(1)}, f32[12,8,640]{2,1,0:T(8,128)S(1)}, u32[]{:S(2)}, u32[]{:S(2)}) collective-permute-start(f32[12,8,640]{2,1,0:T(8,128)S(1)} %get-tuple-element.41.cur.prev), channel_id=1, source_target_pairs={{0,2},{2,0},{4,6},{6,4},{8,10},{10,8},{12,14},{14,12},{1,3},{3,1},... | collective-permute-start | bytes 737288 | tf_op jit(solution)/shard_map/ppermute | solution.py:29
  58.6 2.0 %collective-permute-start.4 = (f32[4,8,640]{2,1,0:T(8,128)S(1)}, f32[4,8,640]{2,1,0:T(8,128)S(1)}, u32[]{:S(2)}, u32[]{:S(2)}) collective-permute-start(f32[4,8,640]{2,1,0:T(8,128)S(1)} %get-tuple-element.42), channel_id=1, source_target_pairs={{0,16},{16,0},{32,48},{48,32},{64,80},{80,64},{96,112},{112,96},{1... | collective-permute-start | bytes 245768 | tf_op jit(solution)/shard_map/ppermute | solution.py:29
  60.6 2.0 %collective-permute-start.5 = (f32[4,8,640]{2,1,0:T(8,128)S(1)}, f32[4,8,640]{2,1,0:T(8,128)S(1)}, u32[]{:S(2)}, u32[]{:S(2)}) collective-permute-start(f32[4,8,640]{2,1,0:T(8,128)S(1)} %get-tuple-element.43), channel_id=1, source_target_pairs={{16,32},{32,16},{48,64},{64,48},{80,96},{96,80},{112,128},{128,112... | collective-permute-start | bytes 245768 | tf_op jit(solution)/shard_map/ppermute | solution.py:29
  62.5 2.4 %collective-permute-done.4.xa = f32[4,8,640]{2,1,0:T(8,128)S(1)} collective-permute-done((f32[4,8,640]{2,1,0:T(8,128)S(1)}, f32[4,8,640]{2,1,0:T(8,128)S(1)}, u32[]{:S(2)}, u32[]{:S(2)}) %collective-permute-start.4) | collective-permute-done | bytes 81952 | tf_op jit(solution)/shard_map/ppermute | solution.py:29
  65.0 2.0 %collective-permute-done.5.xb = f32[4,8,640]{2,1,0:T(8,128)S(1)} collective-permute-done((f32[4,8,640]{2,1,0:T(8,128)S(1)}, f32[4,8,640]{2,1,0:T(8,128)S(1)}, u32[]{:S(2)}, u32[]{:S(2)}) %collective-permute-start.5) | collective-permute-done | bytes 81952 | tf_op jit(solution)/shard_map/ppermute | solution.py:29
  66.9 0.0 collective-permute-done.7.yb
  67.0 0.0 collective-permute-done.6.ya
  67.0 0.7 second_step.1
  67.7 2.0 %collective-permute-start.11 = (f32[12,8,640]{2,1,0:T(8,128)S(1)}, f32[12,8,640]{2,1,0:T(8,128)S(1)}, u32[]{:S(2)}, u32[]{:S(2)}) collective-permute-start(f32[12,8,640]{2,1,0:T(8,128)S(1)} %get-tuple-element.44.cur.prev), channel_id=1, source_target_pairs={{2,4},{4,2},{6,8},{8,6},{10,12},{12,10},{3,5},{5,3},{7,9},{9,7},{1... | collective-permute-start | bytes 737288 | tf_op jit(solution)/shard_map/ppermute | solution.py:29
  69.6 2.0 %collective-permute-start.10 = (f32[12,8,640]{2,1,0:T(8,128)S(1)}, f32[12,8,640]{2,1,0:T(8,128)S(1)}, u32[]{:S(2)}, u32[]{:S(2)}) collective-permute-start(f32[12,8,640]{2,1,0:T(8,128)S(1)} %get-tuple-element.44.cur.prev), channel_id=1, source_target_pairs={{0,2},{2,0},{4,6},{6,4},{8,10},{10,8},{12,14},{14,12},{1,3},{3,1},... | collective-permute-start | bytes 737288 | tf_op jit(solution)/shard_map/ppermute | solution.py:29
  71.6 2.0 %collective-permute-start.8 = (f32[9,8,640]{2,1,0:T(8,128)S(1)}, f32[9,8,640]{2,1,0:T(8,128)S(1)}, u32[]{:S(2)}, u32[]{:S(2)}) collective-permute-start(f32[9,8,640]{2,1,0:T(8,128)S(1)} %get-tuple-element.45), channel_id=1, source_target_pairs={{0,16},{16,0},{32,48},{48,32},{64,80},{80,64},{96,112},{112,96},{1... | collective-permute-start | bytes 552968 | tf_op jit(solution)/shard_map/ppermute | solution.py:29
  73.5 5.2 %collective-permute-start.9 = (f32[9,8,640]{2,1,0:T(8,128)S(1)}, f32[9,8,640]{2,1,0:T(8,128)S(1)}, u32[]{:S(2)}, u32[]{:S(2)}) collective-permute-start(f32[9,8,640]{2,1,0:T(8,128)S(1)} %get-tuple-element.46), channel_id=1, source_target_pairs={{16,32},{32,16},{48,64},{64,48},{80,96},{96,80},{112,128},{128,112... | collective-permute-start | bytes 552968 | tf_op jit(solution)/shard_map/ppermute | solution.py:29
  78.7 0.3 collective-permute-done.8.xa
  79.0 3.2 %collective-permute-done.9.xb = f32[9,8,640]{2,1,0:T(8,128)S(1)} collective-permute-done((f32[9,8,640]{2,1,0:T(8,128)S(1)}, f32[9,8,640]{2,1,0:T(8,128)S(1)}, u32[]{:S(2)}, u32[]{:S(2)}) %collective-permute-start.9) | collective-permute-done | bytes 184352 | tf_op jit(solution)/shard_map/ppermute | solution.py:29
  82.2 0.0 collective-permute-done.11.yb
  82.2 0.0 collective-permute-done.10.ya
  82.2 0.7 third_step.1
  82.9 5.2 %collective-permute-start.15 = (f32[12,8,640]{2,1,0:T(8,128)S(1)}, f32[12,8,640]{2,1,0:T(8,128)S(1)}, u32[]{:S(2)}, u32[]{:S(2)}) collective-permute-start(f32[12,8,640]{2,1,0:T(8,128)S(1)} %get-tuple-element.49.cur), channel_id=1, source_target_pairs={{2,4},{4,2},{6,8},{8,6},{10,12},{12,10},{3,5},{5,3},{7,9},{9,7},{1... | collective-permute-start | bytes 737288 | tf_op jit(solution)/shard_map/ppermute | solution.py:29
  88.1 2.0 %collective-permute-start.14 = (f32[12,8,640]{2,1,0:T(8,128)S(1)}, f32[12,8,640]{2,1,0:T(8,128)S(1)}, u32[]{:S(2)}, u32[]{:S(2)}) collective-permute-start(f32[12,8,640]{2,1,0:T(8,128)S(1)} %get-tuple-element.49.cur), channel_id=1, source_target_pairs={{0,2},{2,0},{4,6},{6,4},{8,10},{10,8},{12,14},{14,12},{1,3},{3,1},... | collective-permute-start | bytes 737288 | tf_op jit(solution)/shard_map/ppermute | solution.py:29
  90.1 2.0 %collective-permute-start.12 = (f32[9,8,640]{2,1,0:T(8,128)S(1)}, f32[9,8,640]{2,1,0:T(8,128)S(1)}, u32[]{:S(2)}, u32[]{:S(2)}) collective-permute-start(f32[9,8,640]{2,1,0:T(8,128)S(1)} %get-tuple-element.47), channel_id=1, source_target_pairs={{0,16},{16,0},{32,48},{48,32},{64,80},{80,64},{96,112},{112,96},{1... | collective-permute-start | bytes 552968 | tf_op jit(solution)/shard_map/ppermute | solution.py:29
  92.0 5.2 %collective-permute-start.13 = (f32[9,8,640]{2,1,0:T(8,128)S(1)}, f32[9,8,640]{2,1,0:T(8,128)S(1)}, u32[]{:S(2)}, u32[]{:S(2)}) collective-permute-start(f32[9,8,640]{2,1,0:T(8,128)S(1)} %get-tuple-element.48), channel_id=1, source_target_pairs={{16,32},{32,16},{48,64},{64,48},{80,96},{96,80},{112,128},{128,112... | collective-permute-start | bytes 552968 | tf_op jit(solution)/shard_map/ppermute | solution.py:29
  97.2 0.3 collective-permute-done.12.xa.ma
  97.5 3.2 %collective-permute-done.13.xb.mb = f32[9,8,640]{2,1,0:T(8,128)S(1)} collective-permute-done((f32[9,8,640]{2,1,0:T(8,128)S(1)}, f32[9,8,640]{2,1,0:T(8,128)S(1)}, u32[]{:S(2)}, u32[]{:S(2)}) %collective-permute-start.13) | collective-permute-done | bytes 184352 | tf_op jit(solution)/shard_map/ppermute | solution.py:29
  100.7 0.0 collective-permute-done.15.yb
  100.7 0.0 collective-permute-done.14.ya
  100.7 0.7 fourth_step.1
  101.4 4.0 %collective-permute-start.16 = (f32[3,8,512]{2,1,0:T(8,128)S(1)}, f32[3,8,512]{2,1,0:T(8,128)S(1)}, u32[]{:S(2)}, u32[]{:S(2)}) collective-permute-start(f32[3,8,512]{2,1,0:T(8,128)S(1)} %get-tuple-element.54), channel_id=1, source_target_pairs={{0,2},{2,0},{4,6},{6,4},{8,10},{10,8},{12,14},{14,12},{1,3},{3,1},... | collective-permute-start | bytes 147464 | tf_op jit(solution)/shard_map/ppermute | solution.py:29
  105.4 2.0 %collective-permute-start.17 = (f32[3,8,512]{2,1,0:T(8,128)S(1)}, f32[3,8,512]{2,1,0:T(8,128)S(1)}, u32[]{:S(2)}, u32[]{:S(2)}) collective-permute-start(f32[3,8,512]{2,1,0:T(8,128)S(1)} %get-tuple-element.55), channel_id=1, source_target_pairs={{2,4},{4,2},{6,8},{8,6},{10,12},{12,10},{3,5},{5,3},{7,9},{9,7},{1... | collective-permute-start | bytes 147464 | tf_op jit(solution)/shard_map/ppermute | solution.py:29
  107.4 0.1 collective-permute-done.16.ya
  107.5 5.2 %collective-permute-done.17.yb = f32[3,8,512]{2,1,0:T(8,128)S(1)} collective-permute-done((f32[3,8,512]{2,1,0:T(8,128)S(1)}, f32[3,8,512]{2,1,0:T(8,128)S(1)}, u32[]{:S(2)}, u32[]{:S(2)}) %collective-permute-start.17) | collective-permute-done | bytes 49184 | tf_op jit(solution)/shard_map/ppermute | solution.py:29
  112.6 0.1 gather_edges.1
  112.7 2.0 %collective-permute-start.18 = (f32[14,8,640]{2,1,0:T(8,128)S(1)}, f32[14,8,640]{2,1,0:T(8,128)S(1)}, u32[]{:S(2)}, u32[]{:S(2)}) collective-permute-start(f32[14,8,640]{2,1,0:T(8,128)S(1)} %get-tuple-element.57), channel_id=1, source_target_pairs={{0,16},{16,0},{32,48},{48,32},{64,80},{80,64},{96,112},{112,96},{1... | collective-permute-start | bytes 860168 | tf_op jit(solution)/shard_map/ppermute | solution.py:29
  114.7 6.0 %collective-permute-start.19 = (f32[14,8,640]{2,1,0:T(8,128)S(1)}, f32[14,8,640]{2,1,0:T(8,128)S(1)}, u32[]{:S(2)}, u32[]{:S(2)}) collective-permute-start(f32[14,8,640]{2,1,0:T(8,128)S(1)} %get-tuple-element.58), channel_id=1, source_target_pairs={{16,32},{32,16},{48,64},{64,48},{80,96},{96,80},{112,128},{128,112... | collective-permute-start | bytes 860168 | tf_op jit(solution)/shard_map/ppermute | solution.py:29
  120.6 2.5 %early.1 = (f32[8,12,8,512]{3,2,1,0:T(8,128)S(1)}, f32[12,4,512]{2,1,0:T(4,128)}, f32[12,4,512]{2,1,0:T(4,128)}) custom-call(f32[12,8,640]{2,1,0:T(8,128)S(1)} %get-tuple-element.44.cur.prev, f32[9,8,640]{2,1,0:T(8,128)S(1)} %collective-permute-done.8.xa, f32[9,8,640]{2,1,0:T(8,128)S(1)} %collective-permute-done.9.xb, ...), custom_call_target="tpu_custom_call" | custom-call | tf_op jit(solution)/shard_map/early/pallas_call | solution.py:62
  123.2 0.0 collective-permute-done.18.xa
  123.2 2.0 %collective-permute-done.19.xb = f32[14,8,640]{2,1,0:T(8,128)S(1)} collective-permute-done((f32[14,8,640]{2,1,0:T(8,128)S(1)}, f32[14,8,640]{2,1,0:T(8,128)S(1)}, u32[]{:S(2)}, u32[]{:S(2)}) %collective-permute-start.19) | collective-permute-done | bytes 286752 | tf_op jit(solution)/shard_map/ppermute | solution.py:29
  125.2 2.8 %filtered.1 = bf16[16,12,4,512]{3,2,1,0:T(4,128)(2,1)} custom-call(f32[8,12,8,512]{3,2,1,0:T(8,128)S(1)} %get-tuple-element.53.partial, f32[12,8,640]{2,1,0:T(8,128)S(1)} %get-tuple-element.50.last.cur, f32[12,8,512]{2,1,0:T(8,128)S(1)} %get-tuple-element.56.margins, f32[14,8,640]{2,1,0:T(8,128)S(1)} %collective-permute-done.18.xa, ...), custom_call_target="tpu_custom_call" | custom-call | tf_op jit(solution)/shard_map/filtered/pallas_call | solution.py:62
  (1 shorter events, 0.0 us)
Async XLA Ops:
  4.0 21.2 %collective-permute-start.3 = (f32[12,8,640]{2,1,0:T(8,128)S(1)}, f32[12,8,640]{2,1,0:T(8,128)S(1)}, u32[]{:S(2)}, u32[]{:S(2)}) collective-permute-start(f32[12,8,640]{2,1,0:T(8,128)S(1)} %get-tuple-element.33.cur.prev), channel_id=1, source_target_pairs={{2,4},{4,2},{6,8},{8,6},{10,12},{12,10},{3,5},{5,3},{7,9},{9,7},{1... | collective-permute-start | bytes 737288 | tf_op jit(solution)/shard_map/ppermute | solution.py:29
  8.7 16.4 %collective-permute-start.2 = (f32[12,8,640]{2,1,0:T(8,128)S(1)}, f32[12,8,640]{2,1,0:T(8,128)S(1)}, u32[]{:S(2)}, u32[]{:S(2)}) collective-permute-start(f32[12,8,640]{2,1,0:T(8,128)S(1)} %get-tuple-element.33.cur.prev), channel_id=1, source_target_pairs={{0,2},{2,0},{4,6},{6,4},{8,10},{10,8},{12,14},{14,12},{1,3},{3,1},... | collective-permute-start | bytes 737288 | tf_op jit(solution)/shard_map/ppermute | solution.py:29
  10.7 14.3 %collective-permute-start = (f32[4,8,640]{2,1,0:T(8,128)S(1)}, f32[4,8,640]{2,1,0:T(8,128)S(1)}, u32[]{:S(2)}, u32[]{:S(2)}) collective-permute-start(f32[4,8,640]{2,1,0:T(8,128)S(1)} %get-tuple-element.39), channel_id=1, source_target_pairs={{0,16},{16,0},{32,48},{48,32},{64,80},{80,64},{96,112},{112,96},{1... | collective-permute-start | bytes 245768 | tf_op jit(solution)/shard_map/ppermute | solution.py:29
  12.7 12.5 %collective-permute-start.1 = (f32[4,8,640]{2,1,0:T(8,128)S(1)}, f32[4,8,640]{2,1,0:T(8,128)S(1)}, u32[]{:S(2)}, u32[]{:S(2)}) collective-permute-start(f32[4,8,640]{2,1,0:T(8,128)S(1)} %get-tuple-element.40), channel_id=1, source_target_pairs={{16,32},{32,16},{48,64},{64,48},{80,96},{96,80},{112,128},{128,112... | collective-permute-start | bytes 245768 | tf_op jit(solution)/shard_map/ppermute | solution.py:29
  25.9 41.1 %collective-permute-start.7 = (f32[12,8,640]{2,1,0:T(8,128)S(1)}, f32[12,8,640]{2,1,0:T(8,128)S(1)}, u32[]{:S(2)}, u32[]{:S(2)}) collective-permute-start(f32[12,8,640]{2,1,0:T(8,128)S(1)} %get-tuple-element.41.cur.prev), channel_id=1, source_target_pairs={{2,4},{4,2},{6,8},{8,6},{10,12},{12,10},{3,5},{5,3},{7,9},{9,7},{1... | collective-permute-start | bytes 737288 | tf_op jit(solution)/shard_map/ppermute | solution.py:29
  29.3 37.7 %collective-permute-start.6 = (f32[12,8,640]{2,1,0:T(8,128)S(1)}, f32[12,8,640]{2,1,0:T(8,128)S(1)}, u32[]{:S(2)}, u32[]{:S(2)}) collective-permute-start(f32[12,8,640]{2,1,0:T(8,128)S(1)} %get-tuple-element.41.cur.prev), channel_id=1, source_target_pairs={{0,2},{2,0},{4,6},{6,4},{8,10},{10,8},{12,14},{14,12},{1,3},{3,1},... | collective-permute-start | bytes 737288 | tf_op jit(solution)/shard_map/ppermute | solution.py:29
  58.6 6.4 %collective-permute-start.4 = (f32[4,8,640]{2,1,0:T(8,128)S(1)}, f32[4,8,640]{2,1,0:T(8,128)S(1)}, u32[]{:S(2)}, u32[]{:S(2)}) collective-permute-start(f32[4,8,640]{2,1,0:T(8,128)S(1)} %get-tuple-element.42), channel_id=1, source_target_pairs={{0,16},{16,0},{32,48},{48,32},{64,80},{80,64},{96,112},{112,96},{1... | collective-permute-start | bytes 245768 | tf_op jit(solution)/shard_map/ppermute | solution.py:29
  60.6 6.4 %collective-permute-start.5 = (f32[4,8,640]{2,1,0:T(8,128)S(1)}, f32[4,8,640]{2,1,0:T(8,128)S(1)}, u32[]{:S(2)}, u32[]{:S(2)}) collective-permute-start(f32[4,8,640]{2,1,0:T(8,128)S(1)} %get-tuple-element.43), channel_id=1, source_target_pairs={{16,32},{32,16},{48,64},{64,48},{80,96},{96,80},{112,128},{128,112... | collective-permute-start | bytes 245768 | tf_op jit(solution)/shard_map/ppermute | solution.py:29
  67.7 14.6 %collective-permute-start.11 = (f32[12,8,640]{2,1,0:T(8,128)S(1)}, f32[12,8,640]{2,1,0:T(8,128)S(1)}, u32[]{:S(2)}, u32[]{:S(2)}) collective-permute-start(f32[12,8,640]{2,1,0:T(8,128)S(1)} %get-tuple-element.44.cur.prev), channel_id=1, source_target_pairs={{2,4},{4,2},{6,8},{8,6},{10,12},{12,10},{3,5},{5,3},{7,9},{9,7},{1... | collective-permute-start | bytes 737288 | tf_op jit(solution)/shard_map/ppermute | solution.py:29
  69.6 12.6 %collective-permute-start.10 = (f32[12,8,640]{2,1,0:T(8,128)S(1)}, f32[12,8,640]{2,1,0:T(8,128)S(1)}, u32[]{:S(2)}, u32[]{:S(2)}) collective-permute-start(f32[12,8,640]{2,1,0:T(8,128)S(1)} %get-tuple-element.44.cur.prev), channel_id=1, source_target_pairs={{0,2},{2,0},{4,6},{6,4},{8,10},{10,8},{12,14},{14,12},{1,3},{3,1},... | collective-permute-start | bytes 737288 | tf_op jit(solution)/shard_map/ppermute | solution.py:29
  71.6 7.5 %collective-permute-start.8 = (f32[9,8,640]{2,1,0:T(8,128)S(1)}, f32[9,8,640]{2,1,0:T(8,128)S(1)}, u32[]{:S(2)}, u32[]{:S(2)}) collective-permute-start(f32[9,8,640]{2,1,0:T(8,128)S(1)} %get-tuple-element.45), channel_id=1, source_target_pairs={{0,16},{16,0},{32,48},{48,32},{64,80},{80,64},{96,112},{112,96},{1... | collective-permute-start | bytes 552968 | tf_op jit(solution)/shard_map/ppermute | solution.py:29
  73.5 8.7 %collective-permute-start.9 = (f32[9,8,640]{2,1,0:T(8,128)S(1)}, f32[9,8,640]{2,1,0:T(8,128)S(1)}, u32[]{:S(2)}, u32[]{:S(2)}) collective-permute-start(f32[9,8,640]{2,1,0:T(8,128)S(1)} %get-tuple-element.46), channel_id=1, source_target_pairs={{16,32},{32,16},{48,64},{64,48},{80,96},{96,80},{112,128},{128,112... | collective-permute-start | bytes 552968 | tf_op jit(solution)/shard_map/ppermute | solution.py:29
  82.9 17.8 %collective-permute-start.15 = (f32[12,8,640]{2,1,0:T(8,128)S(1)}, f32[12,8,640]{2,1,0:T(8,128)S(1)}, u32[]{:S(2)}, u32[]{:S(2)}) collective-permute-start(f32[12,8,640]{2,1,0:T(8,128)S(1)} %get-tuple-element.49.cur), channel_id=1, source_target_pairs={{2,4},{4,2},{6,8},{8,6},{10,12},{12,10},{3,5},{5,3},{7,9},{9,7},{1... | collective-permute-start | bytes 737288 | tf_op jit(solution)/shard_map/ppermute | solution.py:29
  88.1 12.6 %collective-permute-start.14 = (f32[12,8,640]{2,1,0:T(8,128)S(1)}, f32[12,8,640]{2,1,0:T(8,128)S(1)}, u32[]{:S(2)}, u32[]{:S(2)}) collective-permute-start(f32[12,8,640]{2,1,0:T(8,128)S(1)} %get-tuple-element.49.cur), channel_id=1, source_target_pairs={{0,2},{2,0},{4,6},{6,4},{8,10},{10,8},{12,14},{14,12},{1,3},{3,1},... | collective-permute-start | bytes 737288 | tf_op jit(solution)/shard_map/ppermute | solution.py:29
  90.1 7.5 %collective-permute-start.12 = (f32[9,8,640]{2,1,0:T(8,128)S(1)}, f32[9,8,640]{2,1,0:T(8,128)S(1)}, u32[]{:S(2)}, u32[]{:S(2)}) collective-permute-start(f32[9,8,640]{2,1,0:T(8,128)S(1)} %get-tuple-element.47), channel_id=1, source_target_pairs={{0,16},{16,0},{32,48},{48,32},{64,80},{80,64},{96,112},{112,96},{1... | collective-permute-start | bytes 552968 | tf_op jit(solution)/shard_map/ppermute | solution.py:29
  92.0 8.7 %collective-permute-start.13 = (f32[9,8,640]{2,1,0:T(8,128)S(1)}, f32[9,8,640]{2,1,0:T(8,128)S(1)}, u32[]{:S(2)}, u32[]{:S(2)}) collective-permute-start(f32[9,8,640]{2,1,0:T(8,128)S(1)} %get-tuple-element.48), channel_id=1, source_target_pairs={{16,32},{32,16},{48,64},{64,48},{80,96},{96,80},{112,128},{128,112... | collective-permute-start | bytes 552968 | tf_op jit(solution)/shard_map/ppermute | solution.py:29
  101.4 6.0 %collective-permute-start.16 = (f32[3,8,512]{2,1,0:T(8,128)S(1)}, f32[3,8,512]{2,1,0:T(8,128)S(1)}, u32[]{:S(2)}, u32[]{:S(2)}) collective-permute-start(f32[3,8,512]{2,1,0:T(8,128)S(1)} %get-tuple-element.54), channel_id=1, source_target_pairs={{0,2},{2,0},{4,6},{6,4},{8,10},{10,8},{12,14},{14,12},{1,3},{3,1},... | collective-permute-start | bytes 147464 | tf_op jit(solution)/shard_map/ppermute | solution.py:29
  105.4 7.2 %collective-permute-start.17 = (f32[3,8,512]{2,1,0:T(8,128)S(1)}, f32[3,8,512]{2,1,0:T(8,128)S(1)}, u32[]{:S(2)}, u32[]{:S(2)}) collective-permute-start(f32[3,8,512]{2,1,0:T(8,128)S(1)} %get-tuple-element.55), channel_id=1, source_target_pairs={{2,4},{4,2},{6,8},{8,6},{10,12},{12,10},{3,5},{5,3},{7,9},{9,7},{1... | collective-permute-start | bytes 147464 | tf_op jit(solution)/shard_map/ppermute | solution.py:29
  112.7 10.5 %collective-permute-start.18 = (f32[14,8,640]{2,1,0:T(8,128)S(1)}, f32[14,8,640]{2,1,0:T(8,128)S(1)}, u32[]{:S(2)}, u32[]{:S(2)}) collective-permute-start(f32[14,8,640]{2,1,0:T(8,128)S(1)} %get-tuple-element.57), channel_id=1, source_target_pairs={{0,16},{16,0},{32,48},{48,32},{64,80},{80,64},{96,112},{112,96},{1... | collective-permute-start | bytes 860168 | tf_op jit(solution)/shard_map/ppermute | solution.py:29
  114.7 10.6 %collective-permute-start.19 = (f32[14,8,640]{2,1,0:T(8,128)S(1)}, f32[14,8,640]{2,1,0:T(8,128)S(1)}, u32[]{:S(2)}, u32[]{:S(2)}) collective-permute-start(f32[14,8,640]{2,1,0:T(8,128)S(1)} %get-tuple-element.58), channel_id=1, source_target_pairs={{16,32},{32,16},{48,64},{64,48},{80,96},{96,80},{112,128},{128,112... | collective-permute-start | bytes 860168 | tf_op jit(solution)/shard_map/ppermute | solution.py:29
